TPU v7x, 128 devices: a whole 4x4x4 slice. The times are simulated.
128 devices in a mesh: gx: 8 (over z, core), gy: 4 (over y), gz: 4 (over x).
Axes of the slice: x: 4, y: 4, z: 4, core: 2. Of those that a mesh axis runs over, the one named last changes fastest.
Arguments:
- pressure_rhs: float32 [128, 128, 2048], P('gx', 'gy', 'gz'), may hold values from -6 to 6
- shift_diag: float32 [128, 128, 2048], P('gx', 'gy', 'gz'), may hold values from 0.02 to 0.3
- positions: float32 [3, 1048576], P(None, ('gx', 'gy', 'gz')), may hold values from -6 to 6
- normals: float32 [3, 1048576], P(None, ('gx', 'gy', 'gz')), may hold values from -6 to 6
- tension: float32 [1048576], P(('gx', 'gy', 'gz')), may hold values from 0.3 to 3
- edge_weight: float32 [6, 1048576], P(None, ('gx', 'gy', 'gz')), may hold values from 0.5 to 2
- owner_map: int32 [1048576, 1], P(('gx', 'gy', 'gz')), may hold values from 0 to 127; in each aligned block of 8192 rows (0 to 8191, 8192 to 16383, ...) at most 256 rows name the same one
- cell_map: int32 [1048576], P(('gx', 'gy', 'gz')), may hold values from 0 to 262143
- connectivity: int32 [6, 1048576], P(None, ('gx', 'gy', 'gz')), may hold values from 0 to 1048575, as said below
Outputs:
- pressure: float32 [128, 128, 2048], P('gx', 'gy', 'gz')
- surface_force: float32 [3, 1048576], P(None, ('gx', 'gy', 'gz'))
Inputs may be any that keep to these rules, and one draw needn't show every extreme that they name: `connectivity`: each neighbour index differs from the point's own index by 1 to 64, counted cyclically over 1048576; the distance 64 occurs. `owner_map`: among the points of one device no owner is named more than 256 times, a bound that some block reaches.
All inputs are finite; a program needn't handle non-finite values.
Results may differ from a plain program's by a relative error of at most 0.0003.
Values sent between devices are 32-bit elements; how exact they have to be, the bound alone decides.
No kernel may reach another device: no remote copies, remote signals or barrier semaphores. Data moves between devices by JAX's collectives and lax.ppermute only.
A program may use at most 192 MiB of HBM per device.

v0:
```python
import jax
import jax.numpy as jnp
from jax import lax
from jax.sharding import PartitionSpec as P

HALO = 64
SMOOTH = 3
COARSE_SMOOTH = 4


centre = 1.125
spread = 0.875


def extended(value, sides, width):
    edges = {}
    for axis, dim in sides:
        devices, length = (lax.axis_size(axis), value.shape[dim])
        up = [(i, (i + 1) % devices) for i in range(devices - 1)]
        last = lax.slice_in_dim(value, length - width, length, axis=dim)
        initial = lax.slice_in_dim(value, 0, width, axis=dim)
        edges[dim] = (
            lax.ppermute(last, axis, up),
            lax.ppermute(initial, axis, [(b, a) for a, b in up]),
        )
    done = []
    for _, dim in sides:
        low, high = edges[dim]
        around = [(width, width) if d in done else (0, 0) for d in range(value.ndim)]
        value = jnp.concatenate([jnp.pad(low, around), value, jnp.pad(high, around)], axis=dim)
        done.append(dim)
    return value


def padded_2(cells, sides, width, closed):
    for axis, dim in sides:
        count = lax.axis_size(axis)
        ends = count if closed else count - 1
        head = lax.slice_in_dim(cells, 0, width, axis=dim)
        tail = lax.slice_in_dim(cells, cells.shape[dim] - width, cells.shape[dim], axis=dim)
        cells = jnp.concatenate(
            [
                lax.ppermute(tail, axis, [(i, (i + 1) % count) for i in range(ends)]),
                cells,
                lax.ppermute(head, axis, [((i + 1) % count, i) for i in range(ends)]),
            ],
            axis=dim,
        )
    return cells


def side_by_side(arrays, axis, split_dim, concat_dim, along):
    both = jnp.concatenate(arrays, axis=along)
    filled, at, outs = (
        lax.all_to_all(both, axis, split_axis=split_dim, concat_axis=concat_dim, tiled=True),
        0,
        [],
    )
    for a in arrays:
        outs.append(lax.slice_in_dim(filled, at, at + a.shape[along], axis=along))
        at += a.shape[along]
    return tuple(outs)


def stencil(padded, field, shift):
    beside = padded[2:, 1:-1, 1:-1] + padded[:-2, 1:-1, 1:-1]
    beside = beside + padded[1:-1, 2:, 1:-1] + padded[1:-1, :-2, 1:-1]
    beside = beside + padded[1:-1, 1:-1, 2:] + padded[1:-1, 1:-1, :-2]
    return (6.0 + shift) * field - beside


def coarse_apply(field, shift):
    padded = extended(field, (("gx", 0), ("gy", 1), ("gz", 2)), 1)
    return stencil(padded, field, shift)


def local_apply(field, shift):
    return stencil(jnp.pad(field, 1), field, shift)


def chebyshev(target, shift, start, sweeps, apply_fn, inside):
    inverse = 1.0 / (6.0 + shift)
    ratio = centre / spread
    factor = 1.0 / ratio
    if start is None:
        update = inverse * target / centre
        answer = update
    else:
        update = inverse * (target - apply_fn(start, shift)) / centre
        update = update * inside
        answer = start + update
    for sweep in range(1, sweeps):
        remain = inverse * (target - apply_fn(answer, shift))
        if inside is not None:
            remain = remain * inside
        factor_new = 1.0 / (2.0 * ratio - factor)
        update = factor_new * factor * update + 2.0 * factor_new / spread * remain
        answer = answer + update
        factor = factor_new
    return answer


def domain_mask(shape, width):
    places = (lax.axis_index("gx"), lax.axis_index("gy"), lax.axis_index("gz"))
    counts = (lax.axis_size("gx"), lax.axis_size("gy"), lax.axis_size("gz"))
    factors = []
    for which in range(3):
        length = shape[which]
        where = places[which] * length - width + jnp.arange(length + 2 * width, dtype=jnp.int32)
        factors.append(((where >= 0) & (where < length * counts[which])).astype(jnp.float32))
    return factors[0][:, None, None] * factors[1][None, :, None] * factors[2][None, None, :]


def interior(field, width):
    return field[width:-width, width:-width, width:-width]


def blocks(field):
    return field.reshape(field.shape[0] // 2, 2, field.shape[1] // 2, 2, field.shape[2] // 2, 2)


def gather_neighbours(padded, relative, npoint):
    block_len = 2 * HALO
    nblock = npoint // block_len
    lower = padded[:, :npoint].reshape(3, nblock, block_len)
    upper = padded[:, block_len:].reshape(3, nblock, block_len)
    window = jnp.concatenate([lower, upper], axis=2)
    starts = (jnp.arange(nblock, dtype=jnp.int32) * block_len)[None, :, None]
    local_idx = relative.reshape(relative.shape[0], nblock, block_len) - starts
    columns = jnp.arange(2 * block_len, dtype=jnp.int32)
    picked = []
    for which in range(relative.shape[0]):
        select = (local_idx[which][:, :, None] == columns[None, None, :]).astype(jnp.float32)
        taken = jnp.einsum("bpw,cbw->cbp", select, window, precision=lax.Precision.HIGHEST)
        picked.append(taken.reshape(3, npoint))
    return jnp.stack(picked, axis=1)


def slot_ranks(owner_ids, ndevice, npoint):
    block_len = 2 * HALO
    nblock = npoint // block_len
    owner_hot = (owner_ids[:, None] == jnp.arange(ndevice, dtype=jnp.int32)[None, :]).astype(
        jnp.bfloat16
    )
    owner_blocks = owner_hot.reshape(nblock, block_len, ndevice)
    lower_tri = (jnp.arange(block_len)[:, None] > jnp.arange(block_len)[None, :]).astype(
        jnp.bfloat16
    )
    within = jnp.einsum("pq,bqo->bpo", lower_tri, owner_blocks, preferred_element_type=jnp.float32)
    counts = jnp.sum(owner_blocks.astype(jnp.float32), axis=1)
    before = jnp.cumsum(counts, axis=0) - counts
    ranks = jnp.sum((within + before[:, None, :]) * owner_blocks.astype(jnp.float32), axis=2)
    return (ranks.reshape(npoint).astype(jnp.int32), owner_hot)


def body(
    pressure_rhs,
    shift_diag,
    positions,
    normals,
    tension,
    edge_weight,
    owner_map,
    cell_map,
    connectivity,
):
    npoint = positions.shape[1]
    ndevice = lax.axis_size(("gx", "gy", "gz"))
    total = npoint * ndevice
    begin = lax.axis_index(("gx", "gy", "gz")) * npoint
    padded = padded_2(positions, ((("gx", "gy", "gz"), 1),), HALO, True)
    relative = (connectivity - begin + HALO + total) % total
    neighbours = gather_neighbours(padded, relative, npoint)
    surface_force = tension[None, :] * jnp.sum(
        edge_weight[None, :, :] * (neighbours - positions[:, None, :]), axis=1
    )
    jump = jnp.sum(surface_force * normals, axis=0)
    owner_ids = owner_map[:, 0]
    capacity = 4 * npoint // ndevice
    ranks, owner_hot = slot_ranks(owner_ids, ndevice, npoint)
    rank_hot = (ranks[:, None] == jnp.arange(capacity, dtype=jnp.int32)[None, :]).astype(
        jnp.float32
    )
    carried = jnp.stack([jump, cell_map.astype(jnp.float32)], axis=0)
    weighted = carried[:, :, None] * rank_hot[None, :, :]
    packed = jnp.einsum(
        "po,kpr->kor", owner_hot.astype(jnp.float32), weighted, precision=lax.Precision.HIGHEST
    )
    values = packed[0]
    cell_ids = packed[1]
    got_values, got_cells = side_by_side((values, cell_ids), ("gx", "gy", "gz"), 0, 0, 1)
    shape = pressure_rhs.shape
    source = jnp.zeros((shape[0] * shape[1] * shape[2],), jnp.float32)
    source = source.at[got_cells.reshape(-1).astype(jnp.int32)].add(got_values.reshape(-1))
    forcing = pressure_rhs + source.reshape(shape)
    coarse_shift = 4.0 * jnp.mean(blocks(shift_diag), axis=(1, 3, 5))
    width = SMOOTH
    inside = domain_mask(shape, width)
    forcing_wide, shift_wide = (
        padded_2(forcing, (("gx", 0), ("gy", 1), ("gz", 2)), width, False),
        padded_2(shift_diag, (("gx", 0), ("gy", 1), ("gz", 2)), width, False),
    )
    smooth_wide = chebyshev(forcing_wide, shift_wide, None, SMOOTH, local_apply, inside)
    remain = interior(forcing_wide - local_apply(smooth_wide, shift_wide), width)
    smooth = interior(smooth_wide, width)
    coarse_rhs = 0.5 * jnp.sum(blocks(remain), axis=(1, 3, 5))
    coarse_fix = chebyshev(coarse_rhs, coarse_shift, None, COARSE_SMOOTH, coarse_apply, None)
    spreadout = jnp.broadcast_to(
        coarse_fix[:, None, :, None, :, None], blocks(shift_diag).shape
    ).reshape(shape)
    start_wide = padded_2(smooth + spreadout, (("gx", 0), ("gy", 1), ("gz", 2)), width, False)
    pressure = interior(
        chebyshev(forcing_wide, shift_wide, start_wide, SMOOTH, local_apply, inside), width
    )
    return (pressure, surface_force)


def solution(mesh):
    return jax.shard_map(
        body,
        mesh=mesh,
        in_specs=(
            P("gx", "gy", "gz"),
            P("gx", "gy", "gz"),
            P(None, ("gx", "gy", "gz")),
            P(None, ("gx", "gy", "gz")),
            P(("gx", "gy", "gz")),
            P(None, ("gx", "gy", "gz")),
            P(("gx", "gy", "gz"), None),
            P(("gx", "gy", "gz")),
            P(None, ("gx", "gy", "gz")),
        ),
        out_specs=(P("gx", "gy", "gz"), P(None, ("gx", "gy", "gz"))),
        check_vma=False,
    )
```

profile of v0, /device:TPU:50, one launch (start us, length us, event | category | flops | bytes accessed | tf_op | source)
XLA Modules:
  0.0 727.0 jit_solution(6783575048737289273)
XLA Ops:
  13.2 4.3 fusion.10
  17.8 4.3 fusion.7
  22.2 4.4 fusion.6
  26.5 4.4 fusion.5
  30.9 4.4 fusion.4
  35.3 4.4 fusion.3
  39.7 4.8 fusion.2
  45.6 8.6 %fusion.46 = f32[2,128,256]{1,2,0:T(8,128)S(1)} fusion(s32[8192]{0:T(1024)S(1)} %bitcast.104, f32[8192,256]{0,1:T(8,128)S(1)} %bitcast.95, f32[2,8192]{1,0:T(2,128)S(1)} %pad_maximum_fusion.72), kind=kOutput, calls=%fused_computation.98 | convolution fusion | flops 6447693824 | bytes 8749056 | tf_op jit(solution)/shard_map/po,kpr->kor/dot_general | solution.py:186
  55.1 10.8 %all-to-all-start = ((f32[128,1,512]{2,1,0:T(1,128)}), f32[128,1,512]{2,1,0:T(1,128)S(1)}, u32[]{:S(2)}, u32[]{:S(2)}) async-start(f32[128,1,512]{2,1,0:T(1,128)} %copy.13), calls=%async_computation | async-start | bytes 524288 | tf_op jit(solution)/shard_map/all_to_all | solution.py:55
  66.1 7.2 all-to-all-done
  73.7 221.5 %scatter_custom_fusion = f32[262144]{0:T(1024)S(1)} fusion(s32[32768]{0:T(1024)S(1)} %bitcast.100, f32[32768]{0:T(1024)S(1)} %bitcast.99, f32[]{:T(128)} %constant.31.clone.1), kind=kCustom, calls=%fused_computation.118 | custom fusion | flops 32768 | bytes 1048580 | tf_op jit(solution)/shard_map/scatter-add | solution.py:194
  311.1 69.1 %reshape.180 = f32[8,2,16,2,256,2]{5,4,3,2,1,0:T(8,128)} reshape(f32[16,32,512]{2,1,0:T(8,128)} %param.10) | data formatting | bytes 2097152 | tf_op jit(solution)/shard_map/reshape | solution.py:119
  380.2 20.8 %reduce_sum.58 = f32[8,16,256]{2,1,0:T(8,128)S(1)} reduce(f32[8,2,16,2,256,2]{5,4,3,2,1,0:T(8,128)} %reshape.180, f32[]{:T(128)} %constant.31.clone.1), dimensions={1,3,5}, to_apply=%region_6.7 | reduce | flops 229376 | bytes 1179652 | tf_op jit(solution)/shard_map/reduce_sum | solution.py:196
  409.4 3.9 collective-permute-start.5
  415.6 4.1 collective-permute-start.13
  442.7 68.4 %reshape.181 = f32[8,2,16,2,256,2]{5,4,3,2,1,0:T(8,128)} reshape(f32[16,32,512]{2,1,0:T(8,128)S(1)} %fusion.54) | data formatting | bytes 2097152 | tf_op jit(solution)/shard_map/reshape | solution.py:119
  511.1 20.8 %reduce_sum.59 = f32[8,16,256]{2,1,0:T(8,128)S(1)} reduce(f32[8,2,16,2,256,2]{5,4,3,2,1,0:T(8,128)} %reshape.181, f32[]{:T(128)} %constant.31.clone.1), dimensions={1,3,5}, to_apply=%region_7.8 | reduce | flops 229376 | bytes 1179652 | tf_op jit(solution)/shard_map/reduce_sum | solution.py:206
  586.7 4.1 collective-permute-start.31
  593.1 21.4 %broadcast_in_dim.5 = f32[8,2,16,2,256,2]{5,4,3,2,1,0:T(8,128)} broadcast(f32[8,16,256]{2,1,0:T(8,128)S(1)} %fusion.66), dimensions={0,2,4} | broadcast | bytes 1179648 | tf_op jit(solution)/shard_map/broadcast_in_dim | solution.py:208
  614.5 47.0 %reshape.182 = f32[16,32,512]{2,1,0:T(8,128)S(1)} reshape(f32[8,2,16,2,256,2]{5,4,3,2,1,0:T(8,128)} %broadcast_in_dim.5) | data formatting | bytes 2097152 | tf_op jit(solution)/shard_map/reshape | solution.py:210
  689.5 8.9 %collective-permute-done.36 = f32[22,38,3]{2,1,0:T(8,128)S(1)} collective-permute-done((f32[22,38,3]{2,1,0:T(8,128)S(1)}, f32[22,38,3]{2,1,0:T(8,128)S(1)}, u32[]{:S(2)}, u32[]{:S(2)}) %collective-permute-start.36) | collective-permute-done | bytes 10064 | tf_op jit(solution)/shard_map/ppermute | solution.py:43
  706.0 4.4 fusion.106
  710.4 9.2 %add_subtract_fusion = f32[22,38,518]{2,1,0:T(8,128)} fusion(f32[22,38,518]{2,1,0:T(8,128)} %get-tuple-element.4, f32[22,38,518]{2,1,0:T(8,128)S(1)} %get-tuple-element.3), kind=kLoop, calls=%fused_computation.53 | loop fusion | flops 3031336 | bytes 5196576 | tf_op jit(solution)/shard_map/sub | solution.py:69
  719.7 7.1 slice_add_fusion.1
  (184 shorter events, 156.6 us)
Async XLA Ops:
  1.4 16.2 %collective-permute-start.6 = (f32[3,64]{1,0:T(4,128)S(1)}, f32[3,64]{1,0:T(4,128)S(1)}, u32[]{:S(2)}, u32[]{:S(2)}) collective-permute-start(f32[3,64]{1,0:T(4,128)S(1)} %get-tuple-element.71), channel_id=1, source_target_pairs={{0,1},{1,2},{2,3},{3,4},{4,5},{5,6},{6,7},{7,8},{8,9},{9,10},{10,1... | collective-permute-start | bytes 2312 | tf_op jit(solution)/shard_map/ppermute | solution.py:43
  2.9 14.7 %collective-permute-start.7 = (f32[3,64]{1,0:T(4,128)S(1)}, f32[3,64]{1,0:T(4,128)S(1)}, u32[]{:S(2)}, u32[]{:S(2)}) collective-permute-start(f32[3,64]{1,0:T(4,128)S(1)} %get-tuple-element.72), channel_id=1, source_target_pairs={{1,0},{2,1},{3,2},{4,3},{5,4},{6,5},{7,6},{8,7},{9,8},{10,9},{11,1... | collective-permute-start | bytes 2312 | tf_op jit(solution)/shard_map/ppermute | solution.py:45
  4.5 61.6 %collective-permute-start.1 = (f32[3,32,512]{2,1,0:T(8,128)S(1)}, f32[3,32,512]{2,1,0:T(8,128)S(1)}, u32[]{:S(2)}, u32[]{:S(2)}) collective-permute-start(f32[3,32,512]{2,1,0:T(8,128)S(1)} %get-tuple-element.39), channel_id=1, source_target_pairs={{16,0},{32,16},{48,32},{64,48},{80,64},{96,80},{112,96},{17,1},{33... | collective-permute-start | bytes 589832 | tf_op jit(solution)/shard_map/ppermute | solution.py:45
  6.4 59.5 %collective-permute-start = (f32[3,32,512]{2,1,0:T(8,128)S(1)}, f32[3,32,512]{2,1,0:T(8,128)S(1)}, u32[]{:S(2)}, u32[]{:S(2)}) collective-permute-start(f32[3,32,512]{2,1,0:T(8,128)S(1)} %get-tuple-element.40), channel_id=1, source_target_pairs={{0,16},{16,32},{32,48},{48,64},{64,80},{80,96},{96,112},{1,17},{17... | collective-permute-start | bytes 589832 | tf_op jit(solution)/shard_map/ppermute | solution.py:43
  55.1 18.2 %all-to-all-start = ((f32[128,1,512]{2,1,0:T(1,128)}), f32[128,1,512]{2,1,0:T(1,128)S(1)}, u32[]{:S(2)}, u32[]{:S(2)}) async-start(f32[128,1,512]{2,1,0:T(1,128)} %copy.13), calls=%async_computation | async-start | bytes 524288 | tf_op jit(solution)/shard_map/all_to_all | solution.py:55
  298.8 102.2 %collective-permute-start.8 = (f32[3,32,512]{2,1,0:T(8,128)}, f32[3,32,512]{2,1,0:T(8,128)S(1)}, u32[]{:S(2)}, u32[]{:S(2)}) collective-permute-start(f32[3,32,512]{2,1,0:T(8,128)} %get-tuple-element.37), channel_id=1, source_target_pairs={{0,16},{16,32},{32,48},{48,64},{64,80},{80,96},{96,112},{1,17},{17... | collective-permute-start | bytes 589832 | tf_op jit(solution)/shard_map/ppermute | solution.py:43
  300.8 100.3 %collective-permute-start.9 = (f32[3,32,512]{2,1,0:T(8,128)}, f32[3,32,512]{2,1,0:T(8,128)S(1)}, u32[]{:S(2)}, u32[]{:S(2)}) collective-permute-start(f32[3,32,512]{2,1,0:T(8,128)} %get-tuple-element.38), channel_id=1, source_target_pairs={{16,0},{32,16},{48,32},{64,48},{80,64},{96,80},{112,96},{17,1},{33... | collective-permute-start | bytes 589832 | tf_op jit(solution)/shard_map/ppermute | solution.py:45
  305.2 101.8 %collective-permute-start.2 = (f32[22,3,512]{2,1,0:T(4,128)}, f32[22,3,512]{2,1,0:T(4,128)S(1)}, u32[]{:S(2)}, u32[]{:S(2)}) collective-permute-start(f32[22,3,512]{2,1,0:T(4,128)} %get-tuple-element.33), channel_id=1, source_target_pairs={{0,4},{4,8},{8,12},{1,5},{5,9},{9,13},{2,6},{6,10},{10,14},{3,7},{... | collective-permute-start | bytes 405512 | tf_op jit(solution)/shard_map/ppermute | solution.py:43
  307.2 99.9 %collective-permute-start.3 = (f32[22,3,512]{2,1,0:T(4,128)}, f32[22,3,512]{2,1,0:T(4,128)S(1)}, u32[]{:S(2)}, u32[]{:S(2)}) collective-permute-start(f32[22,3,512]{2,1,0:T(4,128)} %get-tuple-element.34), channel_id=1, source_target_pairs={{4,0},{8,4},{12,8},{5,1},{9,5},{13,9},{6,2},{10,6},{14,10},{7,3},{... | collective-permute-start | bytes 405512 | tf_op jit(solution)/shard_map/ppermute | solution.py:45
  407.3 15.2 %collective-permute-start.4 = (f32[22,38,3]{2,1,0:T(8,128)S(1)}, f32[22,38,3]{2,1,0:T(8,128)S(1)}, u32[]{:S(2)}, u32[]{:S(2)}) collective-permute-start(f32[22,38,3]{2,1,0:T(8,128)S(1)} %get-tuple-element.27), channel_id=1, source_target_pairs={{0,1},{1,2},{2,3},{4,5},{5,6},{6,7},{8,9},{9,10},{10,11},{12,13},{... | collective-permute-start | bytes 30104 | tf_op jit(solution)/shard_map/ppermute | solution.py:43
  409.4 15.1 %collective-permute-start.5 = (f32[22,38,3]{2,1,0:T(8,128)S(1)}, f32[22,38,3]{2,1,0:T(8,128)S(1)}, u32[]{:S(2)}, u32[]{:S(2)}) collective-permute-start(f32[22,38,3]{2,1,0:T(8,128)S(1)} %get-tuple-element.28), channel_id=1, source_target_pairs={{1,0},{2,1},{3,2},{5,4},{6,5},{7,6},{9,8},{10,9},{11,10},{13,12},{... | collective-permute-start | bytes 30104 | tf_op jit(solution)/shard_map/ppermute | solution.py:45
  413.6 15.3 %collective-permute-start.12 = (f32[22,38,3]{2,1,0:T(8,128)S(1)}, f32[22,38,3]{2,1,0:T(8,128)S(1)}, u32[]{:S(2)}, u32[]{:S(2)}) collective-permute-start(f32[22,38,3]{2,1,0:T(8,128)S(1)} %get-tuple-element.25), channel_id=1, source_target_pairs={{0,1},{1,2},{2,3},{4,5},{5,6},{6,7},{8,9},{9,10},{10,11},{12,13},{... | collective-permute-start | bytes 30104 | tf_op jit(solution)/shard_map/ppermute | solution.py:43
  415.6 15.5 %collective-permute-start.13 = (f32[22,38,3]{2,1,0:T(8,128)S(1)}, f32[22,38,3]{2,1,0:T(8,128)S(1)}, u32[]{:S(2)}, u32[]{:S(2)}) collective-permute-start(f32[22,38,3]{2,1,0:T(8,128)S(1)} %get-tuple-element.26), channel_id=1, source_target_pairs={{1,0},{2,1},{3,2},{5,4},{6,5},{7,6},{9,8},{10,9},{11,10},{13,12},{... | collective-permute-start | bytes 30104 | tf_op jit(solution)/shard_map/ppermute | solution.py:45
  532.0 14.9 %collective-permute-start.17 = (f32[8,1,256]{2,1,0:T(1,128)S(1)}, f32[8,1,256]{2,1,0:T(1,128)S(1)}, u32[]{:S(2)}, u32[]{:S(2)}) collective-permute-start(f32[8,1,256]{2,1,0:T(1,128)S(1)} %get-tuple-element.65), channel_id=1, source_target_pairs={{0,4},{4,8},{8,12},{1,5},{5,9},{9,13},{2,6},{6,10},{10,14},{3,7},{... | collective-permute-start | bytes 24584 | tf_op jit(solution)/shard_map/ppermute | solution.py:23
  535.6 13.7 %collective-permute-start.16 = (f32[8,1,256]{2,1,0:T(1,128)S(1)}, f32[8,1,256]{2,1,0:T(1,128)S(1)}, u32[]{:S(2)}, u32[]{:S(2)}) collective-permute-start(f32[8,1,256]{2,1,0:T(1,128)S(1)} %get-tuple-element.66), channel_id=1, source_target_pairs={{4,0},{8,4},{12,8},{5,1},{9,5},{13,9},{6,2},{10,6},{14,10},{7,3},{... | collective-permute-start | bytes 24584 | tf_op jit(solution)/shard_map/ppermute | solution.py:24
  537.8 15.2 %collective-permute-start.15 = (f32[1,16,256]{2,1,0:T(8,128)S(1)}, f32[1,16,256]{2,1,0:T(8,128)S(1)}, u32[]{:S(2)}, u32[]{:S(2)}) collective-permute-start(f32[1,16,256]{2,1,0:T(8,128)S(1)} %get-tuple-element.67), channel_id=1, source_target_pairs={{0,16},{16,32},{32,48},{48,64},{64,80},{80,96},{96,112},{1,17},{17... | collective-permute-start | bytes 49160 | tf_op jit(solution)/shard_map/ppermute | solution.py:23
  553.4 13.4 %collective-permute-start.23 = (f32[8,1,256]{2,1,0:T(1,128)S(1)}, f32[8,1,256]{2,1,0:T(1,128)S(1)}, u32[]{:S(2)}, u32[]{:S(2)}) collective-permute-start(f32[8,1,256]{2,1,0:T(1,128)S(1)} %get-tuple-element.59), channel_id=1, source_target_pairs={{0,4},{4,8},{8,12},{1,5},{5,9},{9,13},{2,6},{6,10},{10,14},{3,7},{... | collective-permute-start | bytes 24584 | tf_op jit(solution)/shard_map/ppermute | solution.py:23
  555.8 14.9 %collective-permute-start.22 = (f32[8,1,256]{2,1,0:T(1,128)S(1)}, f32[8,1,256]{2,1,0:T(1,128)S(1)}, u32[]{:S(2)}, u32[]{:S(2)}) collective-permute-start(f32[8,1,256]{2,1,0:T(1,128)S(1)} %get-tuple-element.60), channel_id=1, source_target_pairs={{4,0},{8,4},{12,8},{5,1},{9,5},{13,9},{6,2},{10,6},{14,10},{7,3},{... | collective-permute-start | bytes 24584 | tf_op jit(solution)/shard_map/ppermute | solution.py:24
  559.2 13.8 %collective-permute-start.21 = (f32[1,16,256]{2,1,0:T(8,128)S(1)}, f32[1,16,256]{2,1,0:T(8,128)S(1)}, u32[]{:S(2)}, u32[]{:S(2)}) collective-permute-start(f32[1,16,256]{2,1,0:T(8,128)S(1)} %get-tuple-element.61), channel_id=1, source_target_pairs={{0,16},{16,32},{32,48},{48,64},{64,80},{80,96},{96,112},{1,17},{17... | collective-permute-start | bytes 49160 | tf_op jit(solution)/shard_map/ppermute | solution.py:23
  573.2 13.4 %collective-permute-start.29 = (f32[8,1,256]{2,1,0:T(1,128)S(1)}, f32[8,1,256]{2,1,0:T(1,128)S(1)}, u32[]{:S(2)}, u32[]{:S(2)}) collective-permute-start(f32[8,1,256]{2,1,0:T(1,128)S(1)} %get-tuple-element.55), channel_id=1, source_target_pairs={{0,4},{4,8},{8,12},{1,5},{5,9},{9,13},{2,6},{6,10},{10,14},{3,7},{... | collective-permute-start | bytes 24584 | tf_op jit(solution)/shard_map/ppermute | solution.py:23
  575.9 15.0 %collective-permute-start.28 = (f32[8,1,256]{2,1,0:T(1,128)S(1)}, f32[8,1,256]{2,1,0:T(1,128)S(1)}, u32[]{:S(2)}, u32[]{:S(2)}) collective-permute-start(f32[8,1,256]{2,1,0:T(1,128)S(1)} %get-tuple-element.56), channel_id=1, source_target_pairs={{4,0},{8,4},{12,8},{5,1},{9,5},{13,9},{6,2},{10,6},{14,10},{7,3},{... | collective-permute-start | bytes 24584 | tf_op jit(solution)/shard_map/ppermute | solution.py:24
  579.1 13.8 %collective-permute-start.27 = (f32[1,16,256]{2,1,0:T(8,128)S(1)}, f32[1,16,256]{2,1,0:T(8,128)S(1)}, u32[]{:S(2)}, u32[]{:S(2)}) collective-permute-start(f32[1,16,256]{2,1,0:T(8,128)S(1)} %get-tuple-element.53), channel_id=1, source_target_pairs={{0,16},{16,32},{32,48},{48,64},{64,80},{80,96},{96,112},{1,17},{17... | collective-permute-start | bytes 49160 | tf_op jit(solution)/shard_map/ppermute | solution.py:23
  683.5 14.9 %collective-permute-start.36 = (f32[22,38,3]{2,1,0:T(8,128)S(1)}, f32[22,38,3]{2,1,0:T(8,128)S(1)}, u32[]{:S(2)}, u32[]{:S(2)}) collective-permute-start(f32[22,38,3]{2,1,0:T(8,128)S(1)} %get-tuple-element.23), channel_id=1, source_target_pairs={{0,1},{1,2},{2,3},{4,5},{5,6},{6,7},{8,9},{9,10},{10,11},{12,13},{... | collective-permute-start | bytes 30104 | tf_op jit(solution)/shard_map/ppermute | solution.py:43
  687.4 14.8 %collective-permute-start.37 = (f32[22,38,3]{2,1,0:T(8,128)S(1)}, f32[22,38,3]{2,1,0:T(8,128)S(1)}, u32[]{:S(2)}, u32[]{:S(2)}) collective-permute-start(f32[22,38,3]{2,1,0:T(8,128)S(1)} %get-tuple-element.24), channel_id=1, source_target_pairs={{1,0},{2,1},{3,2},{5,4},{6,5},{7,6},{9,8},{10,9},{11,10},{13,12},{... | collective-permute-start | bytes 30104 | tf_op jit(solution)/shard_map/ppermute | solution.py:45
  (36 other events, 666.0 us)
where the time goes:
time: 737 us; the launch traced here: 727 us
  other arithmetic  315 us (43%)
  local copies, waits for them, and re-layouts  212 us (29%)
  starting transfers between devices  116 us (16%)
  waiting for transfers between devices  44.1 us (6%)
  matrix products  37.7 us (5%)
    scatter-add x1, other arithmetic, body(): source.at[got_cells.reshape(-1).astype(jnp.int32)]  221 us
    reshape x2, local copies, waits for them, and re-layouts, blocks(): field.reshape(field.shape[0] // 2, 2, field.shape[1] // 2, 2, field.shape...  138 us
    reshape x1, local copies, waits for them, and re-layouts, body(): spreadout = jnp.broadcast_to(coarse_fix[:, None, :, None, :, None], block...  47 us
    ppermute x10, starting transfers between devices, padded_2(): lax.ppermute(head, axis, [((i + 1) % count, i) for i in range(ends)])  30.9 us
    ppermute x9, starting transfers between devices, extended(): lax.ppermute(initial, axis, [(b, a) for a, b in up])  26.9 us
    dot_general x6, matrix products, gather_neighbours(): jnp.einsum('bpw,cbw->cbp', select, window, precision=lax.Precision.HIGHEST)  26.6 us
    ppermute x9, starting transfers between devices, extended(): lax.ppermute(last, axis, up)  25 us
    ppermute x10, starting transfers between devices, padded_2(): lax.ppermute(tail, axis, [(i, (i + 1) % count) for i in range(ends)])  22.1 us
  transfers between devices with their start and end apart: 39, of which 16 were waited for; matrix products, arithmetic and copies ran while one was open for 20% of the time, Pallas kernels for 0%

commit v1 on v0

v1 whole, which is shorter than its diff:
```python
import jax
import jax.numpy as jnp
from jax import lax
from jax.experimental import pallas as pl
from jax.experimental.pallas import tpu as pltpu
from jax.sharding import PartitionSpec as P

CX, CY, CZ = 16, 32, 512
W = 5
EX = CX + 2 * W
EY = CY + 16
EZ = CZ + 128
ZB = -(-EX * EY // 128)
ALL = ("gx", "gy", "gz")
NPOINT = 8192
CAP = 256
NDEV = 128

CENTRE = 1.125
SPREAD = 0.875
RATIO = CENTRE / SPREAD


def factors(sweeps):
    factor, out = 1.0 / RATIO, []
    for _ in range(1, sweeps):
        fresh = 1.0 / (2.0 * RATIO - factor)
        out.append((fresh * factor, 2.0 * fresh / SPREAD))
        factor = fresh
    return out


def call(kernel, outs, operands, scratch=(), name=None, limit=40):
    specs = [
        pl.BlockSpec(memory_space=pltpu.SMEM)
        if o.dtype == jnp.int32 and o.ndim == 1
        else pl.BlockSpec(memory_space=pltpu.VMEM)
        for o in operands
    ]
    return pl.pallas_call(
        kernel,
        out_shape=[jax.ShapeDtypeStruct(s, jnp.float32) for s in outs],
        in_specs=specs,
        out_specs=[pl.BlockSpec(memory_space=pltpu.VMEM) for _ in outs],
        scratch_shapes=list(scratch),
        compiler_params=pltpu.CompilerParams(vmem_limit_bytes=limit << 20),
        name=name,
    )(*operands)


def lanes(shape):
    return lax.broadcasted_iota(jnp.int32, shape, len(shape) - 1)


def rows(shape):
    return lax.broadcasted_iota(jnp.int32, shape, len(shape) - 2)


def x_faces(force_ref, inv_ref, up_ref, low_ref, to_low_ref, to_up_ref):
    for which, ref in ((0, force_ref), (1, inv_ref)):
        for out, first in ((to_low_ref, 0), (to_up_ref, CX - W)):
            out[which, :, 0:CY, :] = ref[first : first + W]
            out[which, :, CY : CY + 8, :] = up_ref[which, first : first + W]
            out[which, :, CY + 8 : CY + 16, :] = low_ref[which, first : first + W]


def assemble(force_ref, inv_ref, yup_ref, ylow_ref, xup_ref, xlow_ref, f_ref, v_ref, to_low_ref, to_up_ref):
    for which, (src, dst) in enumerate(((force_ref, f_ref), (inv_ref, v_ref))):
        dst[0:W, :, 0:CZ] = xlow_ref[which]
        dst[W + CX :, :, 0:CZ] = xup_ref[which]
        dst[W : W + CX, 0:CY, 0:CZ] = src[...]
        dst[W : W + CX, CY : CY + 8, 0:CZ] = yup_ref[which]
        dst[W : W + CX, CY + 8 : CY + 16, 0:CZ] = ylow_ref[which]
    spot = lanes((128, 128))
    for j in range(ZB):
        first = min(128 * j, EX * EY - 128)

        def edge(ref, at):
            flat = ref.reshape(EX * EY, EZ)
            return flat[first : first + 128, at : at + 128]

        mixed = jnp.where(
            spot < 16,
            edge(f_ref, 0),
            jnp.where(
                spot < 32,
                pltpu.roll(edge(v_ref, 0), 16, 1),
                jnp.where(
                    spot < 48,
                    pltpu.roll(edge(f_ref, CZ - 128), 48, 1),
                    pltpu.roll(edge(v_ref, CZ - 128), 64, 1),
                ),
            ),
        )
        turned = mixed.T
        to_low_ref[:, 128 * j : 128 * j + 128] = turned[0:32]
        to_up_ref[:, 128 * j : 128 * j + 128] = turned[32:64]


def neighbours(ref, x, step):
    plane = ref[x]
    ny, nz = plane.shape
    beside = ref[x - 1] + ref[x + 1]
    beside = beside + (pltpu.roll(plane, 1, 0) + pltpu.roll(plane, ny - 1, 0))
    return plane, beside + (pltpu.roll(plane, step, 1) + pltpu.roll(plane, nz - step, 1))


def planes(first, last, body):
    def step(x, carry):
        body(x)
        return carry

    lax.fori_loop(first, last, step, 0)


def smooth_kernel(fin_ref, vin_ref, zup_ref, zlow_ref, f_ref, v_ref, a_ref, to_low_ref, to_up_ref, coarse_ref, b_ref, tmp_ref):
    f_ref[:, :, 0:CZ] = fin_ref[:, :, 0:CZ]
    v_ref[:, :, 0:CZ] = vin_ref[:, :, 0:CZ]
    gap = jnp.zeros((96, 128), jnp.float32)
    for j in range(ZB):
        first = min(128 * j, EX * EY - 128)
        at = slice(128 * j, 128 * j + 128)
        for dst, part in ((f_ref, slice(0, 16)), (v_ref, slice(16, 32))):
            stack = jnp.concatenate([zup_ref[part, at], gap, zlow_ref[part, at]], axis=0)
            dst.reshape(EX * EY, EZ)[first : first + 128, CZ:] = stack.T
    scale = 1.0 / CENTRE

    def start(x):
        a_ref[x] = v_ref[x] * f_ref[x] * scale

    planes(0, EX, start)
    (a1, b1), (a2, b2) = factors(3)

    def second(x):
        plane, beside = neighbours(a_ref, x, 1)
        left = v_ref[x] * (f_ref[x] + beside) - plane
        b_ref[x] = (1.0 + a1) * plane + b1 * left

    planes(1, EX - 1, second)

    def third(x):
        plane, beside = neighbours(b_ref, x, 1)
        left = v_ref[x] * (f_ref[x] + beside) - plane
        a_ref[x] = plane + a2 * (plane - a_ref[x]) + b2 * left

    planes(2, EX - 2, third)

    def restrict(xc, carry):
        total = jnp.zeros((CY, EZ), jnp.float32)
        weight = jnp.zeros((CY, EZ), jnp.float32)
        for half in range(2):
            x = W + 2 * xc + half
            plane, beside = neighbours(a_ref, x, 1)
            inv = v_ref[x, 0:CY]
            diag = jnp.where(inv > 0.0, 1.0 / inv, 0.0)
            total = total + ((f_ref[x] + beside)[0:CY] - diag * plane[0:CY])
            weight = weight + diag
        even = lanes((CY // 2, EZ)) % 2 == 0

        def pairs(value):
            value = value + pltpu.roll(value, EZ - 1, 1)
            parts = []
            for t in range(EZ // 128):
                tmp_ref[t] = value[:, 128 * t : 128 * t + 128]
                parts.append(tmp_ref[t, pl.ds(0, CY // 2, 2)] + tmp_ref[t, pl.ds(1, CY // 2, 2)])
            return jnp.concatenate(parts, axis=1)

        rhs = 0.5 * pairs(total)
        whole = pairs(weight)
        inv = jnp.where(whole > 0.0, 1.0 / (6.0 + 0.5 * (whole - 48.0)), 0.0)
        both = jnp.where(even, rhs, pltpu.roll(inv, 1, 1))
        coarse_ref[xc] = both
        to_low_ref[xc] = both[0:8]
        to_up_ref[xc] = both[8:16]
        return carry

    lax.fori_loop(0, CX // 2, restrict, 0)


def coarse_faces(own_ref, up_ref, low_ref, to_low_ref, to_up_ref):
    for out, first in ((to_low_ref, 0), (to_up_ref, CX // 2 - W)):
        out[:, 0:16] = own_ref[first : first + W]
        out[:, 16:24] = up_ref[first : first + W]
        out[:, 24:32] = low_ref[first : first + W]


def final_kernel(f_ref, v_ref, ain_ref, own_ref, yup_ref, ylow_ref, xup_ref, xlow_ref, out_ref, a_ref, b_ref, cb_ref, cv_ref, ca_ref, cc_ref, tmp_ref):
    even = lanes((32, EZ)) % 2 == 0

    def unpack(x, value):
        cb_ref[x] = jnp.where(even, value, pltpu.roll(value, 1, 1))
        cv_ref[x] = jnp.where(even, pltpu.roll(value, EZ - 1, 1), value)

    for x in range(W):
        unpack(x, xlow_ref[x])
        unpack(x + W + CX // 2, xup_ref[x])
    for x in range(CX // 2):
        unpack(x + W, jnp.concatenate([own_ref[x], yup_ref[x], ylow_ref[x]], axis=0))
    (a1, b1), (a2, b2), (a3, b3) = factors(4)
    scale = 1.0 / CENTRE
    ex = CX // 2 + 2 * W

    def start(x):
        ca_ref[x] = cv_ref[x] * cb_ref[x] * scale

    planes(0, ex, start)

    def sweep(src, dst, first, last, a, b, fresh):
        def body(x):
            plane, beside = neighbours(src, x, 2)
            left = cv_ref[x] * (cb_ref[x] + beside) - plane
            step = plane if fresh else plane - dst[x]
            dst[x] = plane + a * step + b * left

        planes(first, last, body)

    sweep(ca_ref, cc_ref, 1, ex - 1, a1, b1, True)
    sweep(cc_ref, ca_ref, 2, ex - 2, a2, b2, False)
    sweep(ca_ref, cc_ref, 3, ex - 3, a3, b3, False)

    def spread(x):
        coarse = cc_ref[(x + W) // 2]
        for t in range(EZ // 128):
            at = slice(128 * t, 128 * t + 128)
            tmp_ref[t, pl.ds(0, 32, 2)] = coarse[:, at]
            tmp_ref[t, pl.ds(1, 32, 2)] = coarse[:, at]
            a_ref[x, 0:40, at] = ain_ref[x, 0:40, at] + tmp_ref[t, 0:40]
            a_ref[x, 40:48, at] = ain_ref[x, 40:48, at] + tmp_ref[t, 56:64]

    planes(2, EX - 2, spread)
    (a1, b1), (a2, b2) = factors(3)

    def first(x):
        plane, beside = neighbours(a_ref, x, 1)
        left = v_ref[x] * (f_ref[x] + beside) - plane
        b_ref[x] = plane + scale * left

    planes(3, EX - 3, first)

    def second(x):
        plane, beside = neighbours(b_ref, x, 1)
        left = v_ref[x] * (f_ref[x] + beside) - plane
        a_ref[x] = plane + a1 * (plane - a_ref[x]) + b1 * left

    planes(4, EX - 4, second)

    def third(x):
        plane, beside = neighbours(a_ref, x, 1)
        left = v_ref[x] * (f_ref[x] + beside) - plane
        full = plane + a2 * (plane - b_ref[x]) + b2 * left
        out_ref[x - W] = full[0:CY, 0:CZ]

    planes(W, W + CX, third)


def swap(low, high, axis):
    count = lax.axis_size(axis)
    up = [(i, i + 1) for i in range(count - 1)]
    return lax.ppermute(low, axis, [(b, a) for a, b in up]), lax.ppermute(high, axis, up)


def solve(forcing, inverse, to_low, to_up):
    yup, ylow = swap(to_low, to_up, "gy")
    face = (2, W, EY, CZ)
    xs = call(x_faces, [face, face], (forcing, inverse, yup, ylow), name="x_faces")
    xup, xlow = swap(*xs, "gx")
    ext = (EX, EY, EZ)
    f, v, zl, zu = call(
        assemble,
        [ext, ext, (32, 128 * ZB), (32, 128 * ZB)],
        (forcing, inverse, yup, ylow, xup, xlow),
        name="assemble",
    )
    zup, zlow = swap(zl, zu, "gz")
    cy, cx = (CX // 2, 8, EZ), (W, 32, EZ)
    f, v, a, yl, yu, own = call(
        smooth_kernel,
        [ext, ext, ext, cy, cy, (CX // 2, CY // 2, EZ)],
        (f, v, zup, zlow),
        [pltpu.VMEM(ext, jnp.float32), pltpu.VMEM((EZ // 128, CY, 128), jnp.float32)],
        name="smooth",
    )
    yup, ylow = swap(yl, yu, "gy")
    xs = call(coarse_faces, [cx, cx], (own, yup, ylow), name="coarse_faces")
    xup, xlow = swap(*xs, "gx")
    cext = (CX // 2 + 2 * W, 32, EZ)
    return call(
        final_kernel,
        [(CX, CY, CZ)],
        (f, v, a, own, yup, ylow, xup, xlow),
        [pltpu.VMEM(ext, jnp.float32)] * 2
        + [pltpu.VMEM(cext, jnp.float32)] * 4
        + [pltpu.VMEM((EZ // 128, 64, 128), jnp.float32)],
        name="final",
        limit=50,
    )[0]


def points_kernel(begin_ref, pos_ref, low_ref, up_ref, nrm_ref, ten_ref, edge_ref, conn_ref, force_ref, jump_ref):
    half = lanes((1, 128)) < 64
    tiles = NPOINT // 128

    def tile(ref, row, t):
        if t < 0:
            return low_ref[row : row + 1, :]
        if t >= tiles:
            return up_ref[row : row + 1, :]
        return ref[row : row + 1, 128 * t : 128 * t + 128]

    for t in range(tiles):
        at = slice(128 * t, 128 * t + 128)
        conn = conn_ref[:, at]
        edge = edge_ref[:, at]
        tension = ten_ref[t : t + 1, :]
        same = (conn >> 7) == begin_ref[0] + t
        spot = conn & 127
        jump = jnp.zeros((1, 128), jnp.float32)
        for c in range(3):
            own = tile(pos_ref, c, t)
            other = jnp.where(half, tile(pos_ref, c, t + 1), tile(pos_ref, c, t - 1))
            shape = conn.shape
            near = jnp.take_along_axis(jnp.broadcast_to(own, shape), spot, axis=1, mode="promise_in_bounds")
            far = jnp.take_along_axis(jnp.broadcast_to(other, shape), spot, axis=1, mode="promise_in_bounds")
            pull = jnp.sum(edge * (jnp.where(same, near, far) - own), axis=0, keepdims=True)
            force = tension * pull
            force_ref[c : c + 1, at] = force
            jump = jump + force * nrm_ref[c : c + 1, at]
        jump_ref[t : t + 1, :] = jump


def slot_ranks(owner_ids, ndevice, npoint):
    block_len = 128
    nblock = npoint // block_len
    owner_hot = (owner_ids[:, None] == jnp.arange(ndevice, dtype=jnp.int32)[None, :]).astype(jnp.bfloat16)
    owner_blocks = owner_hot.reshape(nblock, block_len, ndevice)
    lower_tri = (jnp.arange(block_len)[:, None] > jnp.arange(block_len)[None, :]).astype(jnp.bfloat16)
    within = jnp.einsum("pq,bqo->bpo", lower_tri, owner_blocks, preferred_element_type=jnp.float32)
    counts = jnp.sum(owner_blocks.astype(jnp.float32), axis=1)
    before = jnp.cumsum(counts, axis=0) - counts
    ranks = jnp.sum((within + before[:, None, :]) * owner_blocks.astype(jnp.float32), axis=2)
    return (ranks.reshape(npoint).astype(jnp.int32), owner_hot)


def scatter_kernel(rhs_ref, shift_ref, got_ref, force_ref, inv_ref, to_low_ref, to_up_ref, acc_ref):
    group = 8
    acc_ref[...] = jnp.zeros((512, 512), jnp.float32)

    def step(g, carry):
        got = got_ref[pl.ds(g * group, group), :]
        left, right = [], []
        for i in range(group):
            value = got[i : i + 1, 0:CAP]
            cell = got[i : i + 1, CAP : 2 * CAP].astype(jnp.int32)
            top = value.astype(jnp.bfloat16).astype(jnp.float32)
            rest = value - top
            spot = lax.broadcasted_iota(jnp.int32, (512, CAP), 0)
            on_row = (cell >> 9) == spot
            on_col = jnp.where((cell & 511) == spot, 1.0, 0.0).astype(jnp.bfloat16)
            left += [jnp.where(on_row, top, 0.0).astype(jnp.bfloat16), jnp.where(on_row, rest, 0.0).astype(jnp.bfloat16)]
            right += [on_col, on_col]
        acc_ref[...] += lax.dot_general(
            jnp.concatenate(left, axis=1),
            jnp.concatenate(right, axis=1),
            (((1,), (1,)), ((), ())),
            preferred_element_type=jnp.float32,
        )
        return carry

    lax.fori_loop(0, NDEV // group, step, 0)

    def finish(x, carry):
        force = rhs_ref[x] + acc_ref[pl.ds(x * CY, CY), :]
        inv = 1.0 / (6.0 + shift_ref[x])
        force_ref[x] = force
        inv_ref[x] = inv
        for which, value in ((0, force), (1, inv)):
            to_low_ref[which, x] = value[0:8]
            to_up_ref[which, x] = value[CY - 8 : CY]
        return carry

    lax.fori_loop(0, CX, finish, 0)


def body(pressure_rhs, shift_diag, positions, normals, tension, edge_weight, owner_map, cell_map, connectivity):
    device = lax.axis_index(ALL)
    begin = (device * (NPOINT // 128)).reshape(1).astype(jnp.int32)
    ring = [(i, (i + 1) % NDEV) for i in range(NDEV)]
    low = lax.ppermute(positions[:, NPOINT - 128 :], ALL, ring)
    up = lax.ppermute(positions[:, :128], ALL, [(b, a) for a, b in ring])
    force, jump = call(
        points_kernel,
        [(3, NPOINT), (NPOINT // 128, 128)],
        (begin, positions, low, up, normals, tension.reshape(-1, 128), edge_weight, connectivity),
        name="points",
    )
    jump = jump.reshape(-1)
    ranks, owner_hot = slot_ranks(owner_map[:, 0], NDEV, NPOINT)
    rank_hot = (ranks[:, None] == jnp.arange(CAP, dtype=jnp.int32)[None, :]).astype(jnp.float32)
    carried = jnp.stack([jump, cell_map.astype(jnp.float32)], axis=0)
    weighted = carried[:, :, None] * rank_hot[None, :, :]
    packed = jnp.einsum("po,kpr->okr", owner_hot.astype(jnp.float32), weighted, precision=lax.Precision.HIGHEST)
    got = lax.all_to_all(packed.reshape(NDEV, 2 * CAP), ALL, 0, 0, tiled=True)
    block = (CX, CY, CZ)
    forcing, inverse, to_low, to_up = call(
        scatter_kernel,
        [block, block, (2, CX, 8, CZ), (2, CX, 8, CZ)],
        (pressure_rhs, shift_diag, got),
        [pltpu.VMEM((512, 512), jnp.float32)],
        name="scatter",
    )
    return solve(forcing, inverse, to_low, to_up), force


def solution(mesh):
    point, row = P(ALL), P(None, ALL)
    grid = P("gx", "gy", "gz")
    return jax.shard_map(
        body,
        mesh=mesh,
        in_specs=(grid, grid, row, row, point, row, P(ALL, None), point, row),
        out_specs=(grid, row),
        check_vma=False,
    )
```

time: 737 us -> 204 us (0.28); the launches traced: 727 us -> 204 us
  other arithmetic: 315 us -> 7.42 us
  local copies, waits for them, and re-layouts: 212 us -> 7.6 us
  starting transfers between devices: 116 us -> 28.2 us
  Pallas kernels: 0 us -> 73.9 us
  blocking collectives: 0 us -> 21.4 us
  matrix products: 37.7 us -> 21.6 us
    scatter-add x1 -> x0, other arithmetic: 221 us -> none  [body(): source.at[got_cells.reshape(-1).astype(jnp.int32)]]
    reshape x4 -> x0, local copies, waits for them, and re-layouts: 186 us -> none  [the longest x2 138 us: blocks(): field.reshape(field.shape[0] // 2, 2, field.shape[1] // 2, 2, field.shape...]
    ppermute x38 -> x12, starting transfers between devices: 105 us -> 28.2 us  [the longest x5 14.7 us: swap(): lax.ppermute(low, axis, [(b, a) for a, b in up])]
    pallas_call x0 -> x7, Pallas kernels: none -> 73.9 us  [call(): pl.pallas_call(kernel, out_shape=[jax.ShapeDtypeStruct(s, jnp.float32) fo...]
    reduce_sum x4 -> x0, other arithmetic: 42.5 us -> none  [the longest x1 20.8 us: body(): coarse_shift = 4.0 * jnp.mean(blocks(shift_diag), axis=(1, 3, 5))]
    add x11 -> x0, other arithmetic: 25.6 us -> none  [the longest x7 17.6 us: chebyshev(): answer = answer + update]
    broadcast_in_dim x1 -> x0, local copies, waits for them, and re-layouts: 21.4 us -> none  [body(): jnp.broadcast_to(coarse_fix[:, None, :, None, :, None], blocks(shift_diag...]
    all_to_all x0 -> x1, blocking collectives: none -> 21.4 us  [body(): got = lax.all_to_all(packed.reshape(NDEV, 2 * CAP), ALL, 0, 0, tiled=True)]
  transfers between devices with their start and end apart: 39 -> 12, of which waited for: 16 -> 10; matrix products, arithmetic and copies ran while one was open for 20% -> 5% of each run, Pallas kernels for 0% -> 0%
where the time goes in v1:
time: 204 us
  Pallas kernels  73.9 us (36%)
  waiting for transfers between devices  42.5 us (21%)
  starting transfers between devices  28.2 us (14%)
  matrix products  21.6 us (11%)
  blocking collectives  21.4 us (10%)
  local copies, waits for them, and re-layouts  7.6 us (4%)
  other arithmetic  7.42 us (4%)
    pallas_call x7, Pallas kernels, call(): pl.pallas_call(kernel, out_shape=[jax.ShapeDtypeStruct(s, jnp.float32) fo...  73.9 us
    ppermute x5, waiting for transfers between devices, swap(): lax.ppermute(low, axis, [(b, a) for a, b in up])  24.6 us
    all_to_all x1, blocking collectives, body(): got = lax.all_to_all(packed.reshape(NDEV, 2 * CAP), ALL, 0, 0, tiled=True)  21.4 us
    dot_general x1, matrix products, body(): jnp.einsum('po,kpr->okr', owner_hot.astype(jnp.float32), weighted, precis...  19.2 us
    ppermute x5, waiting for transfers between devices, swap(): lax.ppermute(high, axis, up)  17.9 us
    ppermute x5, starting transfers between devices, swap(): lax.ppermute(low, axis, [(b, a) for a, b in up])  14.7 us
    ppermute x5, starting transfers between devices, swap(): lax.ppermute(high, axis, up)  11.5 us
    unnamed x27, local copies, waits for them, and re-layouts  6.75 us
  transfers between devices with their start and end apart: 12, of which 10 were waited for; matrix products, arithmetic and copies ran while one was open for 5% of the time, Pallas kernels for 0%

profile of v1, /device:TPU:50, one launch (start us, length us, event | category | flops | bytes accessed | tf_op | source)
XLA Modules:
  0.0 203.6 jit_solution(7391511611955123511)
XLA Ops:
  4.9 2.5 %fusion.5 = f32[64,128]{1,0:T(8,128)S(1)} fusion(f32[64,128]{1,0:T(8,128)S(1)} %sub.7, s32[64,128]{1,0:T(8,128)} %bitcast.26), kind=kOutput, calls=%fused_computation.8 | convolution fusion | flops 275783680 | bytes 98304 | tf_op jit(solution)/shard_map/pq,bqo->bpo/dot_general | solution.py:337
  7.5 5.8 %fusion.4 = f32[8192,256]{1,0:T(8,128)} fusion(s32[8192]{0:T(1024)S(1)} %convert_bitcast_fusion), kind=kLoop, calls=%fused_computation.5 | loop fusion | flops 4194304 | bytes 8421376 | tf_op jit(solution)/shard_map/convert_element_type | solution.py:398
  14.8 19.2 %fusion = f32[128,2,256]{0,2,1:T(8,128)S(1)} fusion(f32[8192,256]{1,0:T(8,128)} %fusion.4, f32[2,8192]{1,0:T(2,128)S(1)} %pad_maximum_fusion, s32[8192]{0:T(1024)S(1)} %bitcast.27), kind=kOutput, calls=%fused_computation | convolution fusion | flops 6447693824 | bytes 8749056 | tf_op jit(solution)/shard_map/po,kpr->okr/dot_general | solution.py:401
  34.2 21.4 %all_to_all.11 = f32[128,1,512]{2,1,0:T(1,128)S(1)} all-to-all(f32[128,1,512]{2,1,0:T(1,128)S(1)} %copy.13), channel_id=1, replica_groups=mesh['gx'=8,'gy'=4,'gz'=4] {'gx','gy','gz'}, dimensions={0} | all-to-all | bytes 524288 | tf_op jit(solution)/shard_map/all_to_all | solution.py:402
  55.6 38.7 %scatter.1 = (f32[16,32,512]{2,1,0:T(8,128)S(1)}, f32[16,32,512]{2,1,0:T(8,128)S(1)}, f32[2,16,8,512]{3,2,1,0:T(8,128)S(1)}, f32[2,16,8,512]{3,2,1,0:T(8,128)S(1)}) custom-call(f32[16,32,512]{2,1,0:T(8,128)S(1)} %copy-done.4, f32[16,32,512]{2,1,0:T(8,128)S(1)} %copy-done.5, f32[128,512]{1,0:T(8,128)S(1)} %bitcast.20), custom_call_target="tpu_custom_call" | custom-call | tf_op jit(solution)/shard_map/scatter/pallas_call | solution.py:40
  94.4 3.9 %collective-permute-start.2 = (f32[2,16,8,512]{3,2,1,0:T(8,128)S(1)}, f32[2,16,8,512]{3,2,1,0:T(8,128)S(1)}, u32[]{:S(2)}, u32[]{:S(2)}) collective-permute-start(f32[2,16,8,512]{3,2,1,0:T(8,128)S(1)} %get-tuple-element.25), channel_id=1, source_target_pairs={{4,0},{8,4},{12,8},{5,1},{9,5},{13,9},{6,2},{10,6},{14,10},{7,3},{... | collective-permute-start | bytes 1572872 | tf_op jit(solution)/shard_map/ppermute | solution.py:259
  98.3 2.0 collective-permute-start.3
  100.3 9.6 %collective-permute-done.2.up_ref.yup_ref = f32[2,16,8,512]{3,2,1,0:T(8,128)S(1)} collective-permute-done((f32[2,16,8,512]{3,2,1,0:T(8,128)S(1)}, f32[2,16,8,512]{3,2,1,0:T(8,128)S(1)}, u32[]{:S(2)}, u32[]{:S(2)}) %collective-permute-start.2) | collective-permute-done | bytes 524320 | tf_op jit(solution)/shard_map/ppermute | solution.py:259
  109.9 3.3 %collective-permute-done.3.low_ref.ylow_ref = f32[2,16,8,512]{3,2,1,0:T(8,128)S(1)} collective-permute-done((f32[2,16,8,512]{3,2,1,0:T(8,128)S(1)}, f32[2,16,8,512]{3,2,1,0:T(8,128)S(1)}, u32[]{:S(2)}, u32[]{:S(2)}) %collective-permute-start.3) | collective-permute-done | bytes 524320 | tf_op jit(solution)/shard_map/ppermute | solution.py:259
  113.3 1.9 collective-permute-start.4
  115.2 2.4 %collective-permute-start.5 = (f32[2,5,48,512]{3,2,1,0:T(8,128)S(1)}, f32[2,5,48,512]{3,2,1,0:T(8,128)S(1)}, u32[]{:S(2)}, u32[]{:S(2)}) collective-permute-start(f32[2,5,48,512]{3,2,1,0:T(8,128)S(1)} %get-tuple-element.28), channel_id=1, source_target_pairs={{0,16},{16,32},{32,48},{48,64},{64,80},{80,96},{96,112},{1,17},{17... | collective-permute-start | bytes 2949128 | tf_op jit(solution)/shard_map/ppermute | solution.py:259
  117.7 9.2 %collective-permute-done.4.xup_ref = f32[2,5,48,512]{3,2,1,0:T(8,128)S(1)} collective-permute-done((f32[2,5,48,512]{3,2,1,0:T(8,128)S(1)}, f32[2,5,48,512]{3,2,1,0:T(8,128)S(1)}, u32[]{:S(2)}, u32[]{:S(2)}) %collective-permute-start.4) | collective-permute-done | bytes 983072 | tf_op jit(solution)/shard_map/ppermute | solution.py:259
  126.8 3.8 %collective-permute-done.5.xlow_ref = f32[2,5,48,512]{3,2,1,0:T(8,128)S(1)} collective-permute-done((f32[2,5,48,512]{3,2,1,0:T(8,128)S(1)}, f32[2,5,48,512]{3,2,1,0:T(8,128)S(1)}, u32[]{:S(2)}, u32[]{:S(2)}) %collective-permute-start.5) | collective-permute-done | bytes 983072 | tf_op jit(solution)/shard_map/ppermute | solution.py:259
  133.2 3.3 %collective-permute-start.6 = (f32[32,1280]{1,0:T(8,128)S(1)}, f32[32,1280]{1,0:T(8,128)S(1)}, u32[]{:S(2)}, u32[]{:S(2)}) collective-permute-start(f32[32,1280]{1,0:T(8,128)S(1)} %get-tuple-element.31), channel_id=1, source_target_pairs={{1,0},{2,1},{3,2},{5,4},{6,5},{7,6},{9,8},{10,9},{11,10},{13,12},{... | collective-permute-start | bytes 491528 | tf_op jit(solution)/shard_map/ppermute | solution.py:259
  136.5 2.5 %collective-permute-start.7 = (f32[32,1280]{1,0:T(8,128)S(1)}, f32[32,1280]{1,0:T(8,128)S(1)}, u32[]{:S(2)}, u32[]{:S(2)}) collective-permute-start(f32[32,1280]{1,0:T(8,128)S(1)} %get-tuple-element.32), channel_id=1, source_target_pairs={{0,1},{1,2},{2,3},{4,5},{5,6},{6,7},{8,9},{9,10},{10,11},{12,13},{... | collective-permute-start | bytes 491528 | tf_op jit(solution)/shard_map/ppermute | solution.py:259
  140.4 3.3 %collective-permute-done.7.zlow_ref = f32[32,1280]{1,0:T(8,128)S(1)} collective-permute-done((f32[32,1280]{1,0:T(8,128)S(1)}, f32[32,1280]{1,0:T(8,128)S(1)}, u32[]{:S(2)}, u32[]{:S(2)}) %collective-permute-start.7) | collective-permute-done | bytes 163872 | tf_op jit(solution)/shard_map/ppermute | solution.py:259
  143.7 13.2 %smooth.1 = (f32[26,48,640]{2,1,0:T(8,128)S(1)}, f32[26,48,640]{2,1,0:T(8,128)S(1)}, f32[26,48,640]{2,1,0:T(8,128)S(1)}, f32[8,8,640]{2,1,0:T(8,128)S(1)}, f32[8...) custom-call(f32[26,48,640]{2,1,0:T(8,128)S(1)} %get-tuple-element.29.fin_ref, f32[26,48,640]{2,1,0:T(8,128)} %copy-done.3, ...), custom_call_target="tpu_custom_call" | custom-call | tf_op jit(solution)/shard_map/smooth/pallas_call | solution.py:40
  162.0 3.6 %collective-permute-start.8 = (f32[8,8,640]{2,1,0:T(8,128)S(1)}, f32[8,8,640]{2,1,0:T(8,128)S(1)}, u32[]{:S(2)}, u32[]{:S(2)}) collective-permute-start(f32[8,8,640]{2,1,0:T(8,128)S(1)} %get-tuple-element.37), channel_id=1, source_target_pairs={{4,0},{8,4},{12,8},{5,1},{9,5},{13,9},{6,2},{10,6},{14,10},{7,3},{... | collective-permute-start | bytes 491528 | tf_op jit(solution)/shard_map/ppermute | solution.py:259
  165.7 2.2 %collective-permute-start.9 = (f32[8,8,640]{2,1,0:T(8,128)S(1)}, f32[8,8,640]{2,1,0:T(8,128)S(1)}, u32[]{:S(2)}, u32[]{:S(2)}) collective-permute-start(f32[8,8,640]{2,1,0:T(8,128)S(1)} %get-tuple-element.38), channel_id=1, source_target_pairs={{0,4},{4,8},{8,12},{1,5},{5,9},{9,13},{2,6},{6,10},{10,14},{3,7},{... | collective-permute-start | bytes 491528 | tf_op jit(solution)/shard_map/ppermute | solution.py:259
  169.2 3.6 %collective-permute-done.9.low_ref.ylow_ref = f32[8,8,640]{2,1,0:T(8,128)S(1)} collective-permute-done((f32[8,8,640]{2,1,0:T(8,128)S(1)}, f32[8,8,640]{2,1,0:T(8,128)S(1)}, u32[]{:S(2)}, u32[]{:S(2)}) %collective-permute-start.9) | collective-permute-done | bytes 163872 | tf_op jit(solution)/shard_map/ppermute | solution.py:259
  174.9 2.4 %collective-permute-start.11 = (f32[5,32,640]{2,1,0:T(8,128)S(1)}, f32[5,32,640]{2,1,0:T(8,128)S(1)}, u32[]{:S(2)}, u32[]{:S(2)}) collective-permute-start(f32[5,32,640]{2,1,0:T(8,128)S(1)} %get-tuple-element.40), channel_id=1, source_target_pairs={{0,16},{16,32},{32,48},{48,64},{64,80},{80,96},{96,112},{1,17},{17... | collective-permute-start | bytes 1228808 | tf_op jit(solution)/shard_map/ppermute | solution.py:259
  177.3 3.0 %collective-permute-done.10.xup_ref = f32[5,32,640]{2,1,0:T(8,128)S(1)} collective-permute-done((f32[5,32,640]{2,1,0:T(8,128)S(1)}, f32[5,32,640]{2,1,0:T(8,128)S(1)}, u32[]{:S(2)}, u32[]{:S(2)}) %collective-permute-start.10) | collective-permute-done | bytes 409632 | tf_op jit(solution)/shard_map/ppermute | solution.py:259
  180.3 3.8 %collective-permute-done.11.xlow_ref = f32[5,32,640]{2,1,0:T(8,128)S(1)} collective-permute-done((f32[5,32,640]{2,1,0:T(8,128)S(1)}, f32[5,32,640]{2,1,0:T(8,128)S(1)}, u32[]{:S(2)}, u32[]{:S(2)}) %collective-permute-start.11) | collective-permute-done | bytes 409632 | tf_op jit(solution)/shard_map/ppermute | solution.py:259
  184.1 19.5 %final.1 = f32[16,32,512]{2,1,0:T(8,128)} custom-call(f32[26,48,640]{2,1,0:T(8,128)} %copy-done, f32[26,48,640]{2,1,0:T(8,128)} %copy-done.1, f32[26,48,640]{2,1,0:T(8,128)} %copy-done.2, f32[8,16,640]{2,1,0:T(8,128)S(1)} %get-tuple-element.36.own_ref, f32[8,8,640]{2,1,0:T(8,128)S(1)} %collective-permute-done.8.up_ref.yup_ref, ...), custom_call_target="tpu_custom_call" | custom-call | tf_op jit(solution)/shard_map/final/pallas_call | solution.py:40
  (46 shorter events, 18.3 us)
Async XLA Ops:
  1.3 12.0 %collective-permute-start.1 = (f32[3,128]{1,0:T(4,128)S(1)}, f32[3,128]{1,0:T(4,128)S(1)}, u32[]{:S(2)}, u32[]{:S(2)}) collective-permute-start(f32[3,128]{1,0:T(4,128)S(1)} %get-tuple-element.42), channel_id=1, source_target_pairs={{1,0},{2,1},{3,2},{4,3},{5,4},{6,5},{7,6},{8,7},{9,8},{10,9},{11,1... | collective-permute-start | bytes 4616 | tf_op jit(solution)/shard_map/ppermute | solution.py:389
  1.9 11.5 %collective-permute-start = (f32[3,128]{1,0:T(4,128)S(1)}, f32[3,128]{1,0:T(4,128)S(1)}, u32[]{:S(2)}, u32[]{:S(2)}) collective-permute-start(f32[3,128]{1,0:T(4,128)S(1)} %get-tuple-element.43), channel_id=1, source_target_pairs={{0,1},{1,2},{2,3},{3,4},{4,5},{5,6},{6,7},{7,8},{8,9},{9,10},{10,1... | collective-permute-start | bytes 4616 | tf_op jit(solution)/shard_map/ppermute | solution.py:388
  7.4 5.9 %copy-start.11 = (s32[8192]{0:T(1024)S(1)}, s32[8192]{0:T(1024)}, u32[]{:S(2)}) copy-start(s32[8192]{0:T(1024)} %param.16) | copy-start | bytes 98308
  7.4 5.9 %copy-start.6 = (f32[6,8192]{1,0:T(8,128)S(1)}, f32[6,8192]{1,0:T(8,128)}, u32[]{:S(2)}) copy-start(f32[6,8192]{1,0:T(8,128)} %edge_ref.1) | copy-start | bytes 589828
  7.4 5.9 %copy-start.7 = (s32[6,8192]{1,0:T(8,128)S(1)}, s32[6,8192]{1,0:T(8,128)}, u32[]{:S(2)}) copy-start(s32[6,8192]{1,0:T(8,128)} %conn_ref.1) | copy-start | bytes 589828
  7.5 5.9 %copy-start.8 = (f32[3,8192]{1,0:T(4,128)S(1)}, f32[3,8192]{1,0:T(4,128)}, u32[]{:S(2)}) copy-start(f32[3,8192]{1,0:T(4,128)} %pos_ref.1) | copy-start | bytes 294916
  7.5 5.9 %copy-start.9 = (f32[3,8192]{1,0:T(4,128)S(1)}, f32[3,8192]{1,0:T(4,128)}, u32[]{:S(2)}) copy-start(f32[3,8192]{1,0:T(4,128)} %nrm_ref.1) | copy-start | bytes 294916
  7.5 5.9 %copy-start.10 = (f32[8192]{0:T(1024)S(1)}, f32[8192]{0:T(1024)}, u32[]{:S(2)}) copy-start(f32[8192]{0:T(1024)} %param.13) | copy-start | bytes 98308
  7.5 7.3 %copy-start.12 = (s32[8192,1]{0,1:T(1,128)S(1)}, s32[8192,1]{0,1:T(1,128)}, u32[]{:S(2)}) copy-start(s32[8192,1]{0,1:T(1,128)} %param.15) | copy-start | bytes 98308
  14.8 40.8 %copy-start.4 = (f32[16,32,512]{2,1,0:T(8,128)S(1)}, f32[16,32,512]{2,1,0:T(8,128)}, u32[]{:S(2)}) copy-start(f32[16,32,512]{2,1,0:T(8,128)} %rhs_ref.1) | copy-start | bytes 3145732
  14.8 40.8 %copy-start.5 = (f32[16,32,512]{2,1,0:T(8,128)S(1)}, f32[16,32,512]{2,1,0:T(8,128)}, u32[]{:S(2)}) copy-start(f32[16,32,512]{2,1,0:T(8,128)} %shift_ref.1) | copy-start | bytes 3145732
  94.4 15.5 %collective-permute-start.2 = (f32[2,16,8,512]{3,2,1,0:T(8,128)S(1)}, f32[2,16,8,512]{3,2,1,0:T(8,128)S(1)}, u32[]{:S(2)}, u32[]{:S(2)}) collective-permute-start(f32[2,16,8,512]{3,2,1,0:T(8,128)S(1)} %get-tuple-element.25), channel_id=1, source_target_pairs={{4,0},{8,4},{12,8},{5,1},{9,5},{13,9},{6,2},{10,6},{14,10},{7,3},{... | collective-permute-start | bytes 1572872 | tf_op jit(solution)/shard_map/ppermute | solution.py:259
  98.3 14.9 %collective-permute-start.3 = (f32[2,16,8,512]{3,2,1,0:T(8,128)S(1)}, f32[2,16,8,512]{3,2,1,0:T(8,128)S(1)}, u32[]{:S(2)}, u32[]{:S(2)}) collective-permute-start(f32[2,16,8,512]{3,2,1,0:T(8,128)S(1)} %get-tuple-element.26), channel_id=1, source_target_pairs={{0,4},{4,8},{8,12},{1,5},{5,9},{9,13},{2,6},{6,10},{10,14},{3,7},{... | collective-permute-start | bytes 1572872 | tf_op jit(solution)/shard_map/ppermute | solution.py:259
  113.3 13.5 %collective-permute-start.4 = (f32[2,5,48,512]{3,2,1,0:T(8,128)S(1)}, f32[2,5,48,512]{3,2,1,0:T(8,128)S(1)}, u32[]{:S(2)}, u32[]{:S(2)}) collective-permute-start(f32[2,5,48,512]{3,2,1,0:T(8,128)S(1)} %get-tuple-element.27), channel_id=1, source_target_pairs={{16,0},{32,16},{48,32},{64,48},{80,64},{96,80},{112,96},{17,1},{33... | collective-permute-start | bytes 2949128 | tf_op jit(solution)/shard_map/ppermute | solution.py:259
  115.2 15.4 %collective-permute-start.5 = (f32[2,5,48,512]{3,2,1,0:T(8,128)S(1)}, f32[2,5,48,512]{3,2,1,0:T(8,128)S(1)}, u32[]{:S(2)}, u32[]{:S(2)}) collective-permute-start(f32[2,5,48,512]{3,2,1,0:T(8,128)S(1)} %get-tuple-element.28), channel_id=1, source_target_pairs={{0,16},{16,32},{32,48},{48,64},{64,80},{80,96},{96,112},{1,17},{17... | collective-permute-start | bytes 2949128 | tf_op jit(solution)/shard_map/ppermute | solution.py:259
  131.6 1.6 copy-start.3
  133.2 7.2 %collective-permute-start.6 = (f32[32,1280]{1,0:T(8,128)S(1)}, f32[32,1280]{1,0:T(8,128)S(1)}, u32[]{:S(2)}, u32[]{:S(2)}) collective-permute-start(f32[32,1280]{1,0:T(8,128)S(1)} %get-tuple-element.31), channel_id=1, source_target_pairs={{1,0},{2,1},{3,2},{5,4},{6,5},{7,6},{9,8},{10,9},{11,10},{13,12},{... | collective-permute-start | bytes 491528 | tf_op jit(solution)/shard_map/ppermute | solution.py:259
  136.5 7.2 %collective-permute-start.7 = (f32[32,1280]{1,0:T(8,128)S(1)}, f32[32,1280]{1,0:T(8,128)S(1)}, u32[]{:S(2)}, u32[]{:S(2)}) collective-permute-start(f32[32,1280]{1,0:T(8,128)S(1)} %get-tuple-element.32), channel_id=1, source_target_pairs={{0,1},{1,2},{2,3},{4,5},{5,6},{6,7},{8,9},{9,10},{10,11},{12,13},{... | collective-permute-start | bytes 491528 | tf_op jit(solution)/shard_map/ppermute | solution.py:259
  158.6 1.7 copy-start.1
  160.3 1.7 copy-start.2
  162.0 7.2 %collective-permute-start.8 = (f32[8,8,640]{2,1,0:T(8,128)S(1)}, f32[8,8,640]{2,1,0:T(8,128)S(1)}, u32[]{:S(2)}, u32[]{:S(2)}) collective-permute-start(f32[8,8,640]{2,1,0:T(8,128)S(1)} %get-tuple-element.37), channel_id=1, source_target_pairs={{4,0},{8,4},{12,8},{5,1},{9,5},{13,9},{6,2},{10,6},{14,10},{7,3},{... | collective-permute-start | bytes 491528 | tf_op jit(solution)/shard_map/ppermute | solution.py:259
  165.7 7.2 %collective-permute-start.9 = (f32[8,8,640]{2,1,0:T(8,128)S(1)}, f32[8,8,640]{2,1,0:T(8,128)S(1)}, u32[]{:S(2)}, u32[]{:S(2)}) collective-permute-start(f32[8,8,640]{2,1,0:T(8,128)S(1)} %get-tuple-element.38), channel_id=1, source_target_pairs={{0,4},{4,8},{8,12},{1,5},{5,9},{9,13},{2,6},{6,10},{10,14},{3,7},{... | collective-permute-start | bytes 491528 | tf_op jit(solution)/shard_map/ppermute | solution.py:259
  172.9 7.4 %collective-permute-start.10 = (f32[5,32,640]{2,1,0:T(8,128)S(1)}, f32[5,32,640]{2,1,0:T(8,128)S(1)}, u32[]{:S(2)}, u32[]{:S(2)}) collective-permute-start(f32[5,32,640]{2,1,0:T(8,128)S(1)} %get-tuple-element.39), channel_id=1, source_target_pairs={{16,0},{32,16},{48,32},{64,48},{80,64},{96,80},{112,96},{17,1},{33... | collective-permute-start | bytes 1228808 | tf_op jit(solution)/shard_map/ppermute | solution.py:259
  174.9 9.3 %collective-permute-start.11 = (f32[5,32,640]{2,1,0:T(8,128)S(1)}, f32[5,32,640]{2,1,0:T(8,128)S(1)}, u32[]{:S(2)}, u32[]{:S(2)}) collective-permute-start(f32[5,32,640]{2,1,0:T(8,128)S(1)} %get-tuple-element.40), channel_id=1, source_target_pairs={{0,16},{16,32},{32,48},{48,64},{64,80},{80,96},{96,112},{1,17},{17... | collective-permute-start | bytes 1228808 | tf_op jit(solution)/shard_map/ppermute | solution.py:259
  (1 other events, 1.6 us)

commit v2 on v1

--- a/solution.py
+++ b/solution.py
@@ -30,7 +30,7 @@
     return out
 
 
-def call(kernel, outs, operands, scratch=(), name=None, limit=40):
+def call(kernel, outs, operands, scratch=(), name=None, limit=4, alias=None):
     specs = [
         pl.BlockSpec(memory_space=pltpu.SMEM)
         if o.dtype == jnp.int32 and o.ndim == 1
@@ -44,6 +44,7 @@
         out_specs=[pl.BlockSpec(memory_space=pltpu.VMEM) for _ in outs],
         scratch_shapes=list(scratch),
         compiler_params=pltpu.CompilerParams(vmem_limit_bytes=limit << 20),
+        input_output_aliases=alias or {},
         name=name,
     )(*operands)
 
@@ -113,9 +114,7 @@
     lax.fori_loop(first, last, step, 0)
 
 
-def smooth_kernel(fin_ref, vin_ref, zup_ref, zlow_ref, f_ref, v_ref, a_ref, to_low_ref, to_up_ref, coarse_ref, b_ref, tmp_ref):
-    f_ref[:, :, 0:CZ] = fin_ref[:, :, 0:CZ]
-    v_ref[:, :, 0:CZ] = vin_ref[:, :, 0:CZ]
+def smooth_kernel(_fin_ref, _vin_ref, zup_ref, zlow_ref, f_ref, v_ref, a_ref, to_low_ref, to_up_ref, coarse_ref, b_ref, tmp_ref):
     gap = jnp.zeros((96, 128), jnp.float32)
     for j in range(ZB):
         first = min(128 * j, EX * EY - 128)
@@ -279,6 +278,8 @@
         (f, v, zup, zlow),
         [pltpu.VMEM(ext, jnp.float32), pltpu.VMEM((EZ // 128, CY, 128), jnp.float32)],
         name="smooth",
+        limit=8,
+        alias={0: 0, 1: 1},
     )
     yup, ylow = swap(yl, yu, "gy")
     xs = call(coarse_faces, [cx, cx], (own, yup, ylow), name="coarse_faces")
@@ -292,11 +293,327 @@
         + [pltpu.VMEM(cext, jnp.float32)] * 4
         + [pltpu.VMEM((EZ // 128, 64, 128), jnp.float32)],
         name="final",
-        limit=50,
+        limit=20,
     )[0]
 
 
-def points_kernel(begin_ref, pos_ref, low_ref, up_ref, nrm_ref, ten_ref, edge_ref, conn_ref, force_ref, jump_ref):
+def bit_of(b, nv):
+    if b < 3:
+        return (lax.broadcasted_iota(jnp.int32, (8, 128), 0) >> b) & 1
+    return (lax.broadcasted_iota(jnp.int32, (8, 128), 1) >> (b - 3 - nv)) & 1
+
+
+def in_list(b, nv):
+    return 3 <= b < 3 + nv
+
+
+def across(x, b, nv, high):
+    axis, size, d = (0, 8, 1 << b) if b < 3 else (1, 128, 1 << (b - 3 - nv))
+    if 2 * d == size:
+        return pltpu.roll(x, d, axis)
+    return jnp.where(high, pltpu.roll(x, d, axis), pltpu.roll(x, size - d, axis))
+
+
+def exchange(keys, values, b, nv):
+    if in_list(b, nv):
+        d = 1 << (b - 3)
+        for u in range(len(keys)):
+            if u & d:
+                continue
+            low, high = keys[u], keys[u + d]
+            turn = low > high
+            keys[u], keys[u + d] = jnp.minimum(low, high), jnp.maximum(low, high)
+            a, c = values[u], values[u + d]
+            values[u], values[u + d] = jnp.where(turn, c, a), jnp.where(turn, a, c)
+        return
+    high = bit_of(b, nv) != 0
+    others = [across(key, b, nv, high) for key in keys]
+    loads = [across(value, b, nv, high) for value in values]
+    for u, other in enumerate(others):
+        key = keys[u]
+        keys[u] = jnp.where(high, jnp.maximum(key, other), jnp.minimum(key, other))
+        values[u] = jnp.where(keys[u] != key, loads[u], values[u])
+
+
+SIGN = -(1 << 31)
+
+
+def route(goal, loads, b, nv, g):
+    mask, one = jnp.int32(SIGN | (1 << g)), 1 << g
+    if in_list(b, nv):
+        d = 1 << (b - 3)
+        for u in range(len(goal)):
+            if u & d:
+                continue
+            low, high = goal[u], goal[u + d]
+            ml, mh = low & mask, high & mask
+            stay_l, stay_h = ml == 0, mh == one
+            goal[u] = jnp.where(stay_l, low, jnp.where(mh == 0, high, -1))
+            goal[u + d] = jnp.where(stay_h, high, jnp.where(ml == one, low, -1))
+            for load in loads:
+                a, c = load[u], load[u + d]
+                load[u], load[u + d] = jnp.where(stay_l, a, c), jnp.where(stay_h, c, a)
+        return
+    place = bit_of(b, nv)
+    high = place != 0
+    place = place << g
+    others = [across(x, b, nv, high) for x in goal]
+    moved = [[across(x, b, nv, high) for x in load] for load in loads]
+    for u, other in enumerate(others):
+        own = goal[u]
+        stay = (own & mask) == place
+        goal[u] = jnp.where(stay, own, jnp.where((other & mask) == place, other, -1))
+        for load, move in zip(loads, moved):
+            load[u] = jnp.where(stay, load[u], move[u])
+
+
+NONE = 1 << 18
+
+
+def pack(owner_ref, cell_ref, jump_ref, turn, out_ref, key_ref, val_ref, goal_ref):
+    nv = 3
+    keys, values = [], []
+    for u in range(8):
+        at = slice(8 * u, 8 * u + 8)
+        cell = cell_ref[at, :]
+        mixed = (
+            ((cell >> 15) << 15)
+            | ((cell & 127) << 8)
+            | ((cell >> 14) & 1) << 7
+            | ((cell >> 12) & 3) << 5
+            | ((cell >> 7) & 3) << 3
+            | (cell >> 9) & 7
+        )
+        mixed = mixed ^ (turn * (NONE - 1))
+        keys.append((owner_ref[at, :] << 18) | mixed)
+        values.append(jump_ref[at, :])
+    for k in range(1, 14):
+
+        def flip(keys):
+            if k == 13:
+                return keys
+            if in_list(k, nv):
+                return [~key if (u >> (k - 3)) & 1 else key for u, key in enumerate(keys)]
+            turned = -bit_of(k, nv)
+            return [key ^ turned for key in keys]
+
+        keys = flip(keys)
+        for b in range(k - 1, -1, -1):
+            exchange(keys, values, b, nv)
+        keys = flip(keys)
+    owners = [key >> 18 for key in keys]
+    spot = 64 * lanes((8, 128)) + rows((8, 128))
+    tail = [(owner << 13) | (8 * u + spot) for u, owner in enumerate(owners)]
+    runs = list(tail)
+    for b in range(13):
+        if in_list(b, nv):
+            d = 1 << (b - 3)
+            other = [tail[u ^ d] for u in range(8)]
+        else:
+            d, high = 0, bit_of(b, nv) != 0
+            other = [across(x, b, nv, high) for x in tail]
+        for u in range(8):
+            same = (other[u] ^ tail[u]) < 8192
+            joins = (other[u] ^ runs[u]) < 8192
+            if not d:
+                runs[u] = jnp.where(high & joins, other[u], runs[u])
+                tail[u] = jnp.where(high == same, other[u], tail[u])
+            elif u & d:
+                runs[u] = jnp.where(joins, other[u], runs[u])
+                tail[u] = jnp.where(same, other[u], tail[u])
+            else:
+                tail[u] = jnp.where(same, tail[u], other[u])
+    for u in range(8):
+        at = slice(8 * u, 8 * u + 8)
+        goal_ref[at, :] = 256 * owners[u] + 8 * u + spot - (runs[u] & 8191)
+        key_ref[at, :] = (keys[u] & (NONE - 1)) ^ (turn * (NONE - 1))
+        val_ref[at, :] = values[u]
+    empty = NONE * (1 - turn) - turn
+
+    def block(q, carry):
+        sets = []
+        for i in range(2):
+            goal, key, value = [], [], []
+            for u in range(8):
+                at = slice(8 * u, 8 * u + 8)
+                g = goal_ref[at, :]
+                goal.append(jnp.where((g >> 13) == 2 * q + i, g & 8191, -1))
+                key.append(key_ref[at, :])
+                value.append(val_ref[at, :])
+            sets.append((goal, key, value))
+        for b in range(12, -1, -1):
+            for goal, key, value in sets:
+                route(goal, [key, value], b, nv, b)
+        for i, (goal, key, value) in enumerate(sets):
+            full = [g >= 0 for g in goal]
+            parts = [jnp.where(f, v, 0.0) for f, v in zip(full, value)]
+            parts += [jnp.where(f, c, empty).astype(jnp.float32) for f, c in zip(full, key)]
+            first = pl.multiple_of(256 * q + 128 * i, 128)
+            out_ref[pl.ds(first, 128), :] = jnp.concatenate(parts, axis=0).T
+        return carry
+
+    lax.fori_loop(0, 2, block, 0)
+
+
+def regs(ref, first, count, step=8):
+    return [ref[pl.ds(first + step * u, 8), :] for u in range(count)]
+
+
+def put(ref, first, parts, step=8):
+    for u, part in enumerate(parts):
+        ref[pl.ds(first + step * u, 8), :] = part
+
+
+def shifted(x, d):
+    if d >= 256:
+        return pltpu.roll(x, d // 256, 1)
+    y = pltpu.roll(x, d, 0)
+    head = max(d, 8)
+    edge = jnp.where(rows((head, 128)) < d, pltpu.roll(y[:head], 1, 1), y[:head])
+    return jnp.concatenate([edge, y[head:]], axis=0) if head < 256 else edge
+
+
+def unpack_and_merge(got_ref, key_ref, val_ref):
+    nv = 5
+    for quarter in range(4):
+        turned = got_ref[pl.ds(quarter, 128, 4), :].T
+        val_ref[64 * quarter : 64 * quarter + 64, :] = turned[:64]
+        key_ref[64 * quarter : 64 * quarter + 64, :] = turned[64:].astype(jnp.int32)
+    before = 0
+    for k in range(9, 16):
+        turned = -bit_of(k, nv) if k < 15 else 0
+        change = turned ^ before
+        before = turned
+        for b in range(k - 1, 7, -1):
+            for half in range(2):
+                keys, values = regs(key_ref, 128 * half, 16), regs(val_ref, 128 * half, 16)
+                if b == k - 1:
+                    keys = [key ^ change for key in keys]
+                exchange(keys, values, b, nv)
+                put(key_ref, 128 * half, keys)
+                put(val_ref, 128 * half, values)
+        for u in range(8):
+            keys, values = regs(key_ref, 8 * u, 4, 64), regs(val_ref, 8 * u, 4, 64)
+            for b in (4, 3):
+                exchange(keys, values, b, 2)
+            put(key_ref, 8 * u, keys, 64)
+            put(val_ref, 8 * u, values, 64)
+        for u in range(4):
+            keys, values = regs(key_ref, 64 * u, 8), regs(val_ref, 64 * u, 8)
+            for b in range(5, -1, -1):
+                exchange(keys, values, b, 3)
+            put(key_ref, 64 * u, keys)
+            put(val_ref, 64 * u, values)
+
+
+def combine(key_ref, val_ref, rank_ref):
+    spot = rows((256, 128)) + 256 * lanes((256, 128))
+
+    def gather(d):
+        key, value = key_ref[...], val_ref[...]
+        same = (shifted(key, d) == key) & (spot >= d)
+        val_ref[...] = value + jnp.where(same, shifted(value, d), 0.0)
+
+    for d in (1, 2, 4):
+        gather(d)
+    key = key_ref[...]
+    real = (key >= 0) & (key < NONE)
+    long = jnp.where(real & (shifted(key, 8) == key) & (spot >= 8), 1.0, 0.0)
+
+    @pl.when(jnp.max(long) > 0.0)
+    def _():
+        for e in range(3, 15):
+            gather(1 << e)
+
+    after = pltpu.roll(key, 255, 0)
+    edge = jnp.where(rows((8, 128)) == 7, pltpu.roll(after[248:], 127, 1), after[248:])
+    after = jnp.concatenate([after[:248], edge], axis=0)
+    last = real & ((after != key) | (spot == 32767))
+    one = lambda test: jnp.where(test, 1.0, 0.0).astype(jnp.bfloat16)
+    mask = one(last)
+    dot = lambda a, b: jnp.dot(a, b, preferred_element_type=jnp.float32)
+    within = dot(one(rows((256, 256)) > lanes((256, 256))), mask)
+    totals = dot(jnp.ones((256, 256), jnp.bfloat16), mask).astype(jnp.bfloat16)
+    before = dot(totals, one(rows((128, 128)) < lanes((128, 128))))
+    rank_ref[...] = jnp.where(last, (within + before).astype(jnp.int32), -1)
+
+
+def concentrate(key_ref, val_ref, rank_ref, turn_key_ref, turn_val_ref):
+    refs = (rank_ref, key_ref, val_ref)
+
+    def stages(first, count, step, bits):
+        goal, key, value = (regs(r, first, count, step) for r in refs)
+        for b, nv, g in bits:
+            route(goal, [key, value], b, nv, g)
+        for r, parts in zip(refs, (goal, key, value)):
+            put(r, first, parts, step)
+
+    for u in range(4):
+        stages(64 * u, 8, 8, [(b, 3, b) for b in range(6)])
+    for u in range(8):
+        stages(8 * u, 4, 64, [(3, 2, 6), (4, 2, 7)])
+    for b in range(8, 15):
+        for half in range(2):
+            stages(128 * half, 16, 8, [(b, 5, b)])
+    for half in range(2):
+        at = slice(128 * half, 128 * half + 128)
+        turn_key_ref[at, :] = jnp.where(rank_ref[at, :] >= 0, key_ref[at, :], -1).T
+        turn_val_ref[at, :] = val_ref[at, :].T
+
+
+def distribute(turn_key_ref, turn_val_ref, goal_ref, move_ref, write):
+    def block(q, carry):
+        for half in range(2):
+            goal, value = regs(turn_key_ref, 128 * half, 16), regs(turn_val_ref, 128 * half, 16)
+            goal = [jnp.where((x >> 15) == q, x & 32767, -1) for x in goal]
+            for b in range(6, -1, -1):
+                route(goal, [value], b, 4, b + 8)
+            at = slice(128 * half, 128 * half + 128)
+            goal_ref[at, :] = jnp.concatenate(goal, axis=0).T
+            move_ref[at, :] = jnp.concatenate(value, axis=0).T
+        for u in range(8):
+            goal, value = regs(goal_ref, 8 * u, 4, 64), regs(move_ref, 8 * u, 4, 64)
+            route(goal, [value], 4, 2, 7)
+            route(goal, [value], 3, 2, 6)
+            put(goal_ref, 8 * u, goal, 64)
+            put(move_ref, 8 * u, value, 64)
+        for u in range(4):
+            goal, value = regs(goal_ref, 64 * u, 8), regs(move_ref, 64 * u, 8)
+            for b in range(5, -1, -1):
+                route(goal, [value], b, 3, b)
+            write(q, u, [jnp.where(x >= 0, v, 0.0) for x, v in zip(goal, value)])
+        return carry
+
+    lax.fori_loop(0, 8, block, 0)
+
+
+def scatter_kernel(rhs_ref, shift_ref, got_ref, force_ref, inv_ref, to_low_ref, to_up_ref, key_ref, val_ref, rank_ref, turn_key_ref, turn_val_ref):
+    unpack_and_merge(got_ref, key_ref, val_ref)
+    combine(key_ref, val_ref, rank_ref)
+    concentrate(key_ref, val_ref, rank_ref, turn_key_ref, turn_val_ref)
+
+    def write(q, u, values):
+        x = 2 * q + u // 2
+        for i, value in enumerate(values):
+            row, lane = 16 * (u % 2) + 8 * (i // 4), 128 * (i % 4)
+            at = (x, slice(row, row + 8), slice(lane, lane + 128))
+            force_ref[at] = rhs_ref[at] + value
+
+    distribute(turn_key_ref, turn_val_ref, rank_ref, val_ref, write)
+
+    def finish(x, carry):
+        force = force_ref[x]
+        inv = 1.0 / (6.0 + shift_ref[x])
+        inv_ref[x] = inv
+        for which, value in ((0, force), (1, inv)):
+            to_low_ref[which, x] = value[0:8]
+            to_up_ref[which, x] = value[CY - 8 : CY]
+        return carry
+
+    lax.fori_loop(0, CX, finish, 0)
+
+
+def points_kernel(begin_ref, pos_ref, low_ref, up_ref, nrm_ref, ten_ref, edge_ref, conn_ref, owner_ref, cell_ref, force_ref, send_ref, jump_ref, key_ref, val_ref, goal_ref):
     half = lanes((1, 128)) < 64
     tiles = NPOINT // 128
 
@@ -326,87 +643,45 @@
             force_ref[c : c + 1, at] = force
             jump = jump + force * nrm_ref[c : c + 1, at]
         jump_ref[t : t + 1, :] = jump
-
-
-def slot_ranks(owner_ids, ndevice, npoint):
-    block_len = 128
-    nblock = npoint // block_len
-    owner_hot = (owner_ids[:, None] == jnp.arange(ndevice, dtype=jnp.int32)[None, :]).astype(jnp.bfloat16)
-    owner_blocks = owner_hot.reshape(nblock, block_len, ndevice)
-    lower_tri = (jnp.arange(block_len)[:, None] > jnp.arange(block_len)[None, :]).astype(jnp.bfloat16)
-    within = jnp.einsum("pq,bqo->bpo", lower_tri, owner_blocks, preferred_element_type=jnp.float32)
-    counts = jnp.sum(owner_blocks.astype(jnp.float32), axis=1)
-    before = jnp.cumsum(counts, axis=0) - counts
-    ranks = jnp.sum((within + before[:, None, :]) * owner_blocks.astype(jnp.float32), axis=2)
-    return (ranks.reshape(npoint).astype(jnp.int32), owner_hot)
-
-
-def scatter_kernel(rhs_ref, shift_ref, got_ref, force_ref, inv_ref, to_low_ref, to_up_ref, acc_ref):
-    group = 8
-    acc_ref[...] = jnp.zeros((512, 512), jnp.float32)
-
-    def step(g, carry):
-        got = got_ref[pl.ds(g * group, group), :]
-        left, right = [], []
-        for i in range(group):
-            value = got[i : i + 1, 0:CAP]
-            cell = got[i : i + 1, CAP : 2 * CAP].astype(jnp.int32)
-            top = value.astype(jnp.bfloat16).astype(jnp.float32)
-            rest = value - top
-            spot = lax.broadcasted_iota(jnp.int32, (512, CAP), 0)
-            on_row = (cell >> 9) == spot
-            on_col = jnp.where((cell & 511) == spot, 1.0, 0.0).astype(jnp.bfloat16)
-            left += [jnp.where(on_row, top, 0.0).astype(jnp.bfloat16), jnp.where(on_row, rest, 0.0).astype(jnp.bfloat16)]
-            right += [on_col, on_col]
-        acc_ref[...] += lax.dot_general(
-            jnp.concatenate(left, axis=1),
-            jnp.concatenate(right, axis=1),
-            (((1,), (1,)), ((), ())),
-            preferred_element_type=jnp.float32,
-        )
-        return carry
-
-    lax.fori_loop(0, NDEV // group, step, 0)
-
-    def finish(x, carry):
-        force = rhs_ref[x] + acc_ref[pl.ds(x * CY, CY), :]
-        inv = 1.0 / (6.0 + shift_ref[x])
-        force_ref[x] = force
-        inv_ref[x] = inv
-        for which, value in ((0, force), (1, inv)):
-            to_low_ref[which, x] = value[0:8]
-            to_up_ref[which, x] = value[CY - 8 : CY]
-        return carry
-
-    lax.fori_loop(0, CX, finish, 0)
+    pack(owner_ref, cell_ref, jump_ref, begin_ref[1], send_ref, key_ref, val_ref, goal_ref)
 
 
 def body(pressure_rhs, shift_diag, positions, normals, tension, edge_weight, owner_map, cell_map, connectivity):
     device = lax.axis_index(ALL)
-    begin = (device * (NPOINT // 128)).reshape(1).astype(jnp.int32)
+    begin = jnp.stack([device * (NPOINT // 128), device % 2]).astype(jnp.int32)
     ring = [(i, (i + 1) % NDEV) for i in range(NDEV)]
     low = lax.ppermute(positions[:, NPOINT - 128 :], ALL, ring)
     up = lax.ppermute(positions[:, :128], ALL, [(b, a) for a, b in ring])
-    force, jump = call(
+    flat = (NPOINT // 128, 128)
+    whole = pltpu.VMEM(flat, jnp.int32)
+    force, send = call(
         points_kernel,
-        [(3, NPOINT), (NPOINT // 128, 128)],
-        (begin, positions, low, up, normals, tension.reshape(-1, 128), edge_weight, connectivity),
+        [(3, NPOINT), (4 * NDEV, 128)],
+        (
+            begin,
+            positions,
+            low,
+            up,
+            normals,
+            tension.reshape(flat),
+            edge_weight,
+            connectivity,
+            owner_map.reshape(flat),
+            cell_map.reshape(flat),
+        ),
+        [pltpu.VMEM(flat, jnp.float32), whole, pltpu.VMEM(flat, jnp.float32), whole],
         name="points",
     )
-    jump = jump.reshape(-1)
-    ranks, owner_hot = slot_ranks(owner_map[:, 0], NDEV, NPOINT)
-    rank_hot = (ranks[:, None] == jnp.arange(CAP, dtype=jnp.int32)[None, :]).astype(jnp.float32)
-    carried = jnp.stack([jump, cell_map.astype(jnp.float32)], axis=0)
-    weighted = carried[:, :, None] * rank_hot[None, :, :]
-    packed = jnp.einsum("po,kpr->okr", owner_hot.astype(jnp.float32), weighted, precision=lax.Precision.HIGHEST)
-    got = lax.all_to_all(packed.reshape(NDEV, 2 * CAP), ALL, 0, 0, tiled=True)
+    got = lax.all_to_all(send, ALL, 0, 0, tiled=True)
     block = (CX, CY, CZ)
+    list_i, list_f = pltpu.VMEM((256, 128), jnp.int32), pltpu.VMEM((256, 128), jnp.float32)
     forcing, inverse, to_low, to_up = call(
         scatter_kernel,
         [block, block, (2, CX, 8, CZ), (2, CX, 8, CZ)],
         (pressure_rhs, shift_diag, got),
-        [pltpu.VMEM((512, 512), jnp.float32)],
+        [list_i, list_f, list_i, list_i, list_f],
         name="scatter",
+        limit=8,
     )
     return solve(forcing, inverse, to_low, to_up), force
 

time: 204 us -> 155 us (0.76)
  Pallas kernels: 73.9 us -> 48.3 us
  matrix products: 21.6 us -> 0 us
  other arithmetic: 7.42 us -> 0.07 us
  waiting for transfers between devices: 42.5 us -> 45.1 us
    pallas_call x7, Pallas kernels: 73.9 us -> 48.3 us  [call(): pl.pallas_call(kernel, out_shape=[jax.ShapeDtypeStruct(s, jnp.float32) fo...]
    dot_general x2 -> x0, matrix products: 21.6 us -> none  [the longest x1 19.2 us: body(): jnp.einsum('po,kpr->okr', owner_hot.astype(jnp.float32), weighted, precis...]
    convert_element_type x3 -> x0, other arithmetic: 5.8 us -> none  [the longest x1 5.79 us: body(): (ranks[:, None] == jnp.arange(CAP, dtype=jnp.int32)[None, :]).astype(jnp....]
    unnamed x27 -> x18, local copies, waits for them, and re-layouts: 6.75 us -> 8.43 us
  transfers between devices with their start and end apart: 12 -> 12, of which waited for: 10 -> 12; matrix products, arithmetic and copies ran while one was open for 5% -> 0% of each run, Pallas kernels for 0% -> 0%
where the time goes in v2:
time: 155 us; the launch traced here: 154 us
  Pallas kernels  48.3 us (31%)
  waiting for transfers between devices  45.1 us (29%)
  starting transfers between devices  28.2 us (18%)
  blocking collectives  22.2 us (14%)
  local copies, waits for them, and re-layouts  9.13 us (6%)
    pallas_call x7, Pallas kernels, call(): pl.pallas_call(kernel, out_shape=[jax.ShapeDtypeStruct(s, jnp.float32) fo...  48.3 us
    ppermute x5, waiting for transfers between devices, swap(): lax.ppermute(low, axis, [(b, a) for a, b in up])  24.6 us
    all_to_all x1, blocking collectives, body(): got = lax.all_to_all(send, ALL, 0, 0, tiled=True)  22.2 us
    ppermute x5, waiting for transfers between devices, swap(): lax.ppermute(high, axis, up)  17.9 us
    ppermute x5, starting transfers between devices, swap(): lax.ppermute(low, axis, [(b, a) for a, b in up])  14.7 us
    ppermute x5, starting transfers between devices, swap(): lax.ppermute(high, axis, up)  11.5 us
    unnamed x18, local copies, waits for them, and re-layouts  8.43 us
  transfers between devices with their start and end apart: 12, of which 12 were waited for; matrix products, arithmetic and copies ran while one was open for 0% of the time, Pallas kernels for 0%

profile of v2, /device:TPU:50, one launch (start us, length us, event | category | flops | bytes accessed | tf_op | source)
XLA Modules:
  0.0 153.9 jit_solution(1109978924393855136)
XLA Ops:
  1.9 1.5 collective-permute-start
  12.1 5.9 %points.1 = (f32[3,8192]{1,0:T(4,128)}, f32[512,128]{1,0:T(8,128)S(1)}) custom-call(s32[2]{0:T(128)S(1)} %pad_add_fusion.begin_ref, f32[3,8192]{1,0:T(4,128)S(1)} %copy-done.4, f32[3,128]{1,0:T(4,128)S(1)} %collective-permute-done.low_ref, f32[3,128]{1,0:T(4,128)S(1)} %collective-permute-done.1.up_ref, f32[3,8192]{1,0:T(4,128)S(1)} %copy-done.5, ...), custom_call_target="tpu_custom_call" | custom-call | tf_op jit(solution)/shard_map/points/pallas_call | solution.py:40
  18.0 22.2 %all_to_all.11 = f32[128,4,128]{2,1,0:T(4,128)S(1)} all-to-all(f32[128,4,128]{2,1,0:T(4,128)S(1)} %bitcast.8), channel_id=1, replica_groups=mesh['gx'=8,'gy'=4,'gz'=4] {'gx','gy','gz'}, dimensions={0} | all-to-all | bytes 524288 | tf_op jit(solution)/shard_map/all_to_all | solution.py:675
  42.7 14.6 %scatter.1 = (f32[16,32,512]{2,1,0:T(8,128)S(1)}, f32[16,32,512]{2,1,0:T(8,128)S(1)}, f32[2,16,8,512]{3,2,1,0:T(8,128)S(1)}, f32[2,16,8,512]{3,2,1,0:T(8,128)S(1)}) custom-call(f32[16,32,512]{2,1,0:T(8,128)S(1)} %copy-done, f32[16,32,512]{2,1,0:T(8,128)S(1)} %copy-done.1, f32[512,128]{1,0:T(8,128)S(1)} %bitcast.7), custom_call_target="tpu_custom_call" | custom-call | tf_op jit(solution)/shard_map/scatter/pallas_call | solution.py:40
  57.3 3.9 %collective-permute-start.2 = (f32[2,16,8,512]{3,2,1,0:T(8,128)S(1)}, f32[2,16,8,512]{3,2,1,0:T(8,128)S(1)}, u32[]{:S(2)}, u32[]{:S(2)}) collective-permute-start(f32[2,16,8,512]{3,2,1,0:T(8,128)S(1)} %get-tuple-element.25), channel_id=1, source_target_pairs={{4,0},{8,4},{12,8},{5,1},{9,5},{13,9},{6,2},{10,6},{14,10},{7,3},{... | collective-permute-start | bytes 1572872 | tf_op jit(solution)/shard_map/ppermute | solution.py:258
  61.2 2.0 %collective-permute-start.3 = (f32[2,16,8,512]{3,2,1,0:T(8,128)S(1)}, f32[2,16,8,512]{3,2,1,0:T(8,128)S(1)}, u32[]{:S(2)}, u32[]{:S(2)}) collective-permute-start(f32[2,16,8,512]{3,2,1,0:T(8,128)S(1)} %get-tuple-element.26), channel_id=1, source_target_pairs={{0,4},{4,8},{8,12},{1,5},{5,9},{9,13},{2,6},{6,10},{10,14},{3,7},{... | collective-permute-start | bytes 1572872 | tf_op jit(solution)/shard_map/ppermute | solution.py:258
  63.2 9.6 %collective-permute-done.2.up_ref.yup_ref = f32[2,16,8,512]{3,2,1,0:T(8,128)S(1)} collective-permute-done((f32[2,16,8,512]{3,2,1,0:T(8,128)S(1)}, f32[2,16,8,512]{3,2,1,0:T(8,128)S(1)}, u32[]{:S(2)}, u32[]{:S(2)}) %collective-permute-start.2) | collective-permute-done | bytes 524320 | tf_op jit(solution)/shard_map/ppermute | solution.py:258
  72.8 3.3 %collective-permute-done.3.low_ref.ylow_ref = f32[2,16,8,512]{3,2,1,0:T(8,128)S(1)} collective-permute-done((f32[2,16,8,512]{3,2,1,0:T(8,128)S(1)}, f32[2,16,8,512]{3,2,1,0:T(8,128)S(1)}, u32[]{:S(2)}, u32[]{:S(2)}) %collective-permute-start.3) | collective-permute-done | bytes 524320 | tf_op jit(solution)/shard_map/ppermute | solution.py:258
  76.2 1.9 %collective-permute-start.4 = (f32[2,5,48,512]{3,2,1,0:T(8,128)S(1)}, f32[2,5,48,512]{3,2,1,0:T(8,128)S(1)}, u32[]{:S(2)}, u32[]{:S(2)}) collective-permute-start(f32[2,5,48,512]{3,2,1,0:T(8,128)S(1)} %get-tuple-element.27), channel_id=1, source_target_pairs={{16,0},{32,16},{48,32},{64,48},{80,64},{96,80},{112,96},{17,1},{33... | collective-permute-start | bytes 2949128 | tf_op jit(solution)/shard_map/ppermute | solution.py:258
  78.2 2.4 %collective-permute-start.5 = (f32[2,5,48,512]{3,2,1,0:T(8,128)S(1)}, f32[2,5,48,512]{3,2,1,0:T(8,128)S(1)}, u32[]{:S(2)}, u32[]{:S(2)}) collective-permute-start(f32[2,5,48,512]{3,2,1,0:T(8,128)S(1)} %get-tuple-element.28), channel_id=1, source_target_pairs={{0,16},{16,32},{32,48},{48,64},{64,80},{80,96},{96,112},{1,17},{17... | collective-permute-start | bytes 2949128 | tf_op jit(solution)/shard_map/ppermute | solution.py:258
  80.6 9.2 %collective-permute-done.4.xup_ref = f32[2,5,48,512]{3,2,1,0:T(8,128)S(1)} collective-permute-done((f32[2,5,48,512]{3,2,1,0:T(8,128)S(1)}, f32[2,5,48,512]{3,2,1,0:T(8,128)S(1)}, u32[]{:S(2)}, u32[]{:S(2)}) %collective-permute-start.4) | collective-permute-done | bytes 983072 | tf_op jit(solution)/shard_map/ppermute | solution.py:258
  89.8 3.8 %collective-permute-done.5.xlow_ref = f32[2,5,48,512]{3,2,1,0:T(8,128)S(1)} collective-permute-done((f32[2,5,48,512]{3,2,1,0:T(8,128)S(1)}, f32[2,5,48,512]{3,2,1,0:T(8,128)S(1)}, u32[]{:S(2)}, u32[]{:S(2)}) %collective-permute-start.5) | collective-permute-done | bytes 983072 | tf_op jit(solution)/shard_map/ppermute | solution.py:258
  94.5 3.3 %collective-permute-start.6 = (f32[32,1280]{1,0:T(8,128)S(1)}, f32[32,1280]{1,0:T(8,128)S(1)}, u32[]{:S(2)}, u32[]{:S(2)}) collective-permute-start(f32[32,1280]{1,0:T(8,128)S(1)} %get-tuple-element.31), channel_id=1, source_target_pairs={{1,0},{2,1},{3,2},{5,4},{6,5},{7,6},{9,8},{10,9},{11,10},{13,12},{... | collective-permute-start | bytes 491528 | tf_op jit(solution)/shard_map/ppermute | solution.py:258
  97.8 2.5 %collective-permute-start.7 = (f32[32,1280]{1,0:T(8,128)S(1)}, f32[32,1280]{1,0:T(8,128)S(1)}, u32[]{:S(2)}, u32[]{:S(2)}) collective-permute-start(f32[32,1280]{1,0:T(8,128)S(1)} %get-tuple-element.32), channel_id=1, source_target_pairs={{0,1},{1,2},{2,3},{4,5},{5,6},{6,7},{8,9},{9,10},{10,11},{12,13},{... | collective-permute-start | bytes 491528 | tf_op jit(solution)/shard_map/ppermute | solution.py:258
  101.7 3.3 %collective-permute-done.7.zlow_ref = f32[32,1280]{1,0:T(8,128)S(1)} collective-permute-done((f32[32,1280]{1,0:T(8,128)S(1)}, f32[32,1280]{1,0:T(8,128)S(1)}, u32[]{:S(2)}, u32[]{:S(2)}) %collective-permute-start.7) | collective-permute-done | bytes 163872 | tf_op jit(solution)/shard_map/ppermute | solution.py:258
  105.0 11.0 %smooth.1 = (f32[26,48,640]{2,1,0:T(8,128)S(1)}, f32[26,48,640]{2,1,0:T(8,128)S(1)}, f32[26,48,640]{2,1,0:T(8,128)S(1)}, f32[8,8,640]{2,1,0:T(8,128)S(1)}, f32[8...) custom-call(f32[26,48,640]{2,1,0:T(8,128)S(1)} %get-tuple-element.29._fin_ref, ...), custom_call_target="tpu_custom_call", output_to_operand_aliasing={{0}: (0, {}), {1}: (1, {})} | custom-call | tf_op jit(solution)/shard_map/smooth/pallas_call | solution.py:40
  116.1 3.6 %collective-permute-start.8 = (f32[8,8,640]{2,1,0:T(8,128)S(1)}, f32[8,8,640]{2,1,0:T(8,128)S(1)}, u32[]{:S(2)}, u32[]{:S(2)}) collective-permute-start(f32[8,8,640]{2,1,0:T(8,128)S(1)} %get-tuple-element.37), channel_id=1, source_target_pairs={{4,0},{8,4},{12,8},{5,1},{9,5},{13,9},{6,2},{10,6},{14,10},{7,3},{... | collective-permute-start | bytes 491528 | tf_op jit(solution)/shard_map/ppermute | solution.py:258
  119.7 2.2 %collective-permute-start.9 = (f32[8,8,640]{2,1,0:T(8,128)S(1)}, f32[8,8,640]{2,1,0:T(8,128)S(1)}, u32[]{:S(2)}, u32[]{:S(2)}) collective-permute-start(f32[8,8,640]{2,1,0:T(8,128)S(1)} %get-tuple-element.38), channel_id=1, source_target_pairs={{0,4},{4,8},{8,12},{1,5},{5,9},{9,13},{2,6},{6,10},{10,14},{3,7},{... | collective-permute-start | bytes 491528 | tf_op jit(solution)/shard_map/ppermute | solution.py:258
  123.3 3.6 %collective-permute-done.9.low_ref.ylow_ref = f32[8,8,640]{2,1,0:T(8,128)S(1)} collective-permute-done((f32[8,8,640]{2,1,0:T(8,128)S(1)}, f32[8,8,640]{2,1,0:T(8,128)S(1)}, u32[]{:S(2)}, u32[]{:S(2)}) %collective-permute-start.9) | collective-permute-done | bytes 163872 | tf_op jit(solution)/shard_map/ppermute | solution.py:258
  127.0 1.9 %collective-permute-start.10 = (f32[5,32,640]{2,1,0:T(8,128)S(1)}, f32[5,32,640]{2,1,0:T(8,128)S(1)}, u32[]{:S(2)}, u32[]{:S(2)}) collective-permute-start(f32[5,32,640]{2,1,0:T(8,128)S(1)} %get-tuple-element.39), channel_id=1, source_target_pairs={{16,0},{32,16},{48,32},{64,48},{80,64},{96,80},{112,96},{17,1},{33... | collective-permute-start | bytes 1228808 | tf_op jit(solution)/shard_map/ppermute | solution.py:258
  128.9 2.4 %collective-permute-start.11 = (f32[5,32,640]{2,1,0:T(8,128)S(1)}, f32[5,32,640]{2,1,0:T(8,128)S(1)}, u32[]{:S(2)}, u32[]{:S(2)}) collective-permute-start(f32[5,32,640]{2,1,0:T(8,128)S(1)} %get-tuple-element.40), channel_id=1, source_target_pairs={{0,16},{16,32},{32,48},{48,64},{64,80},{80,96},{96,112},{1,17},{17... | collective-permute-start | bytes 1228808 | tf_op jit(solution)/shard_map/ppermute | solution.py:258
  131.3 3.0 %collective-permute-done.10.xup_ref = f32[5,32,640]{2,1,0:T(8,128)S(1)} collective-permute-done((f32[5,32,640]{2,1,0:T(8,128)S(1)}, f32[5,32,640]{2,1,0:T(8,128)S(1)}, u32[]{:S(2)}, u32[]{:S(2)}) %collective-permute-start.10) | collective-permute-done | bytes 409632 | tf_op jit(solution)/shard_map/ppermute | solution.py:258
  134.4 3.8 %collective-permute-done.11.xlow_ref = f32[5,32,640]{2,1,0:T(8,128)S(1)} collective-permute-done((f32[5,32,640]{2,1,0:T(8,128)S(1)}, f32[5,32,640]{2,1,0:T(8,128)S(1)}, u32[]{:S(2)}, u32[]{:S(2)}) %collective-permute-start.11) | collective-permute-done | bytes 409632 | tf_op jit(solution)/shard_map/ppermute | solution.py:258
  138.2 15.7 %final.1 = f32[16,32,512]{2,1,0:T(8,128)} custom-call(f32[26,48,640]{2,1,0:T(8,128)S(1)} %get-tuple-element.33.f_ref, f32[26,48,640]{2,1,0:T(8,128)S(1)} %get-tuple-element.34.v_ref, f32[26,48,640]{2,1,0:T(8,128)S(1)} %get-tuple-element.35.ain_ref, f32[8,16,640]{2,1,0:T(8,128)S(1)} %get-tuple-element.36.own_ref, ...), custom_call_target="tpu_custom_call" | custom-call | tf_op jit(solution)/shard_map/final/pallas_call | solution.py:40
  (28 shorter events, 16.1 us)
Async XLA Ops:
  1.3 3.6 %collective-permute-start.1 = (f32[3,128]{1,0:T(4,128)S(1)}, f32[3,128]{1,0:T(4,128)S(1)}, u32[]{:S(2)}, u32[]{:S(2)}) collective-permute-start(f32[3,128]{1,0:T(4,128)S(1)} %get-tuple-element.42), channel_id=1, source_target_pairs={{1,0},{2,1},{3,2},{4,3},{5,4},{6,5},{7,6},{8,7},{9,8},{10,9},{11,1... | collective-permute-start | bytes 4616 | tf_op jit(solution)/shard_map/ppermute | solution.py:654
  1.9 4.2 %collective-permute-start = (f32[3,128]{1,0:T(4,128)S(1)}, f32[3,128]{1,0:T(4,128)S(1)}, u32[]{:S(2)}, u32[]{:S(2)}) collective-permute-start(f32[3,128]{1,0:T(4,128)S(1)} %get-tuple-element.43), channel_id=1, source_target_pairs={{0,1},{1,2},{2,3},{3,4},{4,5},{5,6},{6,7},{7,8},{8,9},{9,10},{10,1... | collective-permute-start | bytes 4616 | tf_op jit(solution)/shard_map/ppermute | solution.py:653
  6.1 1.0 copy-start.2
  7.0 0.9 copy-start.3
  8.0 0.9 copy-start.4
  8.9 0.9 copy-start.5
  9.8 0.8 copy-start.6
  10.5 0.8 copy-start.7
  11.3 0.8 copy-start.8
  40.2 1.2 copy-start
  41.4 1.2 copy-start.1
  57.3 15.5 %collective-permute-start.2 = (f32[2,16,8,512]{3,2,1,0:T(8,128)S(1)}, f32[2,16,8,512]{3,2,1,0:T(8,128)S(1)}, u32[]{:S(2)}, u32[]{:S(2)}) collective-permute-start(f32[2,16,8,512]{3,2,1,0:T(8,128)S(1)} %get-tuple-element.25), channel_id=1, source_target_pairs={{4,0},{8,4},{12,8},{5,1},{9,5},{13,9},{6,2},{10,6},{14,10},{7,3},{... | collective-permute-start | bytes 1572872 | tf_op jit(solution)/shard_map/ppermute | solution.py:258
  61.2 14.9 %collective-permute-start.3 = (f32[2,16,8,512]{3,2,1,0:T(8,128)S(1)}, f32[2,16,8,512]{3,2,1,0:T(8,128)S(1)}, u32[]{:S(2)}, u32[]{:S(2)}) collective-permute-start(f32[2,16,8,512]{3,2,1,0:T(8,128)S(1)} %get-tuple-element.26), channel_id=1, source_target_pairs={{0,4},{4,8},{8,12},{1,5},{5,9},{9,13},{2,6},{6,10},{10,14},{3,7},{... | collective-permute-start | bytes 1572872 | tf_op jit(solution)/shard_map/ppermute | solution.py:258
  76.2 13.5 %collective-permute-start.4 = (f32[2,5,48,512]{3,2,1,0:T(8,128)S(1)}, f32[2,5,48,512]{3,2,1,0:T(8,128)S(1)}, u32[]{:S(2)}, u32[]{:S(2)}) collective-permute-start(f32[2,5,48,512]{3,2,1,0:T(8,128)S(1)} %get-tuple-element.27), channel_id=1, source_target_pairs={{16,0},{32,16},{48,32},{64,48},{80,64},{96,80},{112,96},{17,1},{33... | collective-permute-start | bytes 2949128 | tf_op jit(solution)/shard_map/ppermute | solution.py:258
  78.2 15.4 %collective-permute-start.5 = (f32[2,5,48,512]{3,2,1,0:T(8,128)S(1)}, f32[2,5,48,512]{3,2,1,0:T(8,128)S(1)}, u32[]{:S(2)}, u32[]{:S(2)}) collective-permute-start(f32[2,5,48,512]{3,2,1,0:T(8,128)S(1)} %get-tuple-element.28), channel_id=1, source_target_pairs={{0,16},{16,32},{32,48},{48,64},{64,80},{80,96},{96,112},{1,17},{17... | collective-permute-start | bytes 2949128 | tf_op jit(solution)/shard_map/ppermute | solution.py:258
  94.5 7.2 %collective-permute-start.6 = (f32[32,1280]{1,0:T(8,128)S(1)}, f32[32,1280]{1,0:T(8,128)S(1)}, u32[]{:S(2)}, u32[]{:S(2)}) collective-permute-start(f32[32,1280]{1,0:T(8,128)S(1)} %get-tuple-element.31), channel_id=1, source_target_pairs={{1,0},{2,1},{3,2},{5,4},{6,5},{7,6},{9,8},{10,9},{11,10},{13,12},{... | collective-permute-start | bytes 491528 | tf_op jit(solution)/shard_map/ppermute | solution.py:258
  97.8 7.2 %collective-permute-start.7 = (f32[32,1280]{1,0:T(8,128)S(1)}, f32[32,1280]{1,0:T(8,128)S(1)}, u32[]{:S(2)}, u32[]{:S(2)}) collective-permute-start(f32[32,1280]{1,0:T(8,128)S(1)} %get-tuple-element.32), channel_id=1, source_target_pairs={{0,1},{1,2},{2,3},{4,5},{5,6},{6,7},{8,9},{9,10},{10,11},{12,13},{... | collective-permute-start | bytes 491528 | tf_op jit(solution)/shard_map/ppermute | solution.py:258
  116.1 7.2 %collective-permute-start.8 = (f32[8,8,640]{2,1,0:T(8,128)S(1)}, f32[8,8,640]{2,1,0:T(8,128)S(1)}, u32[]{:S(2)}, u32[]{:S(2)}) collective-permute-start(f32[8,8,640]{2,1,0:T(8,128)S(1)} %get-tuple-element.37), channel_id=1, source_target_pairs={{4,0},{8,4},{12,8},{5,1},{9,5},{13,9},{6,2},{10,6},{14,10},{7,3},{... | collective-permute-start | bytes 491528 | tf_op jit(solution)/shard_map/ppermute | solution.py:258
  119.7 7.2 %collective-permute-start.9 = (f32[8,8,640]{2,1,0:T(8,128)S(1)}, f32[8,8,640]{2,1,0:T(8,128)S(1)}, u32[]{:S(2)}, u32[]{:S(2)}) collective-permute-start(f32[8,8,640]{2,1,0:T(8,128)S(1)} %get-tuple-element.38), channel_id=1, source_target_pairs={{0,4},{4,8},{8,12},{1,5},{5,9},{9,13},{2,6},{6,10},{10,14},{3,7},{... | collective-permute-start | bytes 491528 | tf_op jit(solution)/shard_map/ppermute | solution.py:258
  127.0 7.4 %collective-permute-start.10 = (f32[5,32,640]{2,1,0:T(8,128)S(1)}, f32[5,32,640]{2,1,0:T(8,128)S(1)}, u32[]{:S(2)}, u32[]{:S(2)}) collective-permute-start(f32[5,32,640]{2,1,0:T(8,128)S(1)} %get-tuple-element.39), channel_id=1, source_target_pairs={{16,0},{32,16},{48,32},{64,48},{80,64},{96,80},{112,96},{17,1},{33... | collective-permute-start | bytes 1228808 | tf_op jit(solution)/shard_map/ppermute | solution.py:258
  128.9 9.3 %collective-permute-start.11 = (f32[5,32,640]{2,1,0:T(8,128)S(1)}, f32[5,32,640]{2,1,0:T(8,128)S(1)}, u32[]{:S(2)}, u32[]{:S(2)}) collective-permute-start(f32[5,32,640]{2,1,0:T(8,128)S(1)} %get-tuple-element.40), channel_id=1, source_target_pairs={{0,16},{16,32},{32,48},{48,64},{64,80},{80,96},{96,112},{1,17},{17... | collective-permute-start | bytes 1228808 | tf_op jit(solution)/shard_map/ppermute | solution.py:258

commit v3 on v2

--- a/solution.py
+++ b/solution.py
@@ -6,19 +6,20 @@
 from jax.sharding import PartitionSpec as P
 
 CX, CY, CZ = 16, 32, 512
-W = 5
-EX = CX + 2 * W
-EY = CY + 16
-EZ = CZ + 128
+W = 3
+WC = 5
+EX, EY, EZ = CX + 2 * W, CY + 8, CZ + 128
+KX, KY = CX // 2 + 2 * WC, 32
+T, TE = CZ // 128, EZ // 128
 ZB = -(-EX * EY // 128)
 ALL = ("gx", "gy", "gz")
 NPOINT = 8192
-CAP = 256
 NDEV = 128
 
 CENTRE = 1.125
 SPREAD = 0.875
 RATIO = CENTRE / SPREAD
+SCALE = 1.0 / CENTRE
 
 
 def factors(sweeps):
@@ -30,18 +31,19 @@
     return out
 
 
-def call(kernel, outs, operands, scratch=(), name=None, limit=4, alias=None):
+def call(kernel, outs, operands, scratch=(), name=None, limit=4, alias=None, far=(), far_out=()):
+    vmem, anywhere = pl.BlockSpec(memory_space=pltpu.VMEM), pl.BlockSpec(memory_space=pltpu.HBM)
     specs = [
         pl.BlockSpec(memory_space=pltpu.SMEM)
         if o.dtype == jnp.int32 and o.ndim == 1
-        else pl.BlockSpec(memory_space=pltpu.VMEM)
-        for o in operands
+        else (anywhere if i in far else vmem)
+        for i, o in enumerate(operands)
     ]
     return pl.pallas_call(
         kernel,
         out_shape=[jax.ShapeDtypeStruct(s, jnp.float32) for s in outs],
         in_specs=specs,
-        out_specs=[pl.BlockSpec(memory_space=pltpu.VMEM) for _ in outs],
+        out_specs=[anywhere if i in far_out else vmem for i in range(len(outs))],
         scratch_shapes=list(scratch),
         compiler_params=pltpu.CompilerParams(vmem_limit_bytes=limit << 20),
         input_output_aliases=alias or {},
@@ -57,61 +59,86 @@
     return lax.broadcasted_iota(jnp.int32, shape, len(shape) - 2)
 
 
+def span(x, n):
+    return pl.ds(pl.multiple_of(n * x, 8), n)
+
+
+def get(ref, x, n):
+    return jnp.concatenate([ref[t, span(x, n), :] for t in range(TE)], axis=1)
+
+
+def put_plane(ref, x, value):
+    n = value.shape[0]
+    for t in range(TE):
+        ref[t, span(x, n), :] = value[:, 128 * t : 128 * t + 128]
+
+
+def neighbours(ref, x, n, step):
+    plane = get(ref, x, n)
+    nz = plane.shape[1]
+    beside = get(ref, x - 1, n) + get(ref, x + 1, n)
+    beside = beside + (pltpu.roll(plane, 1, 0) + pltpu.roll(plane, n - 1, 0))
+    return plane, beside + (pltpu.roll(plane, step, 1) + pltpu.roll(plane, nz - step, 1))
+
+
+def planes(first, last, body, group=2):
+    count = (last - first) // group
+
+    def step(i, carry):
+        for j in range(group):
+            body(first + group * i + j)
+        return carry
+
+    lax.fori_loop(0, count, step, 0)
+    for x in range(first + group * count, last):
+        body(x)
+
+
 def x_faces(force_ref, inv_ref, up_ref, low_ref, to_low_ref, to_up_ref):
     for which, ref in ((0, force_ref), (1, inv_ref)):
         for out, first in ((to_low_ref, 0), (to_up_ref, CX - W)):
-            out[which, :, 0:CY, :] = ref[first : first + W]
-            out[which, :, CY : CY + 8, :] = up_ref[which, first : first + W]
-            out[which, :, CY + 8 : CY + 16, :] = low_ref[which, first : first + W]
+            for t in range(T):
+                for p in range(W):
+                    x = first + p
+                    out[which, t, EY * p : EY * p + CY, :] = ref[t, CY * x : CY * x + CY, :]
+                    out[which, t, EY * p + CY : EY * p + EY, :] = jnp.zeros((8, 128), jnp.float32)
+                    for r in range(W):
+                        at = EY * p + CY + r
+                        out[which, t, at : at + 1, :] = up_ref[which, r, t, x : x + 1, :]
+                        at = EY * p + EY - W + r
+                        out[which, t, at : at + 1, :] = low_ref[which, r, t, x : x + 1, :]
 
 
 def assemble(force_ref, inv_ref, yup_ref, ylow_ref, xup_ref, xlow_ref, f_ref, v_ref, to_low_ref, to_up_ref):
     for which, (src, dst) in enumerate(((force_ref, f_ref), (inv_ref, v_ref))):
-        dst[0:W, :, 0:CZ] = xlow_ref[which]
-        dst[W + CX :, :, 0:CZ] = xup_ref[which]
-        dst[W : W + CX, 0:CY, 0:CZ] = src[...]
-        dst[W : W + CX, CY : CY + 8, 0:CZ] = yup_ref[which]
-        dst[W : W + CX, CY + 8 : CY + 16, 0:CZ] = ylow_ref[which]
+        for t in range(T):
+            dst[t, 0 : EY * W, :] = xlow_ref[which, t]
+            dst[t, EY * (W + CX) :, :] = xup_ref[which, t]
+            for x in range(CX):
+                at = EY * (W + x)
+                dst[t, at : at + CY, :] = src[t, CY * x : CY * x + CY, :]
+            at = EY * W + CY
+            for r in range(W):
+                dst[t, pl.ds(at + r, CX, EY), :] = yup_ref[which, r, t]
+                dst[t, pl.ds(at + 8 - W + r, CX, EY), :] = ylow_ref[which, r, t]
+            for r in range(W, 8 - W):
+                dst[t, pl.ds(at + r, CX, EY), :] = jnp.zeros((CX, 128), jnp.float32)
     spot = lanes((128, 128))
     for j in range(ZB):
         first = min(128 * j, EX * EY - 128)
-
-        def edge(ref, at):
-            flat = ref.reshape(EX * EY, EZ)
-            return flat[first : first + 128, at : at + 128]
-
+        at = slice(first, first + 128)
         mixed = jnp.where(
             spot < 16,
-            edge(f_ref, 0),
+            f_ref[0, at, :],
             jnp.where(
                 spot < 32,
-                pltpu.roll(edge(v_ref, 0), 16, 1),
-                jnp.where(
-                    spot < 48,
-                    pltpu.roll(edge(f_ref, CZ - 128), 48, 1),
-                    pltpu.roll(edge(v_ref, CZ - 128), 64, 1),
-                ),
+                pltpu.roll(v_ref[0, at, :], 16, 1),
+                jnp.where(spot < 48, pltpu.roll(f_ref[T - 1, at, :], 48, 1), pltpu.roll(v_ref[T - 1, at, :], 64, 1)),
             ),
         )
         turned = mixed.T
         to_low_ref[:, 128 * j : 128 * j + 128] = turned[0:32]
         to_up_ref[:, 128 * j : 128 * j + 128] = turned[32:64]
-
-
-def neighbours(ref, x, step):
-    plane = ref[x]
-    ny, nz = plane.shape
-    beside = ref[x - 1] + ref[x + 1]
-    beside = beside + (pltpu.roll(plane, 1, 0) + pltpu.roll(plane, ny - 1, 0))
-    return plane, beside + (pltpu.roll(plane, step, 1) + pltpu.roll(plane, nz - step, 1))
-
-
-def planes(first, last, body):
-    def step(x, carry):
-        body(x)
-        return carry
-
-    lax.fori_loop(first, last, step, 0)
 
 
 def smooth_kernel(_fin_ref, _vin_ref, zup_ref, zlow_ref, f_ref, v_ref, a_ref, to_low_ref, to_up_ref, coarse_ref, b_ref, tmp_ref):
@@ -121,135 +148,185 @@
         at = slice(128 * j, 128 * j + 128)
         for dst, part in ((f_ref, slice(0, 16)), (v_ref, slice(16, 32))):
             stack = jnp.concatenate([zup_ref[part, at], gap, zlow_ref[part, at]], axis=0)
-            dst.reshape(EX * EY, EZ)[first : first + 128, CZ:] = stack.T
-    scale = 1.0 / CENTRE
+            dst[T, first : first + 128, :] = stack.T
 
     def start(x):
-        a_ref[x] = v_ref[x] * f_ref[x] * scale
+        put_plane(a_ref, x, get(v_ref, x, EY) * get(f_ref, x, EY) * SCALE)
 
     planes(0, EX, start)
     (a1, b1), (a2, b2) = factors(3)
 
     def second(x):
-        plane, beside = neighbours(a_ref, x, 1)
-        left = v_ref[x] * (f_ref[x] + beside) - plane
-        b_ref[x] = (1.0 + a1) * plane + b1 * left
+        plane, beside = neighbours(a_ref, x, EY, 1)
+        left = get(v_ref, x, EY) * (get(f_ref, x, EY) + beside) - plane
+        put_plane(b_ref, x, (1.0 + a1) * plane + b1 * left)
 
     planes(1, EX - 1, second)
 
     def third(x):
-        plane, beside = neighbours(b_ref, x, 1)
-        left = v_ref[x] * (f_ref[x] + beside) - plane
-        a_ref[x] = plane + a2 * (plane - a_ref[x]) + b2 * left
+        plane, beside = neighbours(b_ref, x, EY, 1)
+        left = get(v_ref, x, EY) * (get(f_ref, x, EY) + beside) - plane
+        put_plane(a_ref, x, plane + a2 * (plane - get(a_ref, x, EY)) + b2 * left)
 
     planes(2, EX - 2, third)
-
-    def restrict(xc, carry):
-        total = jnp.zeros((CY, EZ), jnp.float32)
-        weight = jnp.zeros((CY, EZ), jnp.float32)
+    even = lanes((CY // 2, EZ)) % 2 == 0
+
+    def restrict(xc):
+        total, weight = [], []
         for half in range(2):
             x = W + 2 * xc + half
-            plane, beside = neighbours(a_ref, x, 1)
-            inv = v_ref[x, 0:CY]
+            plane, beside = neighbours(a_ref, x, EY, 1)
+            inv = get(v_ref, x, EY)[0:CY]
             diag = jnp.where(inv > 0.0, 1.0 / inv, 0.0)
-            total = total + ((f_ref[x] + beside)[0:CY] - diag * plane[0:CY])
-            weight = weight + diag
-        even = lanes((CY // 2, EZ)) % 2 == 0
-
-        def pairs(value):
+            total.append((get(f_ref, x, EY) + beside)[0:CY] - diag * plane[0:CY])
+            weight.append(diag)
+
+        def pairs(value, slot):
             value = value + pltpu.roll(value, EZ - 1, 1)
             parts = []
-            for t in range(EZ // 128):
-                tmp_ref[t] = value[:, 128 * t : 128 * t + 128]
-                parts.append(tmp_ref[t, pl.ds(0, CY // 2, 2)] + tmp_ref[t, pl.ds(1, CY // 2, 2)])
+            for t in range(TE):
+                tmp_ref[slot, t] = value[:, 128 * t : 128 * t + 128]
+                parts.append(tmp_ref[slot, t, pl.ds(0, CY // 2, 2)] + tmp_ref[slot, t, pl.ds(1, CY // 2, 2)])
             return jnp.concatenate(parts, axis=1)
 
-        rhs = 0.5 * pairs(total)
-        whole = pairs(weight)
+        rhs = 0.5 * pairs(total[0] + total[1], 0)
+        whole = pairs(weight[0] + weight[1], 1)
         inv = jnp.where(whole > 0.0, 1.0 / (6.0 + 0.5 * (whole - 48.0)), 0.0)
-        both = jnp.where(even, rhs, pltpu.roll(inv, 1, 1))
-        coarse_ref[xc] = both
-        to_low_ref[xc] = both[0:8]
-        to_up_ref[xc] = both[8:16]
-        return carry
-
-    lax.fori_loop(0, CX // 2, restrict, 0)
-
-
-def coarse_faces(own_ref, up_ref, low_ref, to_low_ref, to_up_ref):
-    for out, first in ((to_low_ref, 0), (to_up_ref, CX // 2 - W)):
-        out[:, 0:16] = own_ref[first : first + W]
-        out[:, 16:24] = up_ref[first : first + W]
-        out[:, 24:32] = low_ref[first : first + W]
-
-
-def final_kernel(f_ref, v_ref, ain_ref, own_ref, yup_ref, ylow_ref, xup_ref, xlow_ref, out_ref, a_ref, b_ref, cb_ref, cv_ref, ca_ref, cc_ref, tmp_ref):
-    even = lanes((32, EZ)) % 2 == 0
-
-    def unpack(x, value):
-        cb_ref[x] = jnp.where(even, value, pltpu.roll(value, 1, 1))
-        cv_ref[x] = jnp.where(even, pltpu.roll(value, EZ - 1, 1), value)
-
-    for x in range(W):
-        unpack(x, xlow_ref[x])
-        unpack(x + W + CX // 2, xup_ref[x])
-    for x in range(CX // 2):
-        unpack(x + W, jnp.concatenate([own_ref[x], yup_ref[x], ylow_ref[x]], axis=0))
+        put_plane(coarse_ref, xc, jnp.where(even, rhs, pltpu.roll(inv, 1, 1)))
+
+    planes(0, CX // 2, restrict, 1)
+    for t in range(TE):
+        for r in range(WC):
+            at = 8 * (r * TE + t)
+            to_low_ref[at : at + 8, :] = coarse_ref[t, pl.ds(r, CX // 2, CY // 2), :]
+            to_up_ref[at : at + 8, :] = coarse_ref[t, pl.ds(CY // 2 - WC + r, CX // 2, CY // 2), :]
+        for r in range(W):
+            at = 8 * WC * TE + 16 * (r * TE + t)
+            to_low_ref[at : at + 16, :] = a_ref[t, pl.ds(EY * W + r, CX, EY), :]
+            to_up_ref[at : at + 16, :] = a_ref[t, pl.ds(EY * W + CY - W + r, CX, EY), :]
+
+
+def coarse_faces(own_ref, a_ref, up_ref, low_ref, to_low_ref, to_up_ref):
+    none = jnp.zeros((8, 128), jnp.float32)
+    for t in range(TE):
+        for out, first in ((to_low_ref, 0), (to_up_ref, CX // 2 - WC)):
+            for p in range(WC):
+                x = first + p
+                out[t, KY * p : KY * p + 16, :] = own_ref[t, 16 * x : 16 * x + 16, :]
+                out[t, KY * p + 16 : KY * p + 24, :] = none
+                out[t, KY * p + 24 : KY * p + 32, :] = none
+            for r in range(WC):
+                at = 8 * (r * TE + t) + first
+                out[t, pl.ds(16 + r, WC, KY), :] = up_ref[at : at + WC, :]
+                out[t, pl.ds(KY - WC + r, WC, KY), :] = low_ref[at : at + WC, :]
+        base = KY * WC
+        for out, first in ((to_low_ref, 0), (to_up_ref, CX - W)):
+            for p in range(W):
+                at, x = base + EY * p, EY * (W + first + p)
+                out[t, at : at + CY, :] = a_ref[t, x : x + CY, :]
+                out[t, at + CY : at + EY, :] = none
+            for r in range(W):
+                at = 8 * WC * TE + 16 * (r * TE + t) + first
+                out[t, pl.ds(base + CY + r, W, EY), :] = up_ref[at : at + W, :]
+                out[t, pl.ds(base + EY - W + r, W, EY), :] = low_ref[at : at + W, :]
+
+
+def final_kernel(f_ref, v_ref, ain_ref, own_ref, yup_ref, ylow_ref, xup_ref, xlow_ref, out_ref, a_ref, b_ref, cb_ref, cv_ref, ca_ref, cc_ref, tmp_ref, res_ref, sems):
+    half = CX // 2
+    base = KY * WC
+    for t in range(TE):
+        cc_ref[t, 0:base, :] = xlow_ref[t, 0:base, :]
+        cc_ref[t, KY * (WC + half) :, :] = xup_ref[t, 0:base, :]
+        a_ref[t, 0 : EY * W, :] = xlow_ref[t, base:, :]
+        a_ref[t, EY * (W + CX) :, :] = xup_ref[t, base:, :]
+        for x in range(half):
+            at = KY * (WC + x)
+            cc_ref[t, at : at + 16, :] = own_ref[t, 16 * x : 16 * x + 16, :]
+        at = KY * WC + 16
+        for r in range(WC):
+            src = slice(8 * (r * TE + t), 8 * (r * TE + t) + 8)
+            cc_ref[t, pl.ds(at + r, half, KY), :] = yup_ref[src, :]
+            cc_ref[t, pl.ds(at + 16 - WC + r, half, KY), :] = ylow_ref[src, :]
+        for r in range(WC, 16 - WC):
+            cc_ref[t, pl.ds(at + r, half, KY), :] = jnp.zeros((half, 128), jnp.float32)
+        at = EY * W + CY
+        for r in range(W):
+            first = 8 * WC * TE + 16 * (r * TE + t)
+            a_ref[t, pl.ds(at + r, CX, EY), :] = yup_ref[first : first + 16, :]
+            a_ref[t, pl.ds(at + 8 - W + r, CX, EY), :] = ylow_ref[first : first + 16, :]
+        for r in range(W, 8 - W):
+            a_ref[t, pl.ds(at + r, CX, EY), :] = jnp.zeros((CX, 128), jnp.float32)
+    even = lanes((KY, EZ)) % 2 == 0
     (a1, b1), (a2, b2), (a3, b3) = factors(4)
-    scale = 1.0 / CENTRE
-    ex = CX // 2 + 2 * W
 
     def start(x):
-        ca_ref[x] = cv_ref[x] * cb_ref[x] * scale
-
-    planes(0, ex, start)
+        both = get(cc_ref, x, KY)
+        right = jnp.where(even, both, pltpu.roll(both, 1, 1))
+        inv = jnp.where(even, pltpu.roll(both, EZ - 1, 1), both)
+        put_plane(cb_ref, x, right)
+        put_plane(cv_ref, x, inv)
+        put_plane(ca_ref, x, inv * right * SCALE)
+
+    planes(0, KX, start)
 
     def sweep(src, dst, first, last, a, b, fresh):
         def body(x):
-            plane, beside = neighbours(src, x, 2)
-            left = cv_ref[x] * (cb_ref[x] + beside) - plane
-            step = plane if fresh else plane - dst[x]
-            dst[x] = plane + a * step + b * left
+            plane, beside = neighbours(src, x, KY, 2)
+            left = get(cv_ref, x, KY) * (get(cb_ref, x, KY) + beside) - plane
+            step = plane if fresh else plane - get(dst, x, KY)
+            put_plane(dst, x, plane + a * step + b * left)
 
         planes(first, last, body)
 
-    sweep(ca_ref, cc_ref, 1, ex - 1, a1, b1, True)
-    sweep(cc_ref, ca_ref, 2, ex - 2, a2, b2, False)
-    sweep(ca_ref, cc_ref, 3, ex - 3, a3, b3, False)
-
-    def spread(x):
-        coarse = cc_ref[(x + W) // 2]
-        for t in range(EZ // 128):
-            at = slice(128 * t, 128 * t + 128)
-            tmp_ref[t, pl.ds(0, 32, 2)] = coarse[:, at]
-            tmp_ref[t, pl.ds(1, 32, 2)] = coarse[:, at]
-            a_ref[x, 0:40, at] = ain_ref[x, 0:40, at] + tmp_ref[t, 0:40]
-            a_ref[x, 40:48, at] = ain_ref[x, 40:48, at] + tmp_ref[t, 56:64]
-
-    planes(2, EX - 2, spread)
+    sweep(ca_ref, cc_ref, 1, KX - 1, a1, b1, True)
+    sweep(cc_ref, ca_ref, 2, KX - 2, a2, b2, False)
+    sweep(ca_ref, cc_ref, 3, KX - 3, a3, b3, False)
+    low = rows((8, 128)) < 4
+
+    def spread(x, src):
+        xc = (x - W + 2 * WC) // 2
+        for t in range(TE):
+            coarse = cc_ref[t, span(xc, KY), :]
+            tmp_ref[t, pl.ds(0, 32, 2)] = coarse
+            tmp_ref[t, pl.ds(1, 32, 2)] = coarse
+            at = EY * x
+            own, rim = pl.ds(pl.multiple_of(at, 8), CY), pl.ds(pl.multiple_of(at + CY, 8), 8)
+            a_ref[t, own, :] = src[t, own, :] + tmp_ref[t, 0:CY]
+            a_ref[t, rim, :] = a_ref[t, rim, :] + jnp.where(low, tmp_ref[t, 32:40], tmp_ref[t, 56:64])
+
+    planes(0, W, lambda x: spread(x, a_ref), 1)
+    planes(W, W + CX, lambda x: spread(x, ain_ref), 1)
+    planes(W + CX, EX, lambda x: spread(x, a_ref), 1)
     (a1, b1), (a2, b2) = factors(3)
 
     def first(x):
-        plane, beside = neighbours(a_ref, x, 1)
-        left = v_ref[x] * (f_ref[x] + beside) - plane
-        b_ref[x] = plane + scale * left
-
-    planes(3, EX - 3, first)
+        plane, beside = neighbours(a_ref, x, EY, 1)
+        left = get(v_ref, x, EY) * (get(f_ref, x, EY) + beside) - plane
+        put_plane(b_ref, x, plane + SCALE * left)
+
+    planes(1, EX - 1, first)
 
     def second(x):
-        plane, beside = neighbours(b_ref, x, 1)
-        left = v_ref[x] * (f_ref[x] + beside) - plane
-        a_ref[x] = plane + a1 * (plane - a_ref[x]) + b1 * left
-
-    planes(4, EX - 4, second)
+        plane, beside = neighbours(b_ref, x, EY, 1)
+        left = get(v_ref, x, EY) * (get(f_ref, x, EY) + beside) - plane
+        put_plane(a_ref, x, plane + a1 * (plane - get(a_ref, x, EY)) + b1 * left)
+
+    planes(2, EX - 2, second)
 
     def third(x):
-        plane, beside = neighbours(a_ref, x, 1)
-        left = v_ref[x] * (f_ref[x] + beside) - plane
-        full = plane + a2 * (plane - b_ref[x]) + b2 * left
-        out_ref[x - W] = full[0:CY, 0:CZ]
-
-    planes(W, W + CX, third)
+        plane, beside = neighbours(a_ref, x, EY, 1)
+        left = get(v_ref, x, EY) * (get(f_ref, x, EY) + beside) - plane
+        full = plane + a2 * (plane - get(b_ref, x, EY)) + b2 * left
+        res_ref[x - W] = full[0:CY, 0:CZ]
+
+    copies = []
+    for i in range(4):
+        at = pl.ds(4 * i, 4)
+        planes(W + 4 * i, W + 4 * i + 4, third)
+        copies.append(pltpu.make_async_copy(res_ref.at[at], out_ref.at[at], sems.at[i]))
+        copies[-1].start()
+    for copy in copies:
+        copy.wait()
 
 
 def swap(low, high, axis):
@@ -260,10 +337,10 @@
 
 def solve(forcing, inverse, to_low, to_up):
     yup, ylow = swap(to_low, to_up, "gy")
-    face = (2, W, EY, CZ)
+    face = (2, T, W * EY, 128)
     xs = call(x_faces, [face, face], (forcing, inverse, yup, ylow), name="x_faces")
     xup, xlow = swap(*xs, "gx")
-    ext = (EX, EY, EZ)
+    ext = (TE, EX * EY, 128)
     f, v, zl, zu = call(
         assemble,
         [ext, ext, (32, 128 * ZB), (32, 128 * ZB)],
@@ -271,29 +348,30 @@
         name="assemble",
     )
     zup, zlow = swap(zl, zu, "gz")
-    cy, cx = (CX // 2, 8, EZ), (W, 32, EZ)
+    cy, cx = (8 * TE * (WC + 2 * W), 128), (TE, KY * WC + EY * W, 128)
     f, v, a, yl, yu, own = call(
         smooth_kernel,
-        [ext, ext, ext, cy, cy, (CX // 2, CY // 2, EZ)],
+        [ext, ext, ext, cy, cy, (TE, CX // 2 * CY // 2, 128)],
         (f, v, zup, zlow),
-        [pltpu.VMEM(ext, jnp.float32), pltpu.VMEM((EZ // 128, CY, 128), jnp.float32)],
+        [pltpu.VMEM(ext, jnp.float32), pltpu.VMEM((2, TE, CY, 128), jnp.float32)],
         name="smooth",
         limit=8,
         alias={0: 0, 1: 1},
     )
     yup, ylow = swap(yl, yu, "gy")
-    xs = call(coarse_faces, [cx, cx], (own, yup, ylow), name="coarse_faces")
+    xs = call(coarse_faces, [cx, cx], (own, a, yup, ylow), name="coarse_faces")
     xup, xlow = swap(*xs, "gx")
-    cext = (CX // 2 + 2 * W, 32, EZ)
+    cext = pltpu.VMEM((TE, KX * KY, 128), jnp.float32)
     return call(
         final_kernel,
         [(CX, CY, CZ)],
         (f, v, a, own, yup, ylow, xup, xlow),
         [pltpu.VMEM(ext, jnp.float32)] * 2
-        + [pltpu.VMEM(cext, jnp.float32)] * 4
-        + [pltpu.VMEM((EZ // 128, 64, 128), jnp.float32)],
+        + [cext] * 4
+        + [pltpu.VMEM((TE, 64, 128), jnp.float32), pltpu.VMEM((CX, CY, CZ), jnp.float32), pltpu.SemaphoreType.DMA((4,))],
         name="final",
         limit=20,
+        far_out=(0,),
     )[0]
 
 
@@ -587,33 +665,42 @@
     lax.fori_loop(0, 8, block, 0)
 
 
-def scatter_kernel(rhs_ref, shift_ref, got_ref, force_ref, inv_ref, to_low_ref, to_up_ref, key_ref, val_ref, rank_ref, turn_key_ref, turn_val_ref):
+def scatter_kernel(rhs_hbm, shift_hbm, got_ref, force_ref, inv_ref, to_low_ref, to_up_ref, rhs_ref, shift_ref, key_ref, val_ref, rank_ref, turn_key_ref, turn_val_ref, sems):
+    rhs_copy = pltpu.make_async_copy(rhs_hbm, rhs_ref, sems.at[0])
+    shift_copy = pltpu.make_async_copy(shift_hbm, shift_ref, sems.at[1])
+    rhs_copy.start()
+    shift_copy.start()
     unpack_and_merge(got_ref, key_ref, val_ref)
     combine(key_ref, val_ref, rank_ref)
     concentrate(key_ref, val_ref, rank_ref, turn_key_ref, turn_val_ref)
+    rhs_copy.wait()
+    shift_copy.wait()
 
     def write(q, u, values):
         x = 2 * q + u // 2
         for i, value in enumerate(values):
-            row, lane = 16 * (u % 2) + 8 * (i // 4), 128 * (i % 4)
-            at = (x, slice(row, row + 8), slice(lane, lane + 128))
-            force_ref[at] = rhs_ref[at] + value
+            row, t = 16 * (u % 2) + 8 * (i // 4), i % 4
+            at = (x, slice(row, row + 8), slice(128 * t, 128 * t + 128))
+            to = (t, pl.ds(pl.multiple_of(CY * x + row, 8), 8))
+            force_ref[to] = rhs_ref[at] + value
+            inv_ref[to] = 1.0 / (6.0 + shift_ref[at])
 
     distribute(turn_key_ref, turn_val_ref, rank_ref, val_ref, write)
-
-    def finish(x, carry):
-        force = force_ref[x]
-        inv = 1.0 / (6.0 + shift_ref[x])
-        inv_ref[x] = inv
-        for which, value in ((0, force), (1, inv)):
-            to_low_ref[which, x] = value[0:8]
-            to_up_ref[which, x] = value[CY - 8 : CY]
-        return carry
-
-    lax.fori_loop(0, CX, finish, 0)
-
-
-def points_kernel(begin_ref, pos_ref, low_ref, up_ref, nrm_ref, ten_ref, edge_ref, conn_ref, owner_ref, cell_ref, force_ref, send_ref, jump_ref, key_ref, val_ref, goal_ref):
+    for which, ref in ((0, force_ref), (1, inv_ref)):
+        for r in range(W):
+            for t in range(T):
+                to_low_ref[which, r, t] = ref[t, pl.ds(r, CX, CY), :]
+                to_up_ref[which, r, t] = ref[t, pl.ds(CY - W + r, CX, CY), :]
+
+
+def points_kernel(begin_ref, low_ref, up_ref, pos_hbm, nrm_hbm, ten_hbm, edge_hbm, conn_hbm, owner_hbm, cell_hbm, force_ref, send_ref, pos_ref, nrm_ref, ten_ref, edge_ref, conn_ref, owner_ref, cell_ref, jump_ref, key_ref, val_ref, goal_ref, sems):
+    far = (pos_hbm, nrm_hbm, ten_hbm, edge_hbm, conn_hbm, owner_hbm, cell_hbm)
+    near = (pos_ref, nrm_ref, ten_ref, edge_ref, conn_ref, owner_ref, cell_ref)
+    copies = [pltpu.make_async_copy(a, b, sems.at[i]) for i, (a, b) in enumerate(zip(far, near))]
+    for copy in copies:
+        copy.start()
+    for copy in copies:
+        copy.wait()
     half = lanes((1, 128)) < 64
     tiles = NPOINT // 128
 
@@ -659,9 +746,9 @@
         [(3, NPOINT), (4 * NDEV, 128)],
         (
             begin,
-            positions,
             low,
             up,
+            positions,
             normals,
             tension.reshape(flat),
             edge_weight,
@@ -669,19 +756,25 @@
             owner_map.reshape(flat),
             cell_map.reshape(flat),
         ),
-        [pltpu.VMEM(flat, jnp.float32), whole, pltpu.VMEM(flat, jnp.float32), whole],
+        [pltpu.VMEM((3, NPOINT), jnp.float32)] * 2
+        + [pltpu.VMEM(flat, jnp.float32), pltpu.VMEM((6, NPOINT), jnp.float32), pltpu.VMEM((6, NPOINT), jnp.int32)]
+        + [whole, whole, pltpu.VMEM(flat, jnp.float32), whole, pltpu.VMEM(flat, jnp.float32), whole]
+        + [pltpu.SemaphoreType.DMA((7,))],
+        far=range(3, 10),
         name="points",
     )
     got = lax.all_to_all(send, ALL, 0, 0, tiled=True)
-    block = (CX, CY, CZ)
+    block = pltpu.VMEM((CX, CY, CZ), jnp.float32)
     list_i, list_f = pltpu.VMEM((256, 128), jnp.int32), pltpu.VMEM((256, 128), jnp.float32)
+    own, face = (T, CX * CY, 128), (2, W, T, CX, 128)
     forcing, inverse, to_low, to_up = call(
         scatter_kernel,
-        [block, block, (2, CX, 8, CZ), (2, CX, 8, CZ)],
+        [own, own, face, face],
         (pressure_rhs, shift_diag, got),
-        [list_i, list_f, list_i, list_i, list_f],
+        [block, block, list_i, list_f, list_i, list_i, list_f, pltpu.SemaphoreType.DMA((2,))],
         name="scatter",
         limit=8,
+        far=(0, 1),
     )
     return solve(forcing, inverse, to_low, to_up), force
 

time: 155 us -> 139 us (0.90)
  waiting for transfers between devices: 45.1 us -> 36.3 us
  Pallas kernels: 48.3 us -> 41.1 us
    ppermute x5, waiting for transfers between devices: 24.6 us -> 15.7 us  [swap(): lax.ppermute(low, axis, [(b, a) for a, b in up])]
    pallas_call x7, Pallas kernels: 48.3 us -> 41.1 us  [call(): pl.pallas_call(kernel, out_shape=[jax.ShapeDtypeStruct(s, jnp.float32) fo...]
where the time goes in v3:
time: 139 us; the launch traced here: 138 us
  Pallas kernels  41.1 us (30%)
  waiting for transfers between devices  36.3 us (26%)
  starting transfers between devices  28.2 us (20%)
  blocking collectives  22.2 us (16%)
  local copies, waits for them, and re-layouts  9.13 us (7%)
    pallas_call x7, Pallas kernels, call(): pl.pallas_call(kernel, out_shape=[jax.ShapeDtypeStruct(s, jnp.float32) fo...  41.1 us
    all_to_all x1, blocking collectives, body(): got = lax.all_to_all(send, ALL, 0, 0, tiled=True)  22.2 us
    ppermute x5, waiting for transfers between devices, swap(): lax.ppermute(high, axis, up)  17.9 us
    ppermute x5, waiting for transfers between devices, swap(): lax.ppermute(low, axis, [(b, a) for a, b in up])  15.7 us
    ppermute x5, starting transfers between devices, swap(): lax.ppermute(low, axis, [(b, a) for a, b in up])  14.7 us
    ppermute x5, starting transfers between devices, swap(): lax.ppermute(high, axis, up)  11.5 us
    unnamed x18, local copies, waits for them, and re-layouts  8.43 us
  transfers between devices with their start and end apart: 12, of which 12 were waited for; matrix products, arithmetic and copies ran while one was open for 0% of the time, Pallas kernels for 0%

profile of v3, /device:TPU:50, one launch (start us, length us, event | category | flops | bytes accessed | tf_op | source)
XLA Modules:
  0.0 137.9 jit_solution(15357207486607891133)
XLA Ops:
  12.1 6.5 %points.1 = (f32[3,8192]{1,0:T(4,128)}, f32[512,128]{1,0:T(8,128)S(1)}) custom-call(s32[2]{0:T(128)S(1)} %pad_add_fusion.begin_ref, f32[3,128]{1,0:T(4,128)S(1)} %collective-permute-done.low_ref, f32[3,128]{1,0:T(4,128)S(1)} %collective-permute-done.1.up_ref, f32[3,8192]{1,0:T(4,128)S(1)} %copy-done.4, f32[3,8192]{1,0:T(4,128)S(1)} %copy-done.5, ...), custom_call_target="tpu_custom_call" | custom-call | tf_op jit(solution)/shard_map/points/pallas_call | solution.py:42
  18.5 22.2 %all_to_all.11 = f32[128,4,128]{2,1,0:T(4,128)S(1)} all-to-all(f32[128,4,128]{2,1,0:T(4,128)S(1)} %bitcast.8), channel_id=1, replica_groups=mesh['gx'=8,'gy'=4,'gz'=4] {'gx','gy','gz'}, dimensions={0} | all-to-all | bytes 524288 | tf_op jit(solution)/shard_map/all_to_all | solution.py:766
  43.2 14.8 %scatter.1 = (f32[4,512,128]{2,1,0:T(8,128)S(1)}, f32[4,512,128]{2,1,0:T(8,128)S(1)}, f32[2,3,4,16,128]{4,3,2,1,0:T(8,128)S(1)}, f32[2,3,4,16,128]{4,3,2,1,0:T(8,128)S(1)}) custom-call(f32[16,32,512]{2,1,0:T(8,128)S(1)} %copy-done, f32[16,32,512]{2,1,0:T(8,128)S(1)} %copy-done.1, f32[512,128]{1,0:T(8,128)S(1)} %bitcast.7), custom_call_target="tpu_custom_call" | custom-call | tf_op jit(solution)/shard_map/scatter/pallas_call | solution.py:42
  58.0 3.9 %collective-permute-start.2 = (f32[2,3,4,16,128]{4,3,2,1,0:T(8,128)S(1)}, f32[2,3,4,16,128]{4,3,2,1,0:T(8,128)S(1)}, u32[]{:S(2)}, u32[]{:S(2)}) collective-permute-start(f32[2,3,4,16,128]{4,3,2,1,0:T(8,128)S(1)} %get-tuple-element.25), channel_id=1, source_target_pairs={{4,0},{8,4},{12,8},{5,1},{9,5},{13,9},{6,2},{10,6},{14,10},{7,3},{... | collective-permute-start | bytes 589832 | tf_op jit(solution)/shard_map/ppermute | solution.py:335
  61.9 2.0 %collective-permute-start.3 = (f32[2,3,4,16,128]{4,3,2,1,0:T(8,128)S(1)}, f32[2,3,4,16,128]{4,3,2,1,0:T(8,128)S(1)}, u32[]{:S(2)}, u32[]{:S(2)}) collective-permute-start(f32[2,3,4,16,128]{4,3,2,1,0:T(8,128)S(1)} %get-tuple-element.26), channel_id=1, source_target_pairs={{0,4},{4,8},{8,12},{1,5},{5,9},{9,13},{2,6},{6,10},{10,14},{3,7},{... | collective-permute-start | bytes 589832 | tf_op jit(solution)/shard_map/ppermute | solution.py:335
  63.9 2.7 %collective-permute-done.2.up_ref.yup_ref = f32[2,3,4,16,128]{4,3,2,1,0:T(8,128)S(1)} collective-permute-done((f32[2,3,4,16,128]{4,3,2,1,0:T(8,128)S(1)}, f32[2,3,4,16,128]{4,3,2,1,0:T(8,128)S(1)}, u32[]{:S(2)}, u32[]{:S(2)}) %collective-permute-start.2) | collective-permute-done | bytes 196640 | tf_op jit(solution)/shard_map/ppermute | solution.py:335
  66.6 3.3 %collective-permute-done.3.low_ref.ylow_ref = f32[2,3,4,16,128]{4,3,2,1,0:T(8,128)S(1)} collective-permute-done((f32[2,3,4,16,128]{4,3,2,1,0:T(8,128)S(1)}, f32[2,3,4,16,128]{4,3,2,1,0:T(8,128)S(1)}, u32[]{:S(2)}, u32[]{:S(2)}) %collective-permute-start.3) | collective-permute-done | bytes 196640 | tf_op jit(solution)/shard_map/ppermute | solution.py:335
  70.0 1.9 %collective-permute-start.4 = (f32[2,4,120,128]{3,2,1,0:T(8,128)S(1)}, f32[2,4,120,128]{3,2,1,0:T(8,128)S(1)}, u32[]{:S(2)}, u32[]{:S(2)}) collective-permute-start(f32[2,4,120,128]{3,2,1,0:T(8,128)S(1)} %get-tuple-element.27), channel_id=1, source_target_pairs={{16,0},{32,16},{48,32},{64,48},{80,64},{96,80},{112,96},{17,1},{33... | collective-permute-start | bytes 1474568 | tf_op jit(solution)/shard_map/ppermute | solution.py:335
  71.9 2.4 %collective-permute-start.5 = (f32[2,4,120,128]{3,2,1,0:T(8,128)S(1)}, f32[2,4,120,128]{3,2,1,0:T(8,128)S(1)}, u32[]{:S(2)}, u32[]{:S(2)}) collective-permute-start(f32[2,4,120,128]{3,2,1,0:T(8,128)S(1)} %get-tuple-element.28), channel_id=1, source_target_pairs={{0,16},{16,32},{32,48},{48,64},{64,80},{80,96},{96,112},{1,17},{17... | collective-permute-start | bytes 1474568 | tf_op jit(solution)/shard_map/ppermute | solution.py:335
  74.3 3.9 %collective-permute-done.4.xup_ref = f32[2,4,120,128]{3,2,1,0:T(8,128)S(1)} collective-permute-done((f32[2,4,120,128]{3,2,1,0:T(8,128)S(1)}, f32[2,4,120,128]{3,2,1,0:T(8,128)S(1)}, u32[]{:S(2)}, u32[]{:S(2)}) %collective-permute-start.4) | collective-permute-done | bytes 491552 | tf_op jit(solution)/shard_map/ppermute | solution.py:335
  78.2 3.8 %collective-permute-done.5.xlow_ref = f32[2,4,120,128]{3,2,1,0:T(8,128)S(1)} collective-permute-done((f32[2,4,120,128]{3,2,1,0:T(8,128)S(1)}, f32[2,4,120,128]{3,2,1,0:T(8,128)S(1)}, u32[]{:S(2)}, u32[]{:S(2)}) %collective-permute-start.5) | collective-permute-done | bytes 491552 | tf_op jit(solution)/shard_map/ppermute | solution.py:335
  82.8 3.3 %collective-permute-start.6 = (f32[32,896]{1,0:T(8,128)S(1)}, f32[32,896]{1,0:T(8,128)S(1)}, u32[]{:S(2)}, u32[]{:S(2)}) collective-permute-start(f32[32,896]{1,0:T(8,128)S(1)} %get-tuple-element.31), channel_id=1, source_target_pairs={{1,0},{2,1},{3,2},{5,4},{6,5},{7,6},{9,8},{10,9},{11,10},{13,12},{... | collective-permute-start | bytes 344072 | tf_op jit(solution)/shard_map/ppermute | solution.py:335
  86.1 2.5 %collective-permute-start.7 = (f32[32,896]{1,0:T(8,128)S(1)}, f32[32,896]{1,0:T(8,128)S(1)}, u32[]{:S(2)}, u32[]{:S(2)}) collective-permute-start(f32[32,896]{1,0:T(8,128)S(1)} %get-tuple-element.32), channel_id=1, source_target_pairs={{0,1},{1,2},{2,3},{4,5},{5,6},{6,7},{8,9},{9,10},{10,11},{12,13},{... | collective-permute-start | bytes 344072 | tf_op jit(solution)/shard_map/ppermute | solution.py:335
  89.5 3.3 %collective-permute-done.7.zlow_ref = f32[32,896]{1,0:T(8,128)S(1)} collective-permute-done((f32[32,896]{1,0:T(8,128)S(1)}, f32[32,896]{1,0:T(8,128)S(1)}, u32[]{:S(2)}, u32[]{:S(2)}) %collective-permute-start.7) | collective-permute-done | bytes 114720 | tf_op jit(solution)/shard_map/ppermute | solution.py:335
  92.8 6.9 %smooth.1 = (f32[5,880,128]{2,1,0:T(8,128)S(1)}, f32[5,880,128]{2,1,0:T(8,128)S(1)}, f32[5,880,128]{2,1,0:T(8,128)S(1)}, f32[440,128]{1,0:T(8,128)S(1)}, f32[440...) custom-call(f32[5,880,128]{2,1,0:T(8,128)S(1)} %get-tuple-element.29._fin_ref, ...), custom_call_target="tpu_custom_call", output_to_operand_aliasing={{0}: (0, {}), {1}: (1, {})} | custom-call | tf_op jit(solution)/shard_map/smooth/pallas_call | solution.py:42
  99.7 3.6 %collective-permute-start.8 = (f32[440,128]{1,0:T(8,128)S(1)}, f32[440,128]{1,0:T(8,128)S(1)}, u32[]{:S(2)}, u32[]{:S(2)}) collective-permute-start(f32[440,128]{1,0:T(8,128)S(1)} %get-tuple-element.37), channel_id=1, source_target_pairs={{4,0},{8,4},{12,8},{5,1},{9,5},{13,9},{6,2},{10,6},{14,10},{7,3},{... | collective-permute-start | bytes 675848 | tf_op jit(solution)/shard_map/ppermute | solution.py:335
  103.4 2.2 %collective-permute-start.9 = (f32[440,128]{1,0:T(8,128)S(1)}, f32[440,128]{1,0:T(8,128)S(1)}, u32[]{:S(2)}, u32[]{:S(2)}) collective-permute-start(f32[440,128]{1,0:T(8,128)S(1)} %get-tuple-element.38), channel_id=1, source_target_pairs={{0,4},{4,8},{8,12},{1,5},{5,9},{9,13},{2,6},{6,10},{10,14},{3,7},{... | collective-permute-start | bytes 675848 | tf_op jit(solution)/shard_map/ppermute | solution.py:335
  105.6 2.0 %collective-permute-done.8.up_ref.yup_ref = f32[440,128]{1,0:T(8,128)S(1)} collective-permute-done((f32[440,128]{1,0:T(8,128)S(1)}, f32[440,128]{1,0:T(8,128)S(1)}, u32[]{:S(2)}, u32[]{:S(2)}) %collective-permute-start.8) | collective-permute-done | bytes 225312 | tf_op jit(solution)/shard_map/ppermute | solution.py:335
  107.6 3.6 %collective-permute-done.9.low_ref.ylow_ref = f32[440,128]{1,0:T(8,128)S(1)} collective-permute-done((f32[440,128]{1,0:T(8,128)S(1)}, f32[440,128]{1,0:T(8,128)S(1)}, u32[]{:S(2)}, u32[]{:S(2)}) %collective-permute-start.9) | collective-permute-done | bytes 225312 | tf_op jit(solution)/shard_map/ppermute | solution.py:335
  111.5 1.9 %collective-permute-start.10 = (f32[5,280,128]{2,1,0:T(8,128)S(1)}, f32[5,280,128]{2,1,0:T(8,128)S(1)}, u32[]{:S(2)}, u32[]{:S(2)}) collective-permute-start(f32[5,280,128]{2,1,0:T(8,128)S(1)} %get-tuple-element.39), channel_id=1, source_target_pairs={{16,0},{32,16},{48,32},{64,48},{80,64},{96,80},{112,96},{17,1},{33... | collective-permute-start | bytes 2150408 | tf_op jit(solution)/shard_map/ppermute | solution.py:335
  113.4 2.4 %collective-permute-start.11 = (f32[5,280,128]{2,1,0:T(8,128)S(1)}, f32[5,280,128]{2,1,0:T(8,128)S(1)}, u32[]{:S(2)}, u32[]{:S(2)}) collective-permute-start(f32[5,280,128]{2,1,0:T(8,128)S(1)} %get-tuple-element.40), channel_id=1, source_target_pairs={{0,16},{16,32},{32,48},{48,64},{64,80},{80,96},{96,112},{1,17},{17... | collective-permute-start | bytes 2150408 | tf_op jit(solution)/shard_map/ppermute | solution.py:335
  115.8 6.3 %collective-permute-done.10.xup_ref = f32[5,280,128]{2,1,0:T(8,128)S(1)} collective-permute-done((f32[5,280,128]{2,1,0:T(8,128)S(1)}, f32[5,280,128]{2,1,0:T(8,128)S(1)}, u32[]{:S(2)}, u32[]{:S(2)}) %collective-permute-start.10) | collective-permute-done | bytes 716832 | tf_op jit(solution)/shard_map/ppermute | solution.py:335
  122.2 3.8 %collective-permute-done.11.xlow_ref = f32[5,280,128]{2,1,0:T(8,128)S(1)} collective-permute-done((f32[5,280,128]{2,1,0:T(8,128)S(1)}, f32[5,280,128]{2,1,0:T(8,128)S(1)}, u32[]{:S(2)}, u32[]{:S(2)}) %collective-permute-start.11) | collective-permute-done | bytes 716832 | tf_op jit(solution)/shard_map/ppermute | solution.py:335
  126.0 11.8 %final.1 = f32[16,32,512]{2,1,0:T(8,128)} custom-call(f32[5,880,128]{2,1,0:T(8,128)S(1)} %get-tuple-element.33.f_ref, f32[5,880,128]{2,1,0:T(8,128)S(1)} %get-tuple-element.34.v_ref, f32[5,880,128]{2,1,0:T(8,128)S(1)} %get-tuple-element.35.a_ref.ain_ref, f32[5,128,128]{2,1,0:T(8,128)S(1)} %get-tuple-element.36.own_ref, ...), custom_call_target="tpu_custom_call" | custom-call | tf_op jit(solution)/shard_map/final/pallas_call | solution.py:42
  (28 shorter events, 15.8 us)
Async XLA Ops:
  1.3 3.6 %collective-permute-start.1 = (f32[3,128]{1,0:T(4,128)S(1)}, f32[3,128]{1,0:T(4,128)S(1)}, u32[]{:S(2)}, u32[]{:S(2)}) collective-permute-start(f32[3,128]{1,0:T(4,128)S(1)} %get-tuple-element.42), channel_id=1, source_target_pairs={{1,0},{2,1},{3,2},{4,3},{5,4},{6,5},{7,6},{8,7},{9,8},{10,9},{11,1... | collective-permute-start | bytes 4616 | tf_op jit(solution)/shard_map/ppermute | solution.py:741
  1.9 4.2 %collective-permute-start = (f32[3,128]{1,0:T(4,128)S(1)}, f32[3,128]{1,0:T(4,128)S(1)}, u32[]{:S(2)}, u32[]{:S(2)}) collective-permute-start(f32[3,128]{1,0:T(4,128)S(1)} %get-tuple-element.43), channel_id=1, source_target_pairs={{0,1},{1,2},{2,3},{3,4},{4,5},{5,6},{6,7},{7,8},{8,9},{9,10},{10,1... | collective-permute-start | bytes 4616 | tf_op jit(solution)/shard_map/ppermute | solution.py:740
  6.1 1.0 copy-start.2
  7.0 0.9 copy-start.3
  8.0 0.9 copy-start.4
  8.9 0.9 copy-start.5
  9.8 0.8 copy-start.6
  10.5 0.8 copy-start.7
  11.3 0.8 copy-start.8
  40.7 1.2 copy-start
  42.0 1.2 copy-start.1
  58.0 8.5 %collective-permute-start.2 = (f32[2,3,4,16,128]{4,3,2,1,0:T(8,128)S(1)}, f32[2,3,4,16,128]{4,3,2,1,0:T(8,128)S(1)}, u32[]{:S(2)}, u32[]{:S(2)}) collective-permute-start(f32[2,3,4,16,128]{4,3,2,1,0:T(8,128)S(1)} %get-tuple-element.25), channel_id=1, source_target_pairs={{4,0},{8,4},{12,8},{5,1},{9,5},{13,9},{6,2},{10,6},{14,10},{7,3},{... | collective-permute-start | bytes 589832 | tf_op jit(solution)/shard_map/ppermute | solution.py:335
  61.9 7.9 %collective-permute-start.3 = (f32[2,3,4,16,128]{4,3,2,1,0:T(8,128)S(1)}, f32[2,3,4,16,128]{4,3,2,1,0:T(8,128)S(1)}, u32[]{:S(2)}, u32[]{:S(2)}) collective-permute-start(f32[2,3,4,16,128]{4,3,2,1,0:T(8,128)S(1)} %get-tuple-element.26), channel_id=1, source_target_pairs={{0,4},{4,8},{8,12},{1,5},{5,9},{9,13},{2,6},{6,10},{10,14},{3,7},{... | collective-permute-start | bytes 589832 | tf_op jit(solution)/shard_map/ppermute | solution.py:335
  70.0 8.3 %collective-permute-start.4 = (f32[2,4,120,128]{3,2,1,0:T(8,128)S(1)}, f32[2,4,120,128]{3,2,1,0:T(8,128)S(1)}, u32[]{:S(2)}, u32[]{:S(2)}) collective-permute-start(f32[2,4,120,128]{3,2,1,0:T(8,128)S(1)} %get-tuple-element.27), channel_id=1, source_target_pairs={{16,0},{32,16},{48,32},{64,48},{80,64},{96,80},{112,96},{17,1},{33... | collective-permute-start | bytes 1474568 | tf_op jit(solution)/shard_map/ppermute | solution.py:335
  71.9 10.1 %collective-permute-start.5 = (f32[2,4,120,128]{3,2,1,0:T(8,128)S(1)}, f32[2,4,120,128]{3,2,1,0:T(8,128)S(1)}, u32[]{:S(2)}, u32[]{:S(2)}) collective-permute-start(f32[2,4,120,128]{3,2,1,0:T(8,128)S(1)} %get-tuple-element.28), channel_id=1, source_target_pairs={{0,16},{16,32},{32,48},{48,64},{64,80},{80,96},{96,112},{1,17},{17... | collective-permute-start | bytes 1474568 | tf_op jit(solution)/shard_map/ppermute | solution.py:335
  82.8 6.7 %collective-permute-start.6 = (f32[32,896]{1,0:T(8,128)S(1)}, f32[32,896]{1,0:T(8,128)S(1)}, u32[]{:S(2)}, u32[]{:S(2)}) collective-permute-start(f32[32,896]{1,0:T(8,128)S(1)} %get-tuple-element.31), channel_id=1, source_target_pairs={{1,0},{2,1},{3,2},{5,4},{6,5},{7,6},{9,8},{10,9},{11,10},{13,12},{... | collective-permute-start | bytes 344072 | tf_op jit(solution)/shard_map/ppermute | solution.py:335
  86.1 6.7 %collective-permute-start.7 = (f32[32,896]{1,0:T(8,128)S(1)}, f32[32,896]{1,0:T(8,128)S(1)}, u32[]{:S(2)}, u32[]{:S(2)}) collective-permute-start(f32[32,896]{1,0:T(8,128)S(1)} %get-tuple-element.32), channel_id=1, source_target_pairs={{0,1},{1,2},{2,3},{4,5},{5,6},{6,7},{8,9},{9,10},{10,11},{12,13},{... | collective-permute-start | bytes 344072 | tf_op jit(solution)/shard_map/ppermute | solution.py:335
  99.7 7.9 %collective-permute-start.8 = (f32[440,128]{1,0:T(8,128)S(1)}, f32[440,128]{1,0:T(8,128)S(1)}, u32[]{:S(2)}, u32[]{:S(2)}) collective-permute-start(f32[440,128]{1,0:T(8,128)S(1)} %get-tuple-element.37), channel_id=1, source_target_pairs={{4,0},{8,4},{12,8},{5,1},{9,5},{13,9},{6,2},{10,6},{14,10},{7,3},{... | collective-permute-start | bytes 675848 | tf_op jit(solution)/shard_map/ppermute | solution.py:335
  103.4 7.9 %collective-permute-start.9 = (f32[440,128]{1,0:T(8,128)S(1)}, f32[440,128]{1,0:T(8,128)S(1)}, u32[]{:S(2)}, u32[]{:S(2)}) collective-permute-start(f32[440,128]{1,0:T(8,128)S(1)} %get-tuple-element.38), channel_id=1, source_target_pairs={{0,4},{4,8},{8,12},{1,5},{5,9},{9,13},{2,6},{6,10},{10,14},{3,7},{... | collective-permute-start | bytes 675848 | tf_op jit(solution)/shard_map/ppermute | solution.py:335
  111.5 10.7 %collective-permute-start.10 = (f32[5,280,128]{2,1,0:T(8,128)S(1)}, f32[5,280,128]{2,1,0:T(8,128)S(1)}, u32[]{:S(2)}, u32[]{:S(2)}) collective-permute-start(f32[5,280,128]{2,1,0:T(8,128)S(1)} %get-tuple-element.39), channel_id=1, source_target_pairs={{16,0},{32,16},{48,32},{64,48},{80,64},{96,80},{112,96},{17,1},{33... | collective-permute-start | bytes 2150408 | tf_op jit(solution)/shard_map/ppermute | solution.py:335
  113.4 12.6 %collective-permute-start.11 = (f32[5,280,128]{2,1,0:T(8,128)S(1)}, f32[5,280,128]{2,1,0:T(8,128)S(1)}, u32[]{:S(2)}, u32[]{:S(2)}) collective-permute-start(f32[5,280,128]{2,1,0:T(8,128)S(1)} %get-tuple-element.40), channel_id=1, source_target_pairs={{0,16},{16,32},{32,48},{48,64},{64,80},{80,96},{96,112},{1,17},{17... | collective-permute-start | bytes 2150408 | tf_op jit(solution)/shard_map/ppermute | solution.py:335

commit v4 on v3

--- a/solution.py
+++ b/solution.py
@@ -48,7 +48,7 @@
         compiler_params=pltpu.CompilerParams(vmem_limit_bytes=limit << 20),
         input_output_aliases=alias or {},
         name=name,
-    )(*operands)
+    )(*[pltpu.with_memory_space_constraint(o, pltpu.HBM) if i in far else o for i, o in enumerate(operands)])
 
 
 def lanes(shape):
@@ -81,7 +81,11 @@
     return plane, beside + (pltpu.roll(plane, step, 1) + pltpu.roll(plane, nz - step, 1))
 
 
-def planes(first, last, body, group=2):
+GROUP = 4
+
+
+def planes(first, last, body, group=0):
+    group = group or GROUP
     count = (last - first) // group
 
     def step(i, carry):
@@ -665,32 +669,48 @@
     lax.fori_loop(0, 8, block, 0)
 
 
-def scatter_kernel(rhs_hbm, shift_hbm, got_ref, force_ref, inv_ref, to_low_ref, to_up_ref, rhs_ref, shift_ref, key_ref, val_ref, rank_ref, turn_key_ref, turn_val_ref, sems):
+def inverse_kernel(shift_hbm, inv_ref, to_low_ref, to_up_ref, shift_ref, sems):
+    for i in range(2):
+        at = pl.ds(i * (CX // 2), CX // 2)
+        pltpu.make_async_copy(shift_hbm.at[at], shift_ref.at[at], sems.at[i]).start()
+    for i in range(2):
+        at = pl.ds(i * (CX // 2), CX // 2)
+        pltpu.make_async_copy(shift_hbm.at[at], shift_ref.at[at], sems.at[i]).wait()
+
+        def step(x, carry):
+            for t in range(T):
+                inv_ref[t, span(x, CY), :] = 1.0 / (6.0 + shift_ref[x, :, 128 * t : 128 * t + 128])
+            return carry
+
+        lax.fori_loop(i * (CX // 2), (i + 1) * (CX // 2), step, 0)
+    for r in range(W):
+        for t in range(T):
+            to_low_ref[r, t] = inv_ref[t, pl.ds(r, CX, CY), :]
+            to_up_ref[r, t] = inv_ref[t, pl.ds(CY - W + r, CX, CY), :]
+
+
+def scatter_kernel(rhs_hbm, got_ref, inv_low_ref, inv_up_ref, force_ref, to_low_ref, to_up_ref, rhs_ref, key_ref, val_ref, rank_ref, turn_key_ref, turn_val_ref, sems):
     rhs_copy = pltpu.make_async_copy(rhs_hbm, rhs_ref, sems.at[0])
-    shift_copy = pltpu.make_async_copy(shift_hbm, shift_ref, sems.at[1])
     rhs_copy.start()
-    shift_copy.start()
     unpack_and_merge(got_ref, key_ref, val_ref)
     combine(key_ref, val_ref, rank_ref)
     concentrate(key_ref, val_ref, rank_ref, turn_key_ref, turn_val_ref)
     rhs_copy.wait()
-    shift_copy.wait()
 
     def write(q, u, values):
         x = 2 * q + u // 2
         for i, value in enumerate(values):
             row, t = 16 * (u % 2) + 8 * (i // 4), i % 4
             at = (x, slice(row, row + 8), slice(128 * t, 128 * t + 128))
-            to = (t, pl.ds(pl.multiple_of(CY * x + row, 8), 8))
-            force_ref[to] = rhs_ref[at] + value
-            inv_ref[to] = 1.0 / (6.0 + shift_ref[at])
+            force_ref[t, pl.ds(pl.multiple_of(CY * x + row, 8), 8)] = rhs_ref[at] + value
 
     distribute(turn_key_ref, turn_val_ref, rank_ref, val_ref, write)
-    for which, ref in ((0, force_ref), (1, inv_ref)):
-        for r in range(W):
-            for t in range(T):
-                to_low_ref[which, r, t] = ref[t, pl.ds(r, CX, CY), :]
-                to_up_ref[which, r, t] = ref[t, pl.ds(CY - W + r, CX, CY), :]
+    to_low_ref[1] = inv_low_ref[...]
+    to_up_ref[1] = inv_up_ref[...]
+    for r in range(W):
+        for t in range(T):
+            to_low_ref[0, r, t] = force_ref[t, pl.ds(r, CX, CY), :]
+            to_up_ref[0, r, t] = force_ref[t, pl.ds(CY - W + r, CX, CY), :]
 
 
 def points_kernel(begin_ref, low_ref, up_ref, pos_hbm, nrm_hbm, ten_hbm, edge_hbm, conn_hbm, owner_hbm, cell_hbm, force_ref, send_ref, pos_ref, nrm_ref, ten_ref, edge_ref, conn_ref, owner_ref, cell_ref, jump_ref, key_ref, val_ref, goal_ref, sems):
@@ -767,14 +787,22 @@
     block = pltpu.VMEM((CX, CY, CZ), jnp.float32)
     list_i, list_f = pltpu.VMEM((256, 128), jnp.int32), pltpu.VMEM((256, 128), jnp.float32)
     own, face = (T, CX * CY, 128), (2, W, T, CX, 128)
-    forcing, inverse, to_low, to_up = call(
+    inverse, inv_low, inv_up = call(
+        inverse_kernel,
+        [own, face[1:], face[1:]],
+        (shift_diag,),
+        [block, pltpu.SemaphoreType.DMA((2,))],
+        name="inverse",
+        far=(0,),
+    )
+    forcing, to_low, to_up = call(
         scatter_kernel,
-        [own, own, face, face],
-        (pressure_rhs, shift_diag, got),
-        [block, block, list_i, list_f, list_i, list_i, list_f, pltpu.SemaphoreType.DMA((2,))],
+        [own, face, face],
+        (pressure_rhs, got, inv_low, inv_up),
+        [block, list_i, list_f, list_i, list_i, list_f, pltpu.SemaphoreType.DMA((1,))],
         name="scatter",
         limit=8,
-        far=(0, 1),
+        far=(0,),
     )
     return solve(forcing, inverse, to_low, to_up), force
 

time: 139 us -> 129 us (0.928)
  blocking collectives: 22.2 us -> 0 us
  starting transfers between devices: 28.2 us -> 43.7 us
  local copies, waits for them, and re-layouts: 9.13 us -> 0.7 us
  waiting for transfers between devices: 36.3 us -> 42.2 us
    all_to_all x1 -> x0, blocking collectives: 22.2 us -> none  [body(): got = lax.all_to_all(send, ALL, 0, 0, tiled=True)]
    all_to_all x0 -> x1, starting transfers between devices: none -> 15.5 us  [body(): got = lax.all_to_all(send, ALL, 0, 0, tiled=True)]
    unnamed x18 -> x0, local copies, waits for them, and re-layouts: 8.43 us -> none
    all_to_all x0 -> x1, waiting for transfers between devices: none -> 5.89 us  [body(): got = lax.all_to_all(send, ALL, 0, 0, tiled=True)]
    pallas_call x7 -> x8, Pallas kernels: 41.1 us -> 40.4 us  [call(): pl.pallas_call(kernel, out_shape=[jax.ShapeDtypeStruct(s, jnp.float32) fo...]
  transfers between devices with their start and end apart: 12 -> 13, of which waited for: 12 -> 13; matrix products, arithmetic and copies ran while one was open for 0% -> 0% of each run, Pallas kernels for 0% -> 1%
where the time goes in v4:
time: 129 us; the launch traced here: 128 us
  starting transfers between devices  43.7 us (34%)
  waiting for transfers between devices  42.2 us (33%)
  Pallas kernels  40.4 us (31%)
    pallas_call x8, Pallas kernels, call(): pl.pallas_call(kernel, out_shape=[jax.ShapeDtypeStruct(s, jnp.float32) fo...  40.4 us
    ppermute x5, waiting for transfers between devices, swap(): lax.ppermute(high, axis, up)  17.9 us
    ppermute x5, waiting for transfers between devices, swap(): lax.ppermute(low, axis, [(b, a) for a, b in up])  15.7 us
    all_to_all x1, starting transfers between devices, body(): got = lax.all_to_all(send, ALL, 0, 0, tiled=True)  15.5 us
    ppermute x5, starting transfers between devices, swap(): lax.ppermute(low, axis, [(b, a) for a, b in up])  14.7 us
    ppermute x5, starting transfers between devices, swap(): lax.ppermute(high, axis, up)  11.5 us
    all_to_all x1, waiting for transfers between devices, body(): got = lax.all_to_all(send, ALL, 0, 0, tiled=True)  5.89 us
  transfers between devices with their start and end apart: 13, of which 13 were waited for; matrix products, arithmetic and copies ran while one was open for 0% of the time, Pallas kernels for 1%

profile of v4, /device:TPU:50, one launch (start us, length us, event | category | flops | bytes accessed | tf_op | source)
XLA Modules:
  0.0 128.0 jit_solution(1269051359540858384)
XLA Ops:
  6.1 7.8 %points.1 = (f32[3,8192]{1,0:T(4,128)}, f32[512,128]{1,0:T(8,128)}) custom-call(s32[2]{0:T(128)S(1)} %pad_add_fusion.begin_ref, f32[3,128]{1,0:T(4,128)S(1)} %collective-permute-done.low_ref, f32[3,128]{1,0:T(4,128)S(1)} %collective-permute-done.1.up_ref, f32[3,8192]{1,0:T(4,128)} %pos_hbm.1, f32[3,8192]{1,0:T(4,128)} %nrm_hbm.1, f32[64,128]{1,0:T(8,128)} %bitcast.8, ...), custom_call_target="tpu_custom_call" | custom-call | tf_op jit(solution)/shard_map/points/pallas_call | solution.py:42
  13.9 15.5 %all-to-all-start = ((f32[128,4,128]{2,1,0:T(4,128)}), f32[128,4,128]{2,1,0:T(4,128)S(1)}, u32[]{:S(2)}, u32[]{:S(2)}) async-start(f32[128,4,128]{2,1,0:T(4,128)} %bitcast.5), calls=%async_computation | async-start | bytes 524288 | tf_op jit(solution)/shard_map/all_to_all | solution.py:786
  30.9 5.9 %all-to-all-done = f32[128,4,128]{2,1,0:T(4,128)S(1)} async-done(((f32[128,4,128]{2,1,0:T(4,128)}), f32[128,4,128]{2,1,0:T(4,128)S(1)}, u32[]{:S(2)}, u32[]{:S(2)}) %all-to-all-start) | async-done | bytes 262176 | tf_op jit(solution)/shard_map/all_to_all | solution.py:786
  36.8 14.5 %scatter.1 = (f32[4,512,128]{2,1,0:T(8,128)S(1)}, f32[2,3,4,16,128]{4,3,2,1,0:T(8,128)S(1)}, f32[2,3,4,16,128]{4,3,2,1,0:T(8,128)S(1)}) custom-call(f32[16,32,512]{2,1,0:T(8,128)} %rhs_hbm.1, f32[512,128]{1,0:T(8,128)S(1)} %bitcast.7, f32[3,4,16,128]{3,2,1,0:T(8,128)S(1)} %get-tuple-element.25.inv_low_ref, f32[3,4,16,128]{3,2,1,0:T(8,128)S(1)} %get-tuple-element.26.inv_up_ref), custom_call_target="tpu_custom_call" | custom-call | tf_op jit(solution)/shard_map/scatter/pallas_call | solution.py:42
  51.3 3.9 %collective-permute-start.2 = (f32[2,3,4,16,128]{4,3,2,1,0:T(8,128)S(1)}, f32[2,3,4,16,128]{4,3,2,1,0:T(8,128)S(1)}, u32[]{:S(2)}, u32[]{:S(2)}) collective-permute-start(f32[2,3,4,16,128]{4,3,2,1,0:T(8,128)S(1)} %get-tuple-element.29), channel_id=1, source_target_pairs={{4,0},{8,4},{12,8},{5,1},{9,5},{13,9},{6,2},{10,6},{14,10},{7,3},{... | collective-permute-start | bytes 589832 | tf_op jit(solution)/shard_map/ppermute | solution.py:339
  55.2 2.0 %collective-permute-start.3 = (f32[2,3,4,16,128]{4,3,2,1,0:T(8,128)S(1)}, f32[2,3,4,16,128]{4,3,2,1,0:T(8,128)S(1)}, u32[]{:S(2)}, u32[]{:S(2)}) collective-permute-start(f32[2,3,4,16,128]{4,3,2,1,0:T(8,128)S(1)} %get-tuple-element.30), channel_id=1, source_target_pairs={{0,4},{4,8},{8,12},{1,5},{5,9},{9,13},{2,6},{6,10},{10,14},{3,7},{... | collective-permute-start | bytes 589832 | tf_op jit(solution)/shard_map/ppermute | solution.py:339
  57.2 2.6 %collective-permute-done.2.up_ref.yup_ref = f32[2,3,4,16,128]{4,3,2,1,0:T(8,128)S(1)} collective-permute-done((f32[2,3,4,16,128]{4,3,2,1,0:T(8,128)S(1)}, f32[2,3,4,16,128]{4,3,2,1,0:T(8,128)S(1)}, u32[]{:S(2)}, u32[]{:S(2)}) %collective-permute-start.2) | collective-permute-done | bytes 196640 | tf_op jit(solution)/shard_map/ppermute | solution.py:339
  59.8 3.3 %collective-permute-done.3.low_ref.ylow_ref = f32[2,3,4,16,128]{4,3,2,1,0:T(8,128)S(1)} collective-permute-done((f32[2,3,4,16,128]{4,3,2,1,0:T(8,128)S(1)}, f32[2,3,4,16,128]{4,3,2,1,0:T(8,128)S(1)}, u32[]{:S(2)}, u32[]{:S(2)}) %collective-permute-start.3) | collective-permute-done | bytes 196640 | tf_op jit(solution)/shard_map/ppermute | solution.py:339
  63.2 1.9 %collective-permute-start.4 = (f32[2,4,120,128]{3,2,1,0:T(8,128)S(1)}, f32[2,4,120,128]{3,2,1,0:T(8,128)S(1)}, u32[]{:S(2)}, u32[]{:S(2)}) collective-permute-start(f32[2,4,120,128]{3,2,1,0:T(8,128)S(1)} %get-tuple-element.31), channel_id=1, source_target_pairs={{16,0},{32,16},{48,32},{64,48},{80,64},{96,80},{112,96},{17,1},{33... | collective-permute-start | bytes 1474568 | tf_op jit(solution)/shard_map/ppermute | solution.py:339
  65.2 2.4 %collective-permute-start.5 = (f32[2,4,120,128]{3,2,1,0:T(8,128)S(1)}, f32[2,4,120,128]{3,2,1,0:T(8,128)S(1)}, u32[]{:S(2)}, u32[]{:S(2)}) collective-permute-start(f32[2,4,120,128]{3,2,1,0:T(8,128)S(1)} %get-tuple-element.32), channel_id=1, source_target_pairs={{0,16},{16,32},{32,48},{48,64},{64,80},{80,96},{96,112},{1,17},{17... | collective-permute-start | bytes 1474568 | tf_op jit(solution)/shard_map/ppermute | solution.py:339
  67.6 3.9 %collective-permute-done.4.xup_ref = f32[2,4,120,128]{3,2,1,0:T(8,128)S(1)} collective-permute-done((f32[2,4,120,128]{3,2,1,0:T(8,128)S(1)}, f32[2,4,120,128]{3,2,1,0:T(8,128)S(1)}, u32[]{:S(2)}, u32[]{:S(2)}) %collective-permute-start.4) | collective-permute-done | bytes 491552 | tf_op jit(solution)/shard_map/ppermute | solution.py:339
  71.5 3.8 %collective-permute-done.5.xlow_ref = f32[2,4,120,128]{3,2,1,0:T(8,128)S(1)} collective-permute-done((f32[2,4,120,128]{3,2,1,0:T(8,128)S(1)}, f32[2,4,120,128]{3,2,1,0:T(8,128)S(1)}, u32[]{:S(2)}, u32[]{:S(2)}) %collective-permute-start.5) | collective-permute-done | bytes 491552 | tf_op jit(solution)/shard_map/ppermute | solution.py:339
  76.0 3.3 %collective-permute-start.6 = (f32[32,896]{1,0:T(8,128)S(1)}, f32[32,896]{1,0:T(8,128)S(1)}, u32[]{:S(2)}, u32[]{:S(2)}) collective-permute-start(f32[32,896]{1,0:T(8,128)S(1)} %get-tuple-element.35), channel_id=1, source_target_pairs={{1,0},{2,1},{3,2},{5,4},{6,5},{7,6},{9,8},{10,9},{11,10},{13,12},{... | collective-permute-start | bytes 344072 | tf_op jit(solution)/shard_map/ppermute | solution.py:339
  79.4 2.5 %collective-permute-start.7 = (f32[32,896]{1,0:T(8,128)S(1)}, f32[32,896]{1,0:T(8,128)S(1)}, u32[]{:S(2)}, u32[]{:S(2)}) collective-permute-start(f32[32,896]{1,0:T(8,128)S(1)} %get-tuple-element.36), channel_id=1, source_target_pairs={{0,1},{1,2},{2,3},{4,5},{5,6},{6,7},{8,9},{9,10},{10,11},{12,13},{... | collective-permute-start | bytes 344072 | tf_op jit(solution)/shard_map/ppermute | solution.py:339
  82.7 3.3 %collective-permute-done.7.zlow_ref = f32[32,896]{1,0:T(8,128)S(1)} collective-permute-done((f32[32,896]{1,0:T(8,128)S(1)}, f32[32,896]{1,0:T(8,128)S(1)}, u32[]{:S(2)}, u32[]{:S(2)}) %collective-permute-start.7) | collective-permute-done | bytes 114720 | tf_op jit(solution)/shard_map/ppermute | solution.py:339
  86.0 6.2 %smooth.1 = (f32[5,880,128]{2,1,0:T(8,128)S(1)}, f32[5,880,128]{2,1,0:T(8,128)S(1)}, f32[5,880,128]{2,1,0:T(8,128)S(1)}, f32[440,128]{1,0:T(8,128)S(1)}, f32[440...) custom-call(f32[5,880,128]{2,1,0:T(8,128)S(1)} %get-tuple-element.33._fin_ref, ...), custom_call_target="tpu_custom_call", output_to_operand_aliasing={{0}: (0, {}), {1}: (1, {})} | custom-call | tf_op jit(solution)/shard_map/smooth/pallas_call | solution.py:42
  92.2 3.6 %collective-permute-start.8 = (f32[440,128]{1,0:T(8,128)S(1)}, f32[440,128]{1,0:T(8,128)S(1)}, u32[]{:S(2)}, u32[]{:S(2)}) collective-permute-start(f32[440,128]{1,0:T(8,128)S(1)} %get-tuple-element.41), channel_id=1, source_target_pairs={{4,0},{8,4},{12,8},{5,1},{9,5},{13,9},{6,2},{10,6},{14,10},{7,3},{... | collective-permute-start | bytes 675848 | tf_op jit(solution)/shard_map/ppermute | solution.py:339
  95.9 2.2 %collective-permute-start.9 = (f32[440,128]{1,0:T(8,128)S(1)}, f32[440,128]{1,0:T(8,128)S(1)}, u32[]{:S(2)}, u32[]{:S(2)}) collective-permute-start(f32[440,128]{1,0:T(8,128)S(1)} %get-tuple-element.42), channel_id=1, source_target_pairs={{0,4},{4,8},{8,12},{1,5},{5,9},{9,13},{2,6},{6,10},{10,14},{3,7},{... | collective-permute-start | bytes 675848 | tf_op jit(solution)/shard_map/ppermute | solution.py:339
  98.1 2.0 %collective-permute-done.8.up_ref.yup_ref = f32[440,128]{1,0:T(8,128)S(1)} collective-permute-done((f32[440,128]{1,0:T(8,128)S(1)}, f32[440,128]{1,0:T(8,128)S(1)}, u32[]{:S(2)}, u32[]{:S(2)}) %collective-permute-start.8) | collective-permute-done | bytes 225312 | tf_op jit(solution)/shard_map/ppermute | solution.py:339
  100.1 3.6 %collective-permute-done.9.low_ref.ylow_ref = f32[440,128]{1,0:T(8,128)S(1)} collective-permute-done((f32[440,128]{1,0:T(8,128)S(1)}, f32[440,128]{1,0:T(8,128)S(1)}, u32[]{:S(2)}, u32[]{:S(2)}) %collective-permute-start.9) | collective-permute-done | bytes 225312 | tf_op jit(solution)/shard_map/ppermute | solution.py:339
  105.9 2.4 %collective-permute-start.11 = (f32[5,280,128]{2,1,0:T(8,128)S(1)}, f32[5,280,128]{2,1,0:T(8,128)S(1)}, u32[]{:S(2)}, u32[]{:S(2)}) collective-permute-start(f32[5,280,128]{2,1,0:T(8,128)S(1)} %get-tuple-element.44), channel_id=1, source_target_pairs={{0,16},{16,32},{32,48},{48,64},{64,80},{80,96},{96,112},{1,17},{17... | collective-permute-start | bytes 2150408 | tf_op jit(solution)/shard_map/ppermute | solution.py:339
  108.3 6.3 %collective-permute-done.10.xup_ref = f32[5,280,128]{2,1,0:T(8,128)S(1)} collective-permute-done((f32[5,280,128]{2,1,0:T(8,128)S(1)}, f32[5,280,128]{2,1,0:T(8,128)S(1)}, u32[]{:S(2)}, u32[]{:S(2)}) %collective-permute-start.10) | collective-permute-done | bytes 716832 | tf_op jit(solution)/shard_map/ppermute | solution.py:339
  114.7 3.8 %collective-permute-done.11.xlow_ref = f32[5,280,128]{2,1,0:T(8,128)S(1)} collective-permute-done((f32[5,280,128]{2,1,0:T(8,128)S(1)}, f32[5,280,128]{2,1,0:T(8,128)S(1)}, u32[]{:S(2)}, u32[]{:S(2)}) %collective-permute-start.11) | collective-permute-done | bytes 716832 | tf_op jit(solution)/shard_map/ppermute | solution.py:339
  118.5 9.4 %final.1 = f32[16,32,512]{2,1,0:T(8,128)} custom-call(f32[5,880,128]{2,1,0:T(8,128)S(1)} %get-tuple-element.37.f_ref, f32[5,880,128]{2,1,0:T(8,128)S(1)} %get-tuple-element.38.v_ref, f32[5,880,128]{2,1,0:T(8,128)S(1)} %get-tuple-element.39.a_ref.ain_ref, f32[5,128,128]{2,1,0:T(8,128)S(1)} %get-tuple-element.40.own_ref, ...), custom_call_target="tpu_custom_call" | custom-call | tf_op jit(solution)/shard_map/final/pallas_call | solution.py:42
  (12 shorter events, 10.7 us)
Async XLA Ops:
  1.3 3.6 %collective-permute-start.1 = (f32[3,128]{1,0:T(4,128)S(1)}, f32[3,128]{1,0:T(4,128)S(1)}, u32[]{:S(2)}, u32[]{:S(2)}) collective-permute-start(f32[3,128]{1,0:T(4,128)S(1)} %get-tuple-element.46), channel_id=1, source_target_pairs={{1,0},{2,1},{3,2},{4,3},{5,4},{6,5},{7,6},{8,7},{9,8},{10,9},{11,1... | collective-permute-start | bytes 4616 | tf_op jit(solution)/shard_map/ppermute | solution.py:761
  1.9 4.2 %collective-permute-start = (f32[3,128]{1,0:T(4,128)S(1)}, f32[3,128]{1,0:T(4,128)S(1)}, u32[]{:S(2)}, u32[]{:S(2)}) collective-permute-start(f32[3,128]{1,0:T(4,128)S(1)} %get-tuple-element.47), channel_id=1, source_target_pairs={{0,1},{1,2},{2,3},{3,4},{4,5},{5,6},{6,7},{7,8},{8,9},{9,10},{10,1... | collective-permute-start | bytes 4616 | tf_op jit(solution)/shard_map/ppermute | solution.py:760
  13.9 22.9 %all-to-all-start = ((f32[128,4,128]{2,1,0:T(4,128)}), f32[128,4,128]{2,1,0:T(4,128)S(1)}, u32[]{:S(2)}, u32[]{:S(2)}) async-start(f32[128,4,128]{2,1,0:T(4,128)} %bitcast.5), calls=%async_computation | async-start | bytes 524288 | tf_op jit(solution)/shard_map/all_to_all | solution.py:786
  51.3 8.5 %collective-permute-start.2 = (f32[2,3,4,16,128]{4,3,2,1,0:T(8,128)S(1)}, f32[2,3,4,16,128]{4,3,2,1,0:T(8,128)S(1)}, u32[]{:S(2)}, u32[]{:S(2)}) collective-permute-start(f32[2,3,4,16,128]{4,3,2,1,0:T(8,128)S(1)} %get-tuple-element.29), channel_id=1, source_target_pairs={{4,0},{8,4},{12,8},{5,1},{9,5},{13,9},{6,2},{10,6},{14,10},{7,3},{... | collective-permute-start | bytes 589832 | tf_op jit(solution)/shard_map/ppermute | solution.py:339
  55.2 7.9 %collective-permute-start.3 = (f32[2,3,4,16,128]{4,3,2,1,0:T(8,128)S(1)}, f32[2,3,4,16,128]{4,3,2,1,0:T(8,128)S(1)}, u32[]{:S(2)}, u32[]{:S(2)}) collective-permute-start(f32[2,3,4,16,128]{4,3,2,1,0:T(8,128)S(1)} %get-tuple-element.30), channel_id=1, source_target_pairs={{0,4},{4,8},{8,12},{1,5},{5,9},{9,13},{2,6},{6,10},{10,14},{3,7},{... | collective-permute-start | bytes 589832 | tf_op jit(solution)/shard_map/ppermute | solution.py:339
  63.2 8.3 %collective-permute-start.4 = (f32[2,4,120,128]{3,2,1,0:T(8,128)S(1)}, f32[2,4,120,128]{3,2,1,0:T(8,128)S(1)}, u32[]{:S(2)}, u32[]{:S(2)}) collective-permute-start(f32[2,4,120,128]{3,2,1,0:T(8,128)S(1)} %get-tuple-element.31), channel_id=1, source_target_pairs={{16,0},{32,16},{48,32},{64,48},{80,64},{96,80},{112,96},{17,1},{33... | collective-permute-start | bytes 1474568 | tf_op jit(solution)/shard_map/ppermute | solution.py:339
  65.2 10.1 %collective-permute-start.5 = (f32[2,4,120,128]{3,2,1,0:T(8,128)S(1)}, f32[2,4,120,128]{3,2,1,0:T(8,128)S(1)}, u32[]{:S(2)}, u32[]{:S(2)}) collective-permute-start(f32[2,4,120,128]{3,2,1,0:T(8,128)S(1)} %get-tuple-element.32), channel_id=1, source_target_pairs={{0,16},{16,32},{32,48},{48,64},{64,80},{80,96},{96,112},{1,17},{17... | collective-permute-start | bytes 1474568 | tf_op jit(solution)/shard_map/ppermute | solution.py:339
  76.0 6.7 %collective-permute-start.6 = (f32[32,896]{1,0:T(8,128)S(1)}, f32[32,896]{1,0:T(8,128)S(1)}, u32[]{:S(2)}, u32[]{:S(2)}) collective-permute-start(f32[32,896]{1,0:T(8,128)S(1)} %get-tuple-element.35), channel_id=1, source_target_pairs={{1,0},{2,1},{3,2},{5,4},{6,5},{7,6},{9,8},{10,9},{11,10},{13,12},{... | collective-permute-start | bytes 344072 | tf_op jit(solution)/shard_map/ppermute | solution.py:339
  79.4 6.7 %collective-permute-start.7 = (f32[32,896]{1,0:T(8,128)S(1)}, f32[32,896]{1,0:T(8,128)S(1)}, u32[]{:S(2)}, u32[]{:S(2)}) collective-permute-start(f32[32,896]{1,0:T(8,128)S(1)} %get-tuple-element.36), channel_id=1, source_target_pairs={{0,1},{1,2},{2,3},{4,5},{5,6},{6,7},{8,9},{9,10},{10,11},{12,13},{... | collective-permute-start | bytes 344072 | tf_op jit(solution)/shard_map/ppermute | solution.py:339
  92.2 7.9 %collective-permute-start.8 = (f32[440,128]{1,0:T(8,128)S(1)}, f32[440,128]{1,0:T(8,128)S(1)}, u32[]{:S(2)}, u32[]{:S(2)}) collective-permute-start(f32[440,128]{1,0:T(8,128)S(1)} %get-tuple-element.41), channel_id=1, source_target_pairs={{4,0},{8,4},{12,8},{5,1},{9,5},{13,9},{6,2},{10,6},{14,10},{7,3},{... | collective-permute-start | bytes 675848 | tf_op jit(solution)/shard_map/ppermute | solution.py:339
  95.9 7.9 %collective-permute-start.9 = (f32[440,128]{1,0:T(8,128)S(1)}, f32[440,128]{1,0:T(8,128)S(1)}, u32[]{:S(2)}, u32[]{:S(2)}) collective-permute-start(f32[440,128]{1,0:T(8,128)S(1)} %get-tuple-element.42), channel_id=1, source_target_pairs={{0,4},{4,8},{8,12},{1,5},{5,9},{9,13},{2,6},{6,10},{10,14},{3,7},{... | collective-permute-start | bytes 675848 | tf_op jit(solution)/shard_map/ppermute | solution.py:339
  104.0 10.7 %collective-permute-start.10 = (f32[5,280,128]{2,1,0:T(8,128)S(1)}, f32[5,280,128]{2,1,0:T(8,128)S(1)}, u32[]{:S(2)}, u32[]{:S(2)}) collective-permute-start(f32[5,280,128]{2,1,0:T(8,128)S(1)} %get-tuple-element.43), channel_id=1, source_target_pairs={{16,0},{32,16},{48,32},{64,48},{80,64},{96,80},{112,96},{17,1},{33... | collective-permute-start | bytes 2150408 | tf_op jit(solution)/shard_map/ppermute | solution.py:339
  105.9 12.6 %collective-permute-start.11 = (f32[5,280,128]{2,1,0:T(8,128)S(1)}, f32[5,280,128]{2,1,0:T(8,128)S(1)}, u32[]{:S(2)}, u32[]{:S(2)}) collective-permute-start(f32[5,280,128]{2,1,0:T(8,128)S(1)} %get-tuple-element.44), channel_id=1, source_target_pairs={{0,16},{16,32},{32,48},{48,64},{64,80},{80,96},{96,112},{1,17},{17... | collective-permute-start | bytes 2150408 | tf_op jit(solution)/shard_map/ppermute | solution.py:339
